TPU v7x, 32 devices: a whole 2x2x4 slice. The times are simulated.
32 devices in a mesh: cluster: 4 (over y, core), sub: 8 (over z, x).
Axes of the slice: x: 2, y: 2, z: 4, core: 2. Of those that a mesh axis runs over, the one named last changes fastest.
Arguments:
- compliance: float32 [4, 8, 1024, 1024], P('cluster', 'sub'), may hold values from -0.078125 to 4.078125, as said below
- loads: float32 [4, 8, 1024, 256], P('cluster', 'sub'), may hold values from -6 to 6
- modes: float32 [4, 8, 32, 1024], P('cluster', 'sub'), may hold values from -1 to 1
- coarse_inverse: float32 [4, 256, 256], P('cluster', 'sub'), may hold values from -0.9 to 0.9, as said below
- face_block: int32 [4, 8, 4], replicated, may hold values from 0 to 7, as said below
- edge_rows: int32 [4, 8, 2], replicated, may hold values from 16 to 128
Outputs:
- solution: float32 [4, 8, 1024, 256], P('cluster', 'sub')
- residual: float32 [4, 8, 1024, 256], P('cluster', 'sub')
Inputs may be any that keep to these rules, and one draw needn't show every extreme that they name: `compliance`: symmetric positive definite for every subdomain. `coarse_inverse`: symmetric positive definite for every cluster. `face_block`: the four faces of a subdomain lie in four different row blocks. `edge_rows`: entries of faces with no partner are not read.
All inputs are finite; a program needn't handle non-finite values.
Results may differ from a plain program's by a relative error of at most 0.00018.
Values sent between devices are 32-bit elements; how exact they have to be, the bound alone decides.
No kernel may reach another device: no remote copies, remote signals or barrier semaphores. Data moves between devices by JAX's collectives and lax.ppermute only.
A program may use at most 64 MiB of HBM per device.

v0:
```python
import jax
import jax.numpy as jnp
from jax import lax
from jax.sharding import PartitionSpec as P

BLOCK = 128
ITERS = 3


def from_behind(value, axis, steps):
    count = lax.axis_size(axis)
    initial, last = (max(0, -steps), min(count, count - steps))
    return lax.ppermute(value, axis, [(source, source + steps) for source in range(initial, last)])


def take_block(field, block_index):
    return lax.dynamic_slice_in_dim(field, block_index * BLOCK, BLOCK, 0)


def add_block(field, block_index, arrived, length):
    rows = jnp.arange(BLOCK, dtype=jnp.int32)
    weight = (0.5 * (rows < length).astype(jnp.float32))[:, None]
    current = take_block(field, block_index)
    return lax.dynamic_update_slice_in_dim(
        field, current + weight * arrived, block_index * BLOCK, 0
    )


def assemble(field, faces, sub_routes, clus_routes):
    result = field
    for send_face, recv_face, length, offset in sub_routes:
        arrived = from_behind(take_block(field, faces[send_face]), "sub", offset)
        result = add_block(result, faces[recv_face], arrived, length)
    for send_face, recv_face, length, offset in clus_routes:
        arrived = from_behind(take_block(field, faces[send_face]), "cluster", offset)
        result = add_block(result, faces[recv_face], arrived, length)
    return result


def precondition(basis, inverse_rows, resid):
    coarse = jnp.dot(basis, resid, precision=lax.Precision.HIGHEST)
    solved = jnp.dot(
        inverse_rows,
        lax.all_gather(coarse, "sub", axis=0, tiled=True),
        precision=lax.Precision.HIGHEST,
    )
    return resid + jnp.einsum("mo,ml->ol", basis, solved, precision=lax.Precision.HIGHEST)


def paired_dots(first, second, third):
    return lax.psum(
        (jnp.sum(first * second, axis=0), jnp.sum(third * second, axis=0)), ("cluster", "sub")
    )


def shards(compliance, loads, modes, coarse_inverse, face_block, edge_rows):
    matrix = compliance[0, 0]
    rhs = loads[0, 0]
    basis = modes[0, 0]
    inverse_rows = coarse_inverse[0]
    clus_index = lax.axis_index("cluster")
    sub_index = lax.axis_index("sub")
    faces = face_block[clus_index, sub_index]
    sub_low = edge_rows[clus_index, jnp.maximum(sub_index - 1, 0), 0]
    sub_high = edge_rows[clus_index, sub_index, 0]
    clus_low = edge_rows[jnp.maximum(clus_index - 1, 0), sub_index, 1]
    clus_high = edge_rows[clus_index, sub_index, 1]
    sub_routes = ((1, 0, sub_low, 1), (0, 1, sub_high, -1))
    clus_routes = ((3, 2, clus_low, 1), (2, 3, clus_high, -1))

    def operator(field):
        inner = assemble(field, faces, sub_routes, clus_routes)
        product = jnp.dot(matrix, inner, precision=lax.Precision.HIGHEST)
        return assemble(product, faces, sub_routes, clus_routes)

    solution = jnp.zeros_like(rhs)
    residual = rhs
    precond = precondition(basis, inverse_rows, residual)
    image = operator(precond)
    rz_now, curve = paired_dots(residual, precond, image)
    alpha = rz_now / curve
    direction, along = (precond, image)
    for step in range(ITERS):
        solution = solution + alpha * direction
        residual = residual - alpha * along
        if step + 1 < ITERS:
            precond = precondition(basis, inverse_rows, residual)
            image = operator(precond)
            rz_next, curve = paired_dots(residual, precond, image)
            ratio = rz_next / rz_now
            alpha = rz_next / (curve - ratio * rz_next / alpha)
            direction = precond + ratio * direction
            along = image + ratio * along
            rz_now = rz_next
    return (solution[None, None], residual[None, None])


def solution(mesh):
    return jax.shard_map(
        shards,
        mesh=mesh,
        in_specs=(
            P("cluster", "sub", None, None),
            P("cluster", "sub", None, None),
            P("cluster", "sub", None, None),
            P("cluster", "sub", None),
            P(),
            P(),
        ),
        out_specs=(P("cluster", "sub", None, None), P("cluster", "sub", None, None)),
        check_vma=False,
    )
```

profile of v0, /device:TPU:0, one launch (start us, length us, event | category | flops | bytes accessed | tf_op | source)
XLA Modules:
  0.0 356.5 jit_solution(3308111237335397450)
XLA Ops:
  6.5 32.6 %all_gather.9 = f32[256,256]{1,0:T(8,128)S(1)} all-gather(f32[32,256]{1,0:T(8,128)S(1)} %fusion.9), channel_id=1, replica_groups=mesh['cluster'=4,'sub'=8] {'sub'}, dimensions={0}, use_global_device_ids=true | all-gather | bytes 294912 | tf_op jit(solution)/shard_map/all_gather | solution.py:44
  41.4 3.5 collective-permute-start
  52.6 3.0 collective-permute-start.2
  56.7 5.7 %fusion.4 = f32[256,1024]{1,0:T(8,128)S(1)} fusion(f32[1024,256]{0,1:T(8,128)S(1)} %add_dynamic-update-slice_fusion.20, f32[1,1,1024,1024]{3,2,1,0:T(8,128)} %param.6), kind=kOutput, calls=%fused_computation.4 | convolution fusion | flops 3221225472 | bytes 6291456 | tf_op jit(solution)/shard_map/dot_general | solution.py:73
  62.5 4.6 %collective-permute-start.4 = (f32[128,256]{0,1:T(8,128)S(1)}, f32[128,256]{0,1:T(8,128)S(1)}, u32[]{:S(2)}, u32[]{:S(2)}) collective-permute-start(f32[128,256]{0,1:T(8,128)S(1)} %get-tuple-element.41), channel_id=1, source_target_pairs={{0,1},{1,2},{2,3},{3,4},{4,5},{5,6},{6,7},{8,9},{9,10},{10,11},{11... | collective-permute-start | bytes 393224 | tf_op jit(solution)/shard_map/ppermute | solution.py:13
  68.4 4.4 %collective-permute-start.6 = (f32[128,256]{0,1:T(8,128)S(1)}, f32[128,256]{0,1:T(8,128)S(1)}, u32[]{:S(2)}, u32[]{:S(2)}) collective-permute-start(f32[128,256]{0,1:T(8,128)S(1)} %get-tuple-element.40), channel_id=1, source_target_pairs={{0,8},{8,16},{16,24},{1,9},{9,17},{17,25},{2,10},{10,18},{18,26},{... | collective-permute-start | bytes 393224 | tf_op jit(solution)/shard_map/ppermute | solution.py:13
  74.2 6.1 %collective-permute-done.5 = f32[128,256]{0,1:T(8,128)S(1)} collective-permute-done((f32[128,256]{0,1:T(8,128)S(1)}, f32[128,256]{0,1:T(8,128)S(1)}, u32[]{:S(2)}, u32[]{:S(2)}) %collective-permute-start.5) | collective-permute-done | bytes 131104 | tf_op jit(solution)/shard_map/ppermute | solution.py:13
  80.8 42.1 %all-reduce.2 = (f32[256]{0:T(256)S(1)}, f32[256]{0:T(256)S(1)}) all-reduce(f32[256]{0:T(256)S(1)} %get-tuple-element.11, f32[256]{0:T(256)S(1)} %get-tuple-element.10), channel_id=1, replica_groups=mesh['cluster'=4,'sub'=8] {'cluster','sub'}, use_global_device_ids=true, to_apply=%region_1.0 | all-reduce | flops 512 | bytes 4096 | tf_op jit(solution)/shard_map/psum | solution.py:51
  125.3 30.9 %all_gather.10 = f32[256,256]{1,0:T(8,128)S(1)} all-gather(f32[32,256]{1,0:T(8,128)S(1)} %convolution_bitcast_fusion.4), channel_id=1, replica_groups=mesh['cluster'=4,'sub'=8] {'sub'}, dimensions={0}, use_global_device_ids=true | all-gather | bytes 294912 | tf_op jit(solution)/shard_map/all_gather | solution.py:44
  157.9 3.3 collective-permute-start.8
  166.3 3.2 collective-permute-start.10
  171.2 3.7 %fusion.2 = f32[256,1024]{1,0:T(8,128)S(1)} fusion(f32[1024,256]{0,1:T(8,128)S(1)} %add_dynamic-update-slice_fusion.12, f32[1,1,1024,1024]{3,2,1,0:T(8,128)S(1)} %copy-done.1), kind=kOutput, calls=%fused_computation.2 | convolution fusion | flops 3221225472 | bytes 6291456 | tf_op jit(solution)/shard_map/dot_general | solution.py:73
  175.0 4.8 %collective-permute-start.12 = (f32[128,256]{0,1:T(8,128)S(1)}, f32[128,256]{0,1:T(8,128)S(1)}, u32[]{:S(2)}, u32[]{:S(2)}) collective-permute-start(f32[128,256]{0,1:T(8,128)S(1)} %get-tuple-element.33), channel_id=1, source_target_pairs={{0,1},{1,2},{2,3},{3,4},{4,5},{5,6},{6,7},{8,9},{9,10},{10,11},{11... | collective-permute-start | bytes 393224 | tf_op jit(solution)/shard_map/ppermute | solution.py:13
  185.6 6.2 %collective-permute-done.13 = f32[128,256]{0,1:T(8,128)S(1)} collective-permute-done((f32[128,256]{0,1:T(8,128)S(1)}, f32[128,256]{0,1:T(8,128)S(1)}, u32[]{:S(2)}, u32[]{:S(2)}) %collective-permute-start.13) | collective-permute-done | bytes 131104 | tf_op jit(solution)/shard_map/ppermute | solution.py:13
  193.3 41.8 %all-reduce.1 = (f32[256]{0:T(256)S(1)}, f32[256]{0:T(256)S(1)}) all-reduce(f32[256]{0:T(256)S(1)} %get-tuple-element.9, f32[256]{0:T(256)S(1)} %get-tuple-element.8), channel_id=1, replica_groups=mesh['cluster'=4,'sub'=8] {'cluster','sub'}, use_global_device_ids=true, to_apply=%region_5.0 | all-reduce | flops 512 | bytes 4096 | tf_op jit(solution)/shard_map/psum | solution.py:51
  237.6 30.9 %all_gather.11 = f32[256,256]{1,0:T(8,128)S(1)} all-gather(f32[32,256]{1,0:T(8,128)S(1)} %convolution_bitcast_fusion.3), channel_id=1, replica_groups=mesh['cluster'=4,'sub'=8] {'sub'}, dimensions={0}, use_global_device_ids=true | all-gather | bytes 294912 | tf_op jit(solution)/shard_map/all_gather | solution.py:44
  270.1 3.2 collective-permute-start.16
  278.5 3.0 collective-permute-start.18
  283.3 3.7 %fusion = f32[256,1024]{1,0:T(8,128)S(1)} fusion(f32[1024,256]{0,1:T(8,128)S(1)} %add_dynamic-update-slice_fusion.4, f32[1,1,1024,1024]{3,2,1,0:T(8,128)S(1)} %copy-done.2), kind=kOutput, calls=%fused_computation | convolution fusion | flops 3221225472 | bytes 6291456 | tf_op jit(solution)/shard_map/dot_general | solution.py:73
  287.2 5.0 %collective-permute-start.20 = (f32[128,256]{0,1:T(8,128)S(1)}, f32[128,256]{0,1:T(8,128)S(1)}, u32[]{:S(2)}, u32[]{:S(2)}) collective-permute-start(f32[128,256]{0,1:T(8,128)S(1)} %get-tuple-element.25), channel_id=1, source_target_pairs={{0,1},{1,2},{2,3},{3,4},{4,5},{5,6},{6,7},{8,9},{9,10},{10,11},{11... | collective-permute-start | bytes 393224 | tf_op jit(solution)/shard_map/ppermute | solution.py:13
  293.5 3.0 collective-permute-start.22
  298.1 6.3 %collective-permute-done.21 = f32[128,256]{0,1:T(8,128)S(1)} collective-permute-done((f32[128,256]{0,1:T(8,128)S(1)}, f32[128,256]{0,1:T(8,128)S(1)}, u32[]{:S(2)}, u32[]{:S(2)}) %collective-permute-start.21) | collective-permute-done | bytes 131104 | tf_op jit(solution)/shard_map/ppermute | solution.py:13
  305.6 41.7 %all-reduce = (f32[256]{0:T(256)S(1)}, f32[256]{0:T(256)S(1)}) all-reduce(f32[256]{0:T(256)S(1)} %get-tuple-element.7, f32[256]{0:T(256)S(1)} %get-tuple-element.6), channel_id=1, replica_groups=mesh['cluster'=4,'sub'=8] {'cluster','sub'}, use_global_device_ids=true, to_apply=%region_9.0 | all-reduce | flops 512 | bytes 4096 | tf_op jit(solution)/shard_map/psum | solution.py:51
  347.3 4.1 %subtract_bitcast_fusion = (f32[1,1,1024,256]{2,3,1,0:T(8,128)}, f32[1,1,1024,256]{2,3,1,0:T(8,128)}) fusion(f32[1024,256]{0,1:T(8,128)S(1)} %multiply_subtract_fusion, f32[1024,256]{0,1:T(8,128)} %copy-done.9, f32[256]{0:T(256)S(1)} %get-tuple-element.19, f32[256]{0:T(256)S(1)} %get-tuple-element.18, f32[1024,256]{0,1:T(8,128)S(1)} %copy-done.4, ...), kind=kLoop, calls=%fused_computation.19 | loop fusion | flops 3932160 | bytes 9442304 | tf_op jit(solution)/shard_map/broadcast_in_dim | solution.py:95
  (121 shorter events, 55.6 us)
Async XLA Ops:
  41.4 7.3 %collective-permute-start = (f32[128,256]{0,1:T(8,128)S(1)}, f32[128,256]{0,1:T(8,128)S(1)}, u32[]{:S(2)}, u32[]{:S(2)}) collective-permute-start(f32[128,256]{0,1:T(8,128)S(1)} %constant_dynamic-slice_fusion.11), channel_id=1, source_target_pairs={{0,1},{1,2},{2,3},{3,4},{4,5},{5,6},{6,7},{8,9},{9,10},{10,11},{11... | collective-permute-start | bytes 393224 | tf_op jit(solution)/shard_map/ppermute | solution.py:13
  48.8 6.9 %collective-permute-start.1 = (f32[128,256]{0,1:T(8,128)S(1)}, f32[128,256]{0,1:T(8,128)S(1)}, u32[]{:S(2)}, u32[]{:S(2)}) collective-permute-start(f32[128,256]{0,1:T(8,128)S(1)} %get-tuple-element.46), channel_id=1, source_target_pairs={{1,0},{2,1},{3,2},{4,3},{5,4},{6,5},{7,6},{9,8},{10,9},{11,10},{12... | collective-permute-start | bytes 393224 | tf_op jit(solution)/shard_map/ppermute | solution.py:13
  51.3 5.3 %collective-permute-start.3 = (f32[128,256]{0,1:T(8,128)S(1)}, f32[128,256]{0,1:T(8,128)S(1)}, u32[]{:S(2)}, u32[]{:S(2)}) collective-permute-start(f32[128,256]{0,1:T(8,128)S(1)} %get-tuple-element.43), channel_id=1, source_target_pairs={{8,0},{16,8},{24,16},{9,1},{17,9},{25,17},{10,2},{18,10},{26,18},{... | collective-permute-start | bytes 393224 | tf_op jit(solution)/shard_map/ppermute | solution.py:13
  52.6 4.0 %collective-permute-start.2 = (f32[128,256]{0,1:T(8,128)S(1)}, f32[128,256]{0,1:T(8,128)S(1)}, u32[]{:S(2)}, u32[]{:S(2)}) collective-permute-start(f32[128,256]{0,1:T(8,128)S(1)} %get-tuple-element.44), channel_id=1, source_target_pairs={{0,8},{8,16},{16,24},{1,9},{9,17},{17,25},{2,10},{10,18},{18,26},{... | collective-permute-start | bytes 393224 | tf_op jit(solution)/shard_map/ppermute | solution.py:13
  62.5 11.6 %collective-permute-start.4 = (f32[128,256]{0,1:T(8,128)S(1)}, f32[128,256]{0,1:T(8,128)S(1)}, u32[]{:S(2)}, u32[]{:S(2)}) collective-permute-start(f32[128,256]{0,1:T(8,128)S(1)} %get-tuple-element.41), channel_id=1, source_target_pairs={{0,1},{1,2},{2,3},{3,4},{4,5},{5,6},{6,7},{8,9},{9,10},{10,11},{11... | collective-permute-start | bytes 393224 | tf_op jit(solution)/shard_map/ppermute | solution.py:13
  67.1 13.3 %collective-permute-start.7 = (f32[128,256]{0,1:T(8,128)S(1)}, f32[128,256]{0,1:T(8,128)S(1)}, u32[]{:S(2)}, u32[]{:S(2)}) collective-permute-start(f32[128,256]{0,1:T(8,128)S(1)} %get-tuple-element.39), channel_id=1, source_target_pairs={{8,0},{16,8},{24,16},{9,1},{17,9},{25,17},{10,2},{18,10},{26,18},{... | collective-permute-start | bytes 393224 | tf_op jit(solution)/shard_map/ppermute | solution.py:13
  68.4 12.0 %collective-permute-start.6 = (f32[128,256]{0,1:T(8,128)S(1)}, f32[128,256]{0,1:T(8,128)S(1)}, u32[]{:S(2)}, u32[]{:S(2)}) collective-permute-start(f32[128,256]{0,1:T(8,128)S(1)} %get-tuple-element.40), channel_id=1, source_target_pairs={{0,8},{8,16},{16,24},{1,9},{9,17},{17,25},{2,10},{10,18},{18,26},{... | collective-permute-start | bytes 393224 | tf_op jit(solution)/shard_map/ppermute | solution.py:13
  72.8 7.6 %collective-permute-start.5 = (f32[128,256]{0,1:T(8,128)S(1)}, f32[128,256]{0,1:T(8,128)S(1)}, u32[]{:S(2)}, u32[]{:S(2)}) collective-permute-start(f32[128,256]{0,1:T(8,128)S(1)} %get-tuple-element.42), channel_id=1, source_target_pairs={{1,0},{2,1},{3,2},{4,3},{5,4},{6,5},{7,6},{9,8},{10,9},{11,10},{12... | collective-permute-start | bytes 393224 | tf_op jit(solution)/shard_map/ppermute | solution.py:13
  157.9 5.8 %collective-permute-start.8 = (f32[128,256]{0,1:T(8,128)S(1)}, f32[128,256]{0,1:T(8,128)S(1)}, u32[]{:S(2)}, u32[]{:S(2)}) collective-permute-start(f32[128,256]{0,1:T(8,128)S(1)} %constant_dynamic-slice_fusion.4), channel_id=1, source_target_pairs={{0,1},{1,2},{2,3},{3,4},{4,5},{5,6},{6,7},{8,9},{9,10},{10,11},{11... | collective-permute-start | bytes 393224 | tf_op jit(solution)/shard_map/ppermute | solution.py:13
  163.7 7.3 %collective-permute-start.9 = (f32[128,256]{0,1:T(8,128)S(1)}, f32[128,256]{0,1:T(8,128)S(1)}, u32[]{:S(2)}, u32[]{:S(2)}) collective-permute-start(f32[128,256]{0,1:T(8,128)S(1)} %get-tuple-element.38), channel_id=1, source_target_pairs={{1,0},{2,1},{3,2},{4,3},{5,4},{6,5},{7,6},{9,8},{10,9},{11,10},{12... | collective-permute-start | bytes 393224 | tf_op jit(solution)/shard_map/ppermute | solution.py:13
  165.0 6.1 %collective-permute-start.11 = (f32[128,256]{0,1:T(8,128)S(1)}, f32[128,256]{0,1:T(8,128)S(1)}, u32[]{:S(2)}, u32[]{:S(2)}) collective-permute-start(f32[128,256]{0,1:T(8,128)S(1)} %get-tuple-element.35), channel_id=1, source_target_pairs={{8,0},{16,8},{24,16},{9,1},{17,9},{25,17},{10,2},{18,10},{26,18},{... | collective-permute-start | bytes 393224 | tf_op jit(solution)/shard_map/ppermute | solution.py:13
  166.3 4.7 %collective-permute-start.10 = (f32[128,256]{0,1:T(8,128)S(1)}, f32[128,256]{0,1:T(8,128)S(1)}, u32[]{:S(2)}, u32[]{:S(2)}) collective-permute-start(f32[128,256]{0,1:T(8,128)S(1)} %get-tuple-element.36), channel_id=1, source_target_pairs={{0,8},{8,16},{16,24},{1,9},{9,17},{17,25},{2,10},{10,18},{18,26},{... | collective-permute-start | bytes 393224 | tf_op jit(solution)/shard_map/ppermute | solution.py:13
  175.0 10.6 %collective-permute-start.12 = (f32[128,256]{0,1:T(8,128)S(1)}, f32[128,256]{0,1:T(8,128)S(1)}, u32[]{:S(2)}, u32[]{:S(2)}) collective-permute-start(f32[128,256]{0,1:T(8,128)S(1)} %get-tuple-element.33), channel_id=1, source_target_pairs={{0,1},{1,2},{2,3},{3,4},{4,5},{5,6},{6,7},{8,9},{9,10},{10,11},{11... | collective-permute-start | bytes 393224 | tf_op jit(solution)/shard_map/ppermute | solution.py:13
  179.8 12.1 %collective-permute-start.15 = (f32[128,256]{0,1:T(8,128)S(1)}, f32[128,256]{0,1:T(8,128)S(1)}, u32[]{:S(2)}, u32[]{:S(2)}) collective-permute-start(f32[128,256]{0,1:T(8,128)S(1)} %get-tuple-element.31), channel_id=1, source_target_pairs={{8,0},{16,8},{24,16},{9,1},{17,9},{25,17},{10,2},{18,10},{26,18},{... | collective-permute-start | bytes 393224 | tf_op jit(solution)/shard_map/ppermute | solution.py:13
  181.1 10.7 %collective-permute-start.14 = (f32[128,256]{0,1:T(8,128)S(1)}, f32[128,256]{0,1:T(8,128)S(1)}, u32[]{:S(2)}, u32[]{:S(2)}) collective-permute-start(f32[128,256]{0,1:T(8,128)S(1)} %get-tuple-element.32), channel_id=1, source_target_pairs={{0,8},{8,16},{16,24},{1,9},{9,17},{17,25},{2,10},{10,18},{18,26},{... | collective-permute-start | bytes 393224 | tf_op jit(solution)/shard_map/ppermute | solution.py:13
  184.2 7.7 %collective-permute-start.13 = (f32[128,256]{0,1:T(8,128)S(1)}, f32[128,256]{0,1:T(8,128)S(1)}, u32[]{:S(2)}, u32[]{:S(2)}) collective-permute-start(f32[128,256]{0,1:T(8,128)S(1)} %get-tuple-element.34), channel_id=1, source_target_pairs={{1,0},{2,1},{3,2},{4,3},{5,4},{6,5},{7,6},{9,8},{10,9},{11,10},{12... | collective-permute-start | bytes 393224 | tf_op jit(solution)/shard_map/ppermute | solution.py:13
  270.1 5.7 %collective-permute-start.16 = (f32[128,256]{0,1:T(8,128)S(1)}, f32[128,256]{0,1:T(8,128)S(1)}, u32[]{:S(2)}, u32[]{:S(2)}) collective-permute-start(f32[128,256]{0,1:T(8,128)S(1)} %constant_dynamic-slice_fusion), channel_id=1, source_target_pairs={{0,1},{1,2},{2,3},{3,4},{4,5},{5,6},{6,7},{8,9},{9,10},{10,11},{11... | collective-permute-start | bytes 393224 | tf_op jit(solution)/shard_map/ppermute | solution.py:13
  275.9 7.3 %collective-permute-start.17 = (f32[128,256]{0,1:T(8,128)S(1)}, f32[128,256]{0,1:T(8,128)S(1)}, u32[]{:S(2)}, u32[]{:S(2)}) collective-permute-start(f32[128,256]{0,1:T(8,128)S(1)} %get-tuple-element.30), channel_id=1, source_target_pairs={{1,0},{2,1},{3,2},{4,3},{5,4},{6,5},{7,6},{9,8},{10,9},{11,10},{12... | collective-permute-start | bytes 393224 | tf_op jit(solution)/shard_map/ppermute | solution.py:13
  277.2 6.1 %collective-permute-start.19 = (f32[128,256]{0,1:T(8,128)S(1)}, f32[128,256]{0,1:T(8,128)S(1)}, u32[]{:S(2)}, u32[]{:S(2)}) collective-permute-start(f32[128,256]{0,1:T(8,128)S(1)} %get-tuple-element.27), channel_id=1, source_target_pairs={{8,0},{16,8},{24,16},{9,1},{17,9},{25,17},{10,2},{18,10},{26,18},{... | collective-permute-start | bytes 393224 | tf_op jit(solution)/shard_map/ppermute | solution.py:13
  278.5 4.7 %collective-permute-start.18 = (f32[128,256]{0,1:T(8,128)S(1)}, f32[128,256]{0,1:T(8,128)S(1)}, u32[]{:S(2)}, u32[]{:S(2)}) collective-permute-start(f32[128,256]{0,1:T(8,128)S(1)} %get-tuple-element.28), channel_id=1, source_target_pairs={{0,8},{8,16},{16,24},{1,9},{9,17},{17,25},{2,10},{10,18},{18,26},{... | collective-permute-start | bytes 393224 | tf_op jit(solution)/shard_map/ppermute | solution.py:13
  287.2 10.9 %collective-permute-start.20 = (f32[128,256]{0,1:T(8,128)S(1)}, f32[128,256]{0,1:T(8,128)S(1)}, u32[]{:S(2)}, u32[]{:S(2)}) collective-permute-start(f32[128,256]{0,1:T(8,128)S(1)} %get-tuple-element.25), channel_id=1, source_target_pairs={{0,1},{1,2},{2,3},{3,4},{4,5},{5,6},{6,7},{8,9},{9,10},{10,11},{11... | collective-permute-start | bytes 393224 | tf_op jit(solution)/shard_map/ppermute | solution.py:13
  292.2 12.4 %collective-permute-start.23 = (f32[128,256]{0,1:T(8,128)S(1)}, f32[128,256]{0,1:T(8,128)S(1)}, u32[]{:S(2)}, u32[]{:S(2)}) collective-permute-start(f32[128,256]{0,1:T(8,128)S(1)} %get-tuple-element.23), channel_id=1, source_target_pairs={{8,0},{16,8},{24,16},{9,1},{17,9},{25,17},{10,2},{18,10},{26,18},{... | collective-permute-start | bytes 393224 | tf_op jit(solution)/shard_map/ppermute | solution.py:13
  293.5 11.0 %collective-permute-start.22 = (f32[128,256]{0,1:T(8,128)S(1)}, f32[128,256]{0,1:T(8,128)S(1)}, u32[]{:S(2)}, u32[]{:S(2)}) collective-permute-start(f32[128,256]{0,1:T(8,128)S(1)} %get-tuple-element.24), channel_id=1, source_target_pairs={{0,8},{8,16},{16,24},{1,9},{9,17},{17,25},{2,10},{10,18},{18,26},{... | collective-permute-start | bytes 393224 | tf_op jit(solution)/shard_map/ppermute | solution.py:13
  296.5 8.0 %collective-permute-start.21 = (f32[128,256]{0,1:T(8,128)S(1)}, f32[128,256]{0,1:T(8,128)S(1)}, u32[]{:S(2)}, u32[]{:S(2)}) collective-permute-start(f32[128,256]{0,1:T(8,128)S(1)} %get-tuple-element.26), channel_id=1, source_target_pairs={{1,0},{2,1},{3,2},{4,3},{5,4},{6,5},{7,6},{9,8},{10,9},{11,10},{12... | collective-permute-start | bytes 393224 | tf_op jit(solution)/shard_map/ppermute | solution.py:13
  (12 other events, 463.4 us)
where the time goes:
time: 358 us; the launch traced here: 356 us
  blocking collectives  220 us (61%)
  starting transfers between devices  59.7 us (17%)
  waiting for transfers between devices  27.5 us (8%)
  matrix products  22.8 us (6%)
  other arithmetic  11.4 us (3%)
  local copies, waits for them, and re-layouts  11 us (3%)
  between operations  4.08 us (1%)
    psum x3, blocking collectives, paired_dots(): lax.psum((jnp.sum(first * second, axis=0), jnp.sum(third * second, axis=0...  126 us
    all_gather x3, blocking collectives, precondition(): lax.all_gather(coarse, 'sub', axis=0, tiled=True)  94.3 us
    ppermute x24, starting transfers between devices, from_behind(): lax.ppermute(value, axis, [(source, source + steps) for source in range(i...  59.7 us
    ppermute x24, waiting for transfers between devices, from_behind(): lax.ppermute(value, axis, [(source, source + steps) for source in range(i...  27.5 us
    dot_general x3, matrix products, operator(): product = jnp.dot(matrix, inner, precision=lax.Precision.HIGHEST)  13.2 us
    unnamed x33, local copies, waits for them, and re-layouts  8.69 us
  transfers between devices with their start and end apart: 24, of which 8 were waited for; matrix products, arithmetic and copies ran while one was open for 1% of the time, Pallas kernels for 0%

commit v1 on v0

v1 whole, which is shorter than its diff:
```python
import jax
import jax.numpy as jnp
from jax import lax
from jax.sharding import PartitionSpec as P

BLOCK = 128
ITERS = 3
PAD = 8
HI = lax.Precision.HIGHEST


def mm(left, right):
    return jnp.dot(left, right, precision=HI, preferred_element_type=jnp.float32)


def mm_t(left, right):
    return lax.dot_general(
        left, right, (((0,), (0,)), ((), ())), precision=HI, preferred_element_type=jnp.float32
    )


def pair_list(count, parity, wrap=False):
    pairs = []
    for low in range(parity, count - 1, 2):
        pairs += [(low, low + 1), (low + 1, low)]
    if wrap and parity == 1 and count > 2:
        pairs += [(count - 1, 0), (0, count - 1)]
    return pairs


def rows_of(field, start, count=BLOCK):
    return lax.dynamic_slice_in_dim(field, start, count, 0)


def shards(compliance, loads, modes, coarse_inverse, face_block, edge_rows):
    matrix = compliance[0, 0]
    rhs = loads[0, 0]
    basis = modes[0, 0]
    inverse_rows = coarse_inverse[0]
    nmodes, order = basis.shape
    width = rhs.shape[1]
    nclus, nsub = lax.axis_size("cluster"), lax.axis_size("sub")
    clus, sub = lax.axis_index("cluster"), lax.axis_index("sub")
    faces = face_block[clus, sub]
    row_ids = jnp.arange(BLOCK, dtype=jnp.int32)

    links = []
    for axis, index, count, lower, upper, kind in (
        ("sub", sub, nsub, 0, 1, 0),
        ("cluster", clus, nclus, 2, 3, 1),
    ):
        for parity in (0, 1):
            is_low = lax.rem(index + parity, 2) == 0
            partner = jnp.where(is_low, index + 1, index - 1)
            valid = (partner >= 0) & (partner < count)
            first = jnp.clip(jnp.minimum(index, partner), 0, count - 1)
            at = (clus, first) if kind == 0 else (first, sub)
            length = jnp.where(valid, edge_rows[at[0], at[1], kind], 0)
            start = jnp.where(is_low, faces[upper], faces[lower]) * BLOCK
            mask = (row_ids < length).astype(jnp.float32)[:, None]
            links.append((axis, pair_list(count, parity), start, mask))
    order_of_sends = (1, 0, 3, 2)

    def exchange(messages):
        got = [None] * 4
        for at in order_of_sends:
            got[at] = lax.ppermute(messages[at], links[at][0], links[at][1])
        return got

    def spread(payload, axis, count):
        blocks = jnp.broadcast_to(payload[None], (count,) + payload.shape)
        return lax.all_to_all(blocks, axis, 0, 0, tiled=False)

    def mirror(ymom, doubled):
        first = lax.ppermute(ymom, "cluster", pair_list(nclus, 0))
        if doubled:
            sums = ymom[nmodes:] + first[nmodes:]
            second = lax.ppermute(
                jnp.concatenate([ymom[:nmodes], sums], 0), "cluster", pair_list(nclus, 1, True)
            )
            sums = sums + second[nmodes:]
        else:
            second = lax.ppermute(ymom[:nmodes], "cluster", pair_list(nclus, 1))
            sums = lax.psum(ymom[nmodes:], "cluster") if ymom.shape[0] > nmodes else None
        return first[:nmodes], second[:nmodes], sums

    face_modes = [lax.dynamic_slice_in_dim(basis, link[2], BLOCK, 1) for link in links]
    messages = []
    for at, link in enumerate(links):
        parts = [rows_of(rhs, link[2]), jnp.pad(face_modes[at], ((0, 0), (0, width - BLOCK)))]
        if at < 2:
            parts.append(inverse_rows.reshape(-1, width))
        messages.append(jnp.concatenate(parts, 0))
    got = exchange(messages)
    kappa = mm(basis, rhs)
    gathered = spread(kappa, "sub", nsub).reshape(nsub * nmodes, width)

    inv = [inverse_rows] + [
        got[at][BLOCK + nmodes :].reshape(inverse_rows.shape) for at in (0, 1)
    ]
    three = jnp.concatenate(inv, 0)
    padded = jnp.pad(
        three.reshape(3 * nmodes, nsub, nmodes), ((0, 0), (0, 0), (0, PAD))
    ).reshape(3 * nmodes, nsub * (nmodes + PAD))
    picks = jnp.tile(
        jnp.concatenate([jnp.zeros((PAD, nmodes), jnp.float32), jnp.eye(PAD, dtype=jnp.float32)], 1),
        (1, nsub),
    )
    gather_map = jnp.concatenate([padded[:nmodes], picks, padded[nmodes:]], 0)

    extended = [basis]
    late = []
    for at, link in enumerate(links):
        theirs = got[at][BLOCK : BLOCK + nmodes, :BLOCK]
        weight = (0.5 * link[3][:, 0])[None, :]
        extended.append(
            lax.dynamic_update_slice(
                jnp.zeros((nmodes, order), jnp.float32), weight * theirs, (0, link[2])
            )
        )
        late.append(weight * face_modes[at])
    extended = jnp.concatenate(extended, 0)
    late = jnp.concatenate(late, 1)

    def add_faces(field, blocks):
        for link, block in zip(links, blocks):
            current = rows_of(field, link[2])
            field = lax.dynamic_update_slice_in_dim(field, current + block, link[2], 0)
        return field

    y3 = mm(three, gathered)
    y_c0, y_c1, _ = mirror(y3[:nmodes], False)
    eta = y3[:nmodes]
    stack = jnp.concatenate([y3, y_c0, y_c1], 0)
    base = add_faces(rhs, [0.5 * link[3] * g[:BLOCK] for link, g in zip(links, got)])
    vee = base + mm_t(extended, stack)
    resid = rhs
    doubled = nclus == 4

    betas, alphas, resids, etas, along = [], [], [], [], None
    rz_now = None
    history = []
    for step in range(ITERS):
        image = mm(matrix, vee)
        rz_part = jnp.sum(resid * resid, 0, keepdims=True) + jnp.sum(kappa * eta, 0, keepdims=True)
        curve_part = jnp.sum(vee * image, 0, keepdims=True)
        moments = jnp.concatenate(
            [rz_part, curve_part, jnp.zeros((PAD - 2, width), jnp.float32)], 0
        )
        own = [rows_of(image, link[2]) for link in links]
        got = exchange(own)
        q_image = add_faces(image, [0.5 * link[3] * g for link, g in zip(links, got)])
        resids.append(resid)
        etas.append(eta)
        if step + 1 < ITERS:
            coarse = mm(basis, image) + mm(late, jnp.concatenate(got, 0))
            gathered = spread(jnp.concatenate([coarse, moments], 0), "sub", nsub)
            y3 = mm(gather_map, gathered.reshape(nsub * (nmodes + PAD), width))
            y_c0, y_c1, sums = mirror(y3[: nmodes + PAD], doubled)
            ynew = y3[:nmodes]
            stack = jnp.concatenate([ynew, y3[nmodes + PAD :], y_c0, y_c1], 0)
            qq = add_faces(
                image, [link[3] * (g + 0.25 * f) for link, g, f in zip(links, got, own)]
            )
            tee = qq + mm_t(extended, stack)
        else:
            everyone = spread(moments, ("cluster", "sub"), nclus * nsub)
            sums = jnp.sum(everyone, 0)
            coarse = ynew = tee = None
        rz, curve = sums[0:1], sums[1:2]
        if step == 0:
            alpha = rz / curve
            along = (q_image, coarse, ynew, tee)
        else:
            beta = rz / rz_now
            alpha = rz / (curve - beta * rz / alphas[-1])
            betas.append(beta)
            along = tuple(
                None if new is None else new + beta * old
                for new, old in zip((q_image, coarse, ynew, tee), along)
            )
        alphas.append(alpha)
        rz_now = rz
        resid = resid - alpha * along[0]
        if step + 1 < ITERS:
            kappa = kappa - alpha * along[1]
            eta = eta - alpha * along[2]
            vee = vee - alpha * along[3]

    weights = [None] * ITERS
    running = None
    for step in reversed(range(ITERS)):
        running = alphas[step] if running is None else alphas[step] + betas[step] * running
        weights[step] = running
    total = sum(w * r for w, r in zip(weights, resids))
    coarse_total = sum(w * e for w, e in zip(weights, etas))
    answer = total + mm_t(basis, coarse_total)
    return (answer[None, None], resid[None, None])


def solution(mesh):
    return jax.shard_map(
        shards,
        mesh=mesh,
        in_specs=(
            P("cluster", "sub", None, None),
            P("cluster", "sub", None, None),
            P("cluster", "sub", None, None),
            P("cluster", "sub", None),
            P(),
            P(),
        ),
        out_specs=(P("cluster", "sub", None, None), P("cluster", "sub", None, None)),
        check_vma=False,
    )
```

time: 358 us -> 210 us (0.59)
  blocking collectives: 220 us -> 19.5 us
  other arithmetic: 11.4 us -> 45.5 us
  matrix products: 22.8 us -> 41.9 us
  local copies, waits for them, and re-layouts: 11 us -> 25.6 us
  waiting for transfers between devices: 27.5 us -> 13.6 us
  starting transfers between devices: 59.7 us -> 51.8 us
  between operations: 4.08 us -> 9.66 us
    psum x3 -> x0, blocking collectives: 126 us -> none  [paired_dots(): lax.psum((jnp.sum(first * second, axis=0), jnp.sum(third * second, axis=0...]
    all_gather x3 -> x0, blocking collectives: 94.3 us -> none  [precondition(): lax.all_gather(coarse, 'sub', axis=0, tiled=True)]
    ppermute x24 -> x22, starting transfers between devices: 59.7 us -> 33.1 us  [the longest x16 25.6 us: exchange(): got[at] = lax.ppermute(messages[at], links[at][0], links[at][1])]
    dynamic_update_slice x21 -> x23, other arithmetic: 0.74 us -> 25.8 us  [the longest x19 22.3 us: add_faces(): field = lax.dynamic_update_slice_in_dim(field, current + block, link[2], 0)]
    ppermute x24 -> x22, waiting for transfers between devices: 27.5 us -> 5.92 us  [the longest x16 5.39 us: exchange(): got[at] = lax.ppermute(messages[at], links[at][0], links[at][1])]
    all_to_all x0 -> x1, blocking collectives: none -> 19.5 us  [spread(): return lax.all_to_all(blocks, axis, 0, 0, tiled=False)]
    dot_general x12 -> x15, matrix products: 22.8 us -> 41.9 us  [the longest x11 28.9 us: mm(): jnp.dot(left, right, precision=HI, preferred_element_type=jnp.float32)]
    all_to_all x0 -> x3, starting transfers between devices: none -> 18.8 us  [spread(): return lax.all_to_all(blocks, axis, 0, 0, tiled=False)]
  transfers between devices with their start and end apart: 24 -> 25, of which waited for: 8 -> 7; matrix products, arithmetic and copies ran while one was open for 1% -> 24% of each run, Pallas kernels for 0% -> 0%
where the time goes in v1:
time: 210 us; the launch traced here: 208 us
  starting transfers between devices  51.8 us (25%)
  other arithmetic  45.5 us (22%)
  matrix products  41.9 us (20%)
  local copies, waits for them, and re-layouts  25.6 us (12%)
  blocking collectives  19.5 us (9%)
  waiting for transfers between devices  13.6 us (6%)
  between operations  9.66 us (5%)
    dot_general x11, matrix products, mm(): jnp.dot(left, right, precision=HI, preferred_element_type=jnp.float32)  28.9 us
    ppermute x16, starting transfers between devices, exchange(): got[at] = lax.ppermute(messages[at], links[at][0], links[at][1])  25.6 us
    dynamic_update_slice x19, other arithmetic, add_faces(): field = lax.dynamic_update_slice_in_dim(field, current + block, link[2], 0)  22.3 us
    all_to_all x1, blocking collectives, spread(): return lax.all_to_all(blocks, axis, 0, 0, tiled=False)  19.5 us
    all_to_all x3, starting transfers between devices, spread(): return lax.all_to_all(blocks, axis, 0, 0, tiled=False)  18.8 us
    dot_general x4, matrix products, mm_t(): lax.dot_general(left, right, (((0,), (0,)), ((), ())), precision=HI, pref...  13 us
    unnamed x154, local copies, waits for them, and re-layouts  10.5 us
    all_to_all x3, waiting for transfers between devices, spread(): return lax.all_to_all(blocks, axis, 0, 0, tiled=False)  7.71 us
  transfers between devices with their start and end apart: 25, of which 7 were waited for; matrix products, arithmetic and copies ran while one was open for 24% of the time, Pallas kernels for 0%

profile of v1, /device:TPU:0, one launch (start us, length us, event | category | flops | bytes accessed | tf_op | source)
XLA Modules:
  0.0 207.7 jit_solution(17582133673757076029)
XLA Ops:
  0.7 2.0 fusion.56
  3.4 7.3 %all-to-all-start = ((f32[8,32,256]{2,1,0:T(8,128)}), f32[8,32,256]{2,1,0:T(8,128)S(1)}, u32[]{:S(2)}, u32[]{:S(2)}) async-start(f32[8,32,256]{2,1,0:T(8,128)} %broadcast_in_dim.18), calls=%async_computation | async-start | bytes 524288 | tf_op jit(solution)/shard_map/all_to_all | solution.py:72
  28.2 4.1 %collective-permute-start = (f32[192,256]{1,0:T(8,128)}, f32[192,256]{1,0:T(8,128)}, u32[]{:S(2)}, u32[]{:S(2)}) collective-permute-start(f32[192,256]{1,0:T(8,128)} %get-tuple-element.50), channel_id=1, source_target_pairs={{0,1},{1,0},{2,3},{3,2},{4,5},{5,4},{6,7},{7,6},{8,9},{9,8},{10,11... | collective-permute-start | bytes 589832 | tf_op jit(solution)/shard_map/ppermute | solution.py:67
  50.6 3.8 %collective-permute-start.4 = (f32[32,256]{1,0:T(8,128)S(1)}, f32[32,256]{1,0:T(8,128)S(1)}, u32[]{:S(2)}, u32[]{:S(2)}) collective-permute-start(f32[32,256]{1,0:T(8,128)S(1)} %get-tuple-element.48), channel_id=1, source_target_pairs={{0,8},{8,0},{16,24},{24,16},{1,9},{9,1},{17,25},{25,17},{2,10},{10... | collective-permute-start | bytes 98312 | tf_op jit(solution)/shard_map/ppermute | solution.py:75
  56.8 3.1 %convolution_add_fusion.2 = f32[1024,256]{1,0:T(8,128)S(1)} fusion(f32[1024,256]{1,0:T(8,128)} %copy-done.10, f32[160,1024]{1,0:T(8,128)S(1)} %constant_dynamic-update-slice_fusion.4, f32[32,256]{1,0:T(8,128)S(1)} %collective-permute-done.5, f32[32,256]{1,0:T(8,128)S(1)} %collective-permute-done.4, f32[96,256]{1,0:T(8,128)S(1)} %fusion.58), kind=kOutput, calls=%fused_computation.14 | convolution fusion | flops 503660544 | bytes 2916352 | tf_op jit(solution)/shard_map/dot_general | solution.py:17
  59.9 9.0 %fusion.4 = f32[256,1024]{1,0:T(8,128)S(1)} fusion(f32[1024,256]{1,0:T(8,128)S(1)} %convolution_add_fusion.2, f32[1,1,1024,1024]{3,2,1,0:T(8,128)} %param.6), kind=kOutput, calls=%fused_computation.4 | convolution fusion | flops 3221225472 | bytes 6291456 | tf_op jit(solution)/shard_map/dot_general | solution.py:13
  75.2 2.1 %collective-permute-start.8 = (f32[128,256]{1,0:T(8,128)S(1)}, f32[128,256]{1,0:T(8,128)S(1)}, u32[]{:S(2)}, u32[]{:S(2)}) collective-permute-start(f32[128,256]{1,0:T(8,128)S(1)} %get-tuple-element.34), channel_id=1, source_target_pairs={{0,8},{8,0},{16,24},{24,16},{1,9},{9,1},{17,25},{25,17},{2,10},{10... | collective-permute-start | bytes 393224 | tf_op jit(solution)/shard_map/ppermute | solution.py:67
  77.9 4.2 %collective-permute-start.6 = (f32[128,256]{1,0:T(8,128)S(1)}, f32[128,256]{1,0:T(8,128)S(1)}, u32[]{:S(2)}, u32[]{:S(2)}) collective-permute-start(f32[128,256]{1,0:T(8,128)S(1)} %get-tuple-element.36), channel_id=1, source_target_pairs={{0,1},{1,0},{2,3},{3,2},{4,5},{5,4},{6,7},{7,6},{8,9},{9,8},{10,11... | collective-permute-start | bytes 393224 | tf_op jit(solution)/shard_map/ppermute | solution.py:67
  82.4 4.6 %collective-permute-done.6 = f32[128,256]{1,0:T(8,128)S(1)} collective-permute-done((f32[128,256]{1,0:T(8,128)S(1)}, f32[128,256]{1,0:T(8,128)S(1)}, u32[]{:S(2)}, u32[]{:S(2)}) %collective-permute-start.6) | collective-permute-done | bytes 131104 | tf_op jit(solution)/shard_map/ppermute | solution.py:67
  89.7 5.6 %all-to-all-start.1 = ((f32[8,40,256]{2,1,0:T(8,128)}), f32[8,40,256]{2,1,0:T(8,128)}, u32[]{:S(2)}, u32[]{:S(2)}) async-start(f32[8,40,256]{2,1,0:T(8,128)} %broadcast_in_dim.20), calls=%async_computation.1 | async-start | bytes 655360 | tf_op jit(solution)/shard_map/all_to_all | solution.py:72
  103.9 1.9 all-to-all-done.1
  114.3 3.3 %convolution_add_fusion.1 = f32[1024,256]{1,0:T(8,128)S(1)} fusion(f32[1024,256]{1,0:T(8,128)} %get-tuple-element.31, f32[160,1024]{1,0:T(8,128)} %copy-done.9, f32[32,256]{1,0:T(8,128)S(1)} %slice.201, f32[32,256]{1,0:T(8,128)S(1)} %slice.200, f32[64,256]{1,0:T(8,128)S(1)} %slice.199, f32[32,256]{1,0:T(8,128)S(1)} %slice.195), kind=kOutput, calls=%fused_computation.13 | convolution fusion | flops 503701504 | bytes 2916352 | tf_op jit(solution)/shard_map/dot_general | solution.py:17
  118.6 7.9 %fusion.2 = f32[256,1024]{1,0:T(8,128)} fusion(f32[1,1,1024,1024]{3,2,1,0:T(8,128)S(1)} %copy-done.1, f32[1024,256]{1,0:T(8,128)S(1)} %convolution_add_fusion.2, f32[1024,256]{1,0:T(8,128)S(1)} %convolution_add_fusion.1, f32[256]{0:T(256)S(1)} %bitcast.180), kind=kOutput, calls=%fused_computation.2 | convolution fusion | flops 3221749760 | bytes 7341056 | tf_op jit(solution)/shard_map/dot_general | solution.py:13
  130.4 2.8 %collective-permute-start.14 = (f32[128,256]{1,0:T(8,128)S(1)}, f32[128,256]{1,0:T(8,128)S(1)}, u32[]{:S(2)}, u32[]{:S(2)}) collective-permute-start(f32[128,256]{1,0:T(8,128)S(1)} %get-tuple-element.29), channel_id=1, source_target_pairs={{0,8},{8,0},{16,24},{24,16},{1,9},{9,1},{17,25},{25,17},{2,10},{10... | collective-permute-start | bytes 393224 | tf_op jit(solution)/shard_map/ppermute | solution.py:67
  134.0 3.0 %multiply_reduce_fusion.3 = (f32[256]{0:T(256)S(1)}, f32[1024,256]{1,0:T(8,128)}, f32[256]{0:T(256)S(1)}) fusion(f32[1024,256]{1,0:T(8,128)} %add_dynamic-update-slice_fusion.12, f32[256]{0:T(256)} %bitcast.181, f32[1,1,1024,256]{3,2,1,0:T(8,128)S(1)} %copy-done.3, f32[256,1024]{0,1:T(8,128)S(1)} %copy.51, f32[1024,256]{1,0:T(8,128)S(1)} %convolution_add_fusion.2, ...), kind=kLoop, calls=%fused_computation.25 | loop fusion | flops 2096640 | bytes 6294528 | tf_op jit(solution)/shard_map/reduce_sum | solution.py:145
  140.4 5.9 %all-to-all-start.2 = ((f32[8,40,256]{2,1,0:T(8,128)}), f32[8,40,256]{2,1,0:T(8,128)}, u32[]{:S(2)}, u32[]{:S(2)}) async-start(f32[8,40,256]{2,1,0:T(8,128)} %broadcast_in_dim.22), calls=%async_computation.2 | async-start | bytes 655360 | tf_op jit(solution)/shard_map/all_to_all | solution.py:72
  150.7 5.8 %all-to-all-done.2 = f32[8,40,256]{2,1,0:T(8,128)} async-done(((f32[8,40,256]{2,1,0:T(8,128)}), f32[8,40,256]{2,1,0:T(8,128)}, u32[]{:S(2)}, u32[]{:S(2)}) %all-to-all-start.2) | async-done | bytes 327712 | tf_op jit(solution)/shard_map/all_to_all | solution.py:72
  156.5 1.9 fusion.90
  165.7 3.7 %fusion.10 = f32[1024,256]{1,0:T(8,128)S(1)} fusion(f32[1024,256]{1,0:T(8,128)} %get-tuple-element.25, f32[160,1024]{1,0:T(8,128)} %copy-done.9, f32[1024,256]{1,0:T(8,128)} %copy-done.5, f32[256]{0:T(256)S(1)} %bitcast.185, f32[256]{0:T(256)S(1)} %bitcast.174, f32[1024,256]{1,0:T(8,128)S(1)} %convolution_add_fusion.2, f32[256]{0:T(256)} %bitcast.182, ...), kind=kOutput, calls=%fused_computation.12 | convolution fusion | flops 505274368 | bytes 5016576 | tf_op jit(solution)/shard_map/dot_general | solution.py:17
  169.5 3.4 %multiply_reduce_fusion = (f32[256]{0:T(256)S(1)}, f32[256,1024]{0,1:T(8,128)S(1)}) fusion(f32[1024,256]{1,0:T(8,128)S(1)} %fusion.10, f32[1,1,1024,1024]{3,2,1,0:T(8,128)S(1)} %copy-done.2), kind=kOutput, calls=%fused_computation.20 | convolution fusion | flops 3221749504 | bytes 6292480 | tf_op jit(solution)/shard_map/dot_general | solution.py:13
  175.2 2.6 %collective-permute-start.20 = (f32[128,256]{1,0:T(8,128)S(1)}, f32[128,256]{1,0:T(8,128)S(1)}, u32[]{:S(2)}, u32[]{:S(2)}) collective-permute-start(f32[128,256]{1,0:T(8,128)S(1)} %get-tuple-element.22), channel_id=1, source_target_pairs={{0,8},{8,0},{16,24},{24,16},{1,9},{9,1},{17,25},{25,17},{2,10},{10... | collective-permute-start | bytes 393224 | tf_op jit(solution)/shard_map/ppermute | solution.py:67
  180.9 19.5 %all_to_all.20 = f32[32,8,256]{2,1,0:T(8,128)} all-to-all(f32[32,8,256]{2,1,0:T(8,128)S(1)} %broadcast_in_dim.24), channel_id=1, replica_groups=mesh['cluster'=4,'sub'=8] {'cluster','sub'}, dimensions={0} | all-to-all | bytes 524288 | tf_op jit(solution)/shard_map/all_to_all | solution.py:72
  202.2 2.5 %subtract_bitcast_fusion = f32[1,1,1024,256]{3,2,1,0:T(8,128)} fusion(f32[1024,256]{1,0:T(8,128)} %copy-done.12, f32[1024,256]{1,0:T(8,128)S(1)} %get-tuple-element.7, f32[1024,256]{1,0:T(8,128)S(1)} %copy-done.4, f32[256]{0:T(256)S(1)} %bitcast.197, f32[256]{0:T(256)S(1)} %bitcast.189, f32[256]{0:T(256)} %bitcast.177), kind=kLoop, calls=%fused_computation.19 | loop fusion | flops 1572864 | bytes 4197376 | tf_op jit(solution)/shard_map/broadcast_in_dim | solution.py:198
  204.8 3.0 %fusion.7 = f32[1,1,1024,256]{3,2,1,0:T(8,128)} fusion(f32[1024,256]{1,0:T(8,128)S(1)} %copy-done.4, f32[1024,256]{1,0:T(8,128)S(1)} %get-tuple-element.7, f32[256]{0:T(256)S(1)} %bitcast.190, f32[256]{0:T(256)S(1)} %bitcast.196, f32[256]{0:T(256)S(1)} %bitcast.195, f32[256]{0:T(256)S(1)} %bitcast.178, f32[1,1,32,1024]{3,2,1,0:T(8,128)S(1)} %copy-done.13, ...), kind=kOutput, calls=%fused_computation.8 | convolution fusion | flops 102850560 | bytes 4433920 | tf_op jit(solution)/shard_map/dot_general | solution.py:17
  (293 shorter events, 85.2 us)
Async XLA Ops:
  3.4 46.2 %all-to-all-start = ((f32[8,32,256]{2,1,0:T(8,128)}), f32[8,32,256]{2,1,0:T(8,128)S(1)}, u32[]{:S(2)}, u32[]{:S(2)}) async-start(f32[8,32,256]{2,1,0:T(8,128)} %broadcast_in_dim.18), calls=%async_computation | async-start | bytes 524288 | tf_op jit(solution)/shard_map/all_to_all | solution.py:72
  23.2 13.5 %collective-permute-start.2 = (f32[160,256]{1,0:T(8,128)S(1)}, f32[160,256]{1,0:T(8,128)}, u32[]{:S(2)}, u32[]{:S(2)}) collective-permute-start(f32[160,256]{1,0:T(8,128)S(1)} %select_maximum_fusion.3), channel_id=1, source_target_pairs={{0,8},{8,0},{16,24},{24,16},{1,9},{9,1},{17,25},{25,17},{2,10},{10... | collective-permute-start | bytes 491528 | tf_op jit(solution)/shard_map/ppermute | solution.py:67
  24.0 13.5 %collective-permute-start.3 = (f32[160,256]{1,0:T(8,128)}, f32[160,256]{1,0:T(8,128)}, u32[]{:S(2)}, u32[]{:S(2)}) collective-permute-start(f32[160,256]{1,0:T(8,128)} %select_maximum_fusion.2), channel_id=1, source_target_pairs={{8,16},{16,8},{9,17},{17,9},{10,18},{18,10},{11,19},{19,11},{12,20... | collective-permute-start | bytes 491528 | tf_op jit(solution)/shard_map/ppermute | solution.py:67
  26.8 12.6 %collective-permute-start.1 = (f32[192,256]{1,0:T(8,128)}, f32[192,256]{1,0:T(8,128)}, u32[]{:S(2)}, u32[]{:S(2)}) collective-permute-start(f32[192,256]{1,0:T(8,128)} %get-tuple-element.49), channel_id=1, source_target_pairs={{1,2},{2,1},{3,4},{4,3},{5,6},{6,5},{9,10},{10,9},{11,12},{12,11},... | collective-permute-start | bytes 589832 | tf_op jit(solution)/shard_map/ppermute | solution.py:67
  28.2 13.2 %collective-permute-start = (f32[192,256]{1,0:T(8,128)}, f32[192,256]{1,0:T(8,128)}, u32[]{:S(2)}, u32[]{:S(2)}) collective-permute-start(f32[192,256]{1,0:T(8,128)} %get-tuple-element.50), channel_id=1, source_target_pairs={{0,1},{1,0},{2,3},{3,2},{4,5},{5,4},{6,7},{7,6},{8,9},{9,8},{10,11... | collective-permute-start | bytes 589832 | tf_op jit(solution)/shard_map/ppermute | solution.py:67
  49.9 6.9 %collective-permute-start.5 = (f32[32,256]{1,0:T(8,128)S(1)}, f32[32,256]{1,0:T(8,128)S(1)}, u32[]{:S(2)}, u32[]{:S(2)}) collective-permute-start(f32[32,256]{1,0:T(8,128)S(1)} %get-tuple-element.48), channel_id=1, source_target_pairs={{8,16},{16,8},{9,17},{17,9},{10,18},{18,10},{11,19},{19,11},{12,20... | collective-permute-start | bytes 98312 | tf_op jit(solution)/shard_map/ppermute | solution.py:83
  50.6 6.2 %collective-permute-start.4 = (f32[32,256]{1,0:T(8,128)S(1)}, f32[32,256]{1,0:T(8,128)S(1)}, u32[]{:S(2)}, u32[]{:S(2)}) collective-permute-start(f32[32,256]{1,0:T(8,128)S(1)} %get-tuple-element.48), channel_id=1, source_target_pairs={{0,8},{8,0},{16,24},{24,16},{1,9},{9,1},{17,25},{25,17},{2,10},{10... | collective-permute-start | bytes 98312 | tf_op jit(solution)/shard_map/ppermute | solution.py:75
  74.5 7.9 %collective-permute-start.9 = (f32[128,256]{1,0:T(8,128)S(1)}, f32[128,256]{1,0:T(8,128)S(1)}, u32[]{:S(2)}, u32[]{:S(2)}) collective-permute-start(f32[128,256]{1,0:T(8,128)S(1)} %get-tuple-element.33), channel_id=1, source_target_pairs={{8,16},{16,8},{9,17},{17,9},{10,18},{18,10},{11,19},{19,11},{12,20... | collective-permute-start | bytes 393224 | tf_op jit(solution)/shard_map/ppermute | solution.py:67
  75.2 7.2 %collective-permute-start.8 = (f32[128,256]{1,0:T(8,128)S(1)}, f32[128,256]{1,0:T(8,128)S(1)}, u32[]{:S(2)}, u32[]{:S(2)}) collective-permute-start(f32[128,256]{1,0:T(8,128)S(1)} %get-tuple-element.34), channel_id=1, source_target_pairs={{0,8},{8,0},{16,24},{24,16},{1,9},{9,1},{17,25},{25,17},{2,10},{10... | collective-permute-start | bytes 393224 | tf_op jit(solution)/shard_map/ppermute | solution.py:67
  77.3 5.2 %collective-permute-start.7 = (f32[128,256]{1,0:T(8,128)S(1)}, f32[128,256]{1,0:T(8,128)S(1)}, u32[]{:S(2)}, u32[]{:S(2)}) collective-permute-start(f32[128,256]{1,0:T(8,128)S(1)} %get-tuple-element.35), channel_id=1, source_target_pairs={{1,2},{2,1},{3,4},{4,3},{5,6},{6,5},{9,10},{10,9},{11,12},{12,11},... | collective-permute-start | bytes 393224 | tf_op jit(solution)/shard_map/ppermute | solution.py:67
  77.9 9.1 %collective-permute-start.6 = (f32[128,256]{1,0:T(8,128)S(1)}, f32[128,256]{1,0:T(8,128)S(1)}, u32[]{:S(2)}, u32[]{:S(2)}) collective-permute-start(f32[128,256]{1,0:T(8,128)S(1)} %get-tuple-element.36), channel_id=1, source_target_pairs={{0,1},{1,0},{2,3},{3,2},{4,5},{5,4},{6,7},{7,6},{8,9},{9,8},{10,11... | collective-permute-start | bytes 393224 | tf_op jit(solution)/shard_map/ppermute | solution.py:67
  89.7 16.1 %all-to-all-start.1 = ((f32[8,40,256]{2,1,0:T(8,128)}), f32[8,40,256]{2,1,0:T(8,128)}, u32[]{:S(2)}, u32[]{:S(2)}) async-start(f32[8,40,256]{2,1,0:T(8,128)} %broadcast_in_dim.20), calls=%async_computation.1 | async-start | bytes 655360 | tf_op jit(solution)/shard_map/all_to_all | solution.py:72
  107.7 1.8 collective-permute-start.10
  109.5 3.5 %collective-permute-start.11 = (f32[40,256]{1,0:T(8,128)S(1)}, f32[40,256]{1,0:T(8,128)S(1)}, u32[]{:S(2)}, u32[]{:S(2)}) collective-permute-start(f32[40,256]{1,0:T(8,128)S(1)} %pad_maximum_fusion.6), channel_id=1, source_target_pairs={{8,16},{16,8},{24,0},{0,24},{9,17},{17,9},{25,1},{1,25},{10,18},{1... | collective-permute-start | bytes 122888 | tf_op jit(solution)/shard_map/ppermute | solution.py:78
  128.2 9.8 %collective-permute-start.12 = (f32[128,256]{1,0:T(8,128)S(1)}, f32[128,256]{1,0:T(8,128)S(1)}, u32[]{:S(2)}, u32[]{:S(2)}) collective-permute-start(f32[128,256]{1,0:T(8,128)S(1)} %get-tuple-element.27), channel_id=1, source_target_pairs={{0,1},{1,0},{2,3},{3,2},{4,5},{5,4},{6,7},{7,6},{8,9},{9,8},{10,11... | collective-permute-start | bytes 393224 | tf_op jit(solution)/shard_map/ppermute | solution.py:67
  129.7 8.3 %collective-permute-start.15 = (f32[128,256]{1,0:T(8,128)S(1)}, f32[128,256]{1,0:T(8,128)S(1)}, u32[]{:S(2)}, u32[]{:S(2)}) collective-permute-start(f32[128,256]{1,0:T(8,128)S(1)} %get-tuple-element.28), channel_id=1, source_target_pairs={{8,16},{16,8},{9,17},{17,9},{10,18},{18,10},{11,19},{19,11},{12,20... | collective-permute-start | bytes 393224 | tf_op jit(solution)/shard_map/ppermute | solution.py:67
  130.4 7.6 %collective-permute-start.14 = (f32[128,256]{1,0:T(8,128)S(1)}, f32[128,256]{1,0:T(8,128)S(1)}, u32[]{:S(2)}, u32[]{:S(2)}) collective-permute-start(f32[128,256]{1,0:T(8,128)S(1)} %get-tuple-element.29), channel_id=1, source_target_pairs={{0,8},{8,0},{16,24},{24,16},{1,9},{9,1},{17,25},{25,17},{2,10},{10... | collective-permute-start | bytes 393224 | tf_op jit(solution)/shard_map/ppermute | solution.py:67
  133.2 4.9 %collective-permute-start.13 = (f32[128,256]{1,0:T(8,128)S(1)}, f32[128,256]{1,0:T(8,128)S(1)}, u32[]{:S(2)}, u32[]{:S(2)}) collective-permute-start(f32[128,256]{1,0:T(8,128)S(1)} %get-tuple-element.30), channel_id=1, source_target_pairs={{1,2},{2,1},{3,4},{4,3},{5,6},{6,5},{9,10},{10,9},{11,12},{12,11},... | collective-permute-start | bytes 393224 | tf_op jit(solution)/shard_map/ppermute | solution.py:67
  140.4 16.1 %all-to-all-start.2 = ((f32[8,40,256]{2,1,0:T(8,128)}), f32[8,40,256]{2,1,0:T(8,128)}, u32[]{:S(2)}, u32[]{:S(2)}) async-start(f32[8,40,256]{2,1,0:T(8,128)} %broadcast_in_dim.22), calls=%async_computation.2 | async-start | bytes 655360 | tf_op jit(solution)/shard_map/all_to_all | solution.py:72
  158.4 1.8 collective-permute-start.16
  160.2 3.5 %collective-permute-start.17 = (f32[40,256]{1,0:T(8,128)S(1)}, f32[40,256]{1,0:T(8,128)S(1)}, u32[]{:S(2)}, u32[]{:S(2)}) collective-permute-start(f32[40,256]{1,0:T(8,128)S(1)} %pad_maximum_fusion.7), channel_id=1, source_target_pairs={{8,16},{16,8},{24,0},{0,24},{9,17},{17,9},{25,1},{1,25},{10,18},{1... | collective-permute-start | bytes 122888 | tf_op jit(solution)/shard_map/ppermute | solution.py:78
  173.1 6.0 %collective-permute-start.18 = (f32[128,256]{1,0:T(8,128)S(1)}, f32[128,256]{1,0:T(8,128)S(1)}, u32[]{:S(2)}, u32[]{:S(2)}) collective-permute-start(f32[128,256]{1,0:T(8,128)S(1)} %get-tuple-element.24), channel_id=1, source_target_pairs={{0,1},{1,0},{2,3},{3,2},{4,5},{5,4},{6,7},{7,6},{8,9},{9,8},{10,11... | collective-permute-start | bytes 393224 | tf_op jit(solution)/shard_map/ppermute | solution.py:67
  174.6 4.8 %collective-permute-start.21 = (f32[128,256]{1,0:T(8,128)S(1)}, f32[128,256]{1,0:T(8,128)S(1)}, u32[]{:S(2)}, u32[]{:S(2)}) collective-permute-start(f32[128,256]{1,0:T(8,128)S(1)} %get-tuple-element.21), channel_id=1, source_target_pairs={{8,16},{16,8},{9,17},{17,9},{10,18},{18,10},{11,19},{19,11},{12,20... | collective-permute-start | bytes 393224 | tf_op jit(solution)/shard_map/ppermute | solution.py:67
  175.2 4.0 %collective-permute-start.20 = (f32[128,256]{1,0:T(8,128)S(1)}, f32[128,256]{1,0:T(8,128)S(1)}, u32[]{:S(2)}, u32[]{:S(2)}) collective-permute-start(f32[128,256]{1,0:T(8,128)S(1)} %get-tuple-element.22), channel_id=1, source_target_pairs={{0,8},{8,0},{16,24},{24,16},{1,9},{9,1},{17,25},{25,17},{2,10},{10... | collective-permute-start | bytes 393224 | tf_op jit(solution)/shard_map/ppermute | solution.py:67
  (73 other events, 964.9 us)

commit v2 on v0

v2 whole, which is shorter than its diff:
```python
import jax
import jax.numpy as jnp
from jax import lax
from jax.experimental import pallas as pl
from jax.experimental.pallas import tpu as pltpu
from jax.sharding import PartitionSpec as P


BLOCK = 128
ITERS = 3
PAD = 8
ROWS = 256
F32 = jnp.float32
BF16 = jnp.bfloat16
VM = pl.BlockSpec(memory_space=pltpu.VMEM)
SM = pl.BlockSpec(memory_space=pltpu.SMEM)


def sds(*shape, dtype=F32):
    return jax.ShapeDtypeStruct(shape, dtype)


def call(body, outs, args, smem_in=(), smem_out=(), flops=1_000_000, mib=8):
    outs = list(outs)
    return pl.pallas_call(
        body,
        out_shape=outs,
        in_specs=[SM if at in smem_in else VM for at in range(len(args))],
        out_specs=[SM if at in smem_out else VM for at in range(len(outs))],
        compiler_params=pltpu.CompilerParams(vmem_limit_bytes=mib << 20),
        cost_estimate=pl.CostEstimate(
            flops=flops, bytes_accessed=1 << 20, transcendentals=0),
    )(*args)


def split(value):
    high = value.astype(BF16)
    return high, (value - high.astype(F32)).astype(BF16)


def dot(left, right):
    return jnp.dot(left, right, preferred_element_type=F32)


def dot3(left, right):
    return dot(left[0], right[0]) + (dot(left[0], right[1]) + dot(left[1], right[0]))


def dot6(left, right):
    return jnp.dot(left, right, precision=lax.Precision.HIGHEST, preferred_element_type=F32)


def pair_list(count, parity, wrap=False):
    pairs = []
    for low in range(parity, count - 1, 2):
        pairs += [(low, low + 1), (low + 1, low)]
    if wrap and parity == 1 and count > 2:
        pairs += [(count - 1, 0), (0, count - 1)]
    return pairs


def half(refs, rows):
    return refs[0][rows, :], refs[1][rows, :]


def start_body(face_block, edge_rows, rhs_in, basis_in, inverse_in, *outs):
    *messages, meta, kappa, spread, rhs, basis, inverse_rows, sems = outs
    copies = [
        pltpu.make_async_copy(source, target, sems.at[at])
        for at, (source, target) in enumerate(
            ((rhs_in, rhs), (basis_in, basis), (inverse_in, inverse_rows)))
    ]
    for copy in copies:
        copy.start()
    nmodes = basis.shape[0]
    width = rhs.shape[1]
    clus, sub = lax.axis_index("cluster"), lax.axis_index("sub")
    link = 0
    for index, count, lower, upper, kind in (
        (sub, face_block.shape[2], 0, 1, 0),
        (clus, face_block.shape[0], 2, 3, 1),
    ):
        for parity in (0, 1):
            is_low = lax.rem(index + parity, 2) == 0
            partner = jnp.where(is_low, index + 1, index - 1)
            valid = (partner >= 0) & (partner < count)
            first = jnp.clip(jnp.minimum(index, partner), 0, count - 1)
            place = (clus, first) if kind == 0 else (first, sub)
            meta[link] = face_block[clus, jnp.where(is_low, upper, lower), sub] * BLOCK
            meta[4 + link] = jnp.where(valid, edge_rows[place[0], kind, place[1]], 0)
            link += 1
    for copy in copies:
        copy.wait()
    for at, message in enumerate(messages):
        start = pl.multiple_of(meta[at], BLOCK)
        message[:BLOCK] = rhs[pl.ds(start, BLOCK), :]
        message[BLOCK : BLOCK + nmodes, :BLOCK] = basis[:, pl.ds(start, BLOCK)]
        if width > BLOCK:
            message[BLOCK : BLOCK + nmodes, BLOCK:] = jnp.zeros((nmodes, width - BLOCK), F32)
        if at < 2:
            message[BLOCK + nmodes :] = inverse_rows[...]
    value = dot6(basis[...], rhs[...])
    kappa[...] = value
    for at in range(spread.shape[0]):
        spread[at] = value


def prepare_body(matrix, c_hi, c_lo):
    @pl.loop(0, matrix.shape[0] // BLOCK)
    def _(at):
        rows = pl.ds(pl.multiple_of(at * BLOCK, BLOCK), BLOCK)
        c_hi[rows, :], c_lo[rows, :] = split(matrix[rows, :])


def masks_of(starts, at, width):
    ids = lax.broadcasted_iota(jnp.int32, (BLOCK, width), 0)
    return (ids < starts[4 + at]).astype(F32)


def setup_body(starts, rhs, basis, i0, i1, gathered, g0, g1, g2, g3,
               others, b_hi, b_lo, m_hi, m_lo, l_hi, l_lo, base):
    nmodes, _ = basis.shape
    skip = i0.shape[0] - nmodes
    others[:nmodes] = dot6(i0[skip:], gathered[...])
    others[nmodes:] = dot6(i1[skip:], gathered[...])
    width = rhs.shape[1]
    base[...] = rhs[...]
    m_hi[...], m_lo[...] = split(basis[...])
    b_hi[...] = jnp.zeros_like(b_hi)
    b_lo[...] = jnp.zeros_like(b_lo)
    own = basis[...].T
    b_hi[:, :nmodes], b_lo[:, :nmodes] = split(own)
    for at, got in enumerate((g0, g1, g2, g3)):
        start = pl.multiple_of(starts[at], BLOCK)
        rows = pl.ds(start, BLOCK)
        mask = 0.5 * masks_of(starts, at, width)
        base[rows, :] = base[rows, :] + mask * got[:BLOCK, :]
        theirs = got[BLOCK : BLOCK + nmodes, :BLOCK].T
        cols = slice((at + 1) * nmodes, (at + 2) * nmodes)
        b_hi[rows, cols], b_lo[rows, cols] = split(mask[:, :nmodes] * theirs)
        ids = lax.broadcasted_iota(jnp.int32, (nmodes, BLOCK), 1)
        weight = 0.5 * (ids < starts[4 + at]).astype(F32)
        cols = slice(at * BLOCK, (at + 1) * BLOCK)
        l_hi[:, cols], l_lo[:, cols] = split(weight * basis[:, pl.ds(start, BLOCK)])


def maps_body(c_hi, c_lo, b_hi, b_lo, k_hi, k_lo):
    k_hi[...], k_lo[...] = split(dot3((c_hi[...], c_lo[...]), (b_hi[...], b_lo[...])))


def copy_faces(starts, field, outs):
    for at, out in enumerate(outs):
        out[...] = field[pl.ds(pl.multiple_of(starts[at], BLOCK), BLOCK), :]


def first_y_body(inverse_rows, gathered, own):
    own[...] = dot6(inverse_rows[...], gathered[...])


def fold_body(everyone, out):
    total = everyone[0]
    for at in range(1, everyone.shape[0]):
        total = total + everyone[at]
    out[...] = total


def stacked(own, others, first, second):
    nmodes = others.shape[0] // 2
    return jnp.concatenate([own[:nmodes], others[...], first[:nmodes], second[:nmodes]], 0)


def first_apply_body(starts, base, c_hi, c_lo, b_hi, b_lo, own, others, first, second,
                     vee, image, *outs):
    ys = split(stacked(own, others, first, second))

    @pl.loop(0, base.shape[0] // ROWS)
    def _(at):
        rows = pl.ds(pl.multiple_of(at * ROWS, ROWS), ROWS)
        vee[rows, :] = base[rows, :] + dot3(half((b_hi, b_lo), rows), ys)

    image[...] = dot3((c_hi[...], c_lo[...]), split(vee[...]))

    copy_faces(starts, image, outs)


def column_sum(total):
    return jnp.sum(total, 0, keepdims=True)


def moment_rows(vee, image, resid, kappa, eta):
    width = resid.shape[1]

    def step(at, carry):
        rows = pl.ds(pl.multiple_of(at * BLOCK, BLOCK), BLOCK)
        value = resid[rows, :]
        squares = (value * value).reshape(-1, 8, width)
        curves = (vee[rows, :] * image[rows, :]).reshape(-1, 8, width)
        return carry[0] + jnp.sum(squares, 0), carry[1] + jnp.sum(curves, 0)

    zero = jnp.zeros((8, width), F32)
    rr, curve = lax.fori_loop(0, resid.shape[0] // BLOCK, step, (zero, zero))
    rz = column_sum(rr) + column_sum(kappa[...] * eta[...])
    curve = column_sum(curve)
    ids = lax.broadcasted_iota(jnp.int32, (PAD, width), 0)
    return jnp.where(ids == 0, rz, 0.0) + jnp.where(ids == 1, curve, 0.0)


def sums_body(m_hi, m_lo, vee, image, resid, kappa, eta, out):
    nmodes = kappa.shape[0]
    out[nmodes:] = moment_rows(vee, image, resid, kappa, eta)
    out[:nmodes] = dot3((m_hi[...], m_lo[...]), split(image[...]))


def coarse_late_body(main, l_hi, l_lo, g0, g1, g2, g3, spread):
    nmodes = l_hi.shape[0]
    total = main[:nmodes]
    for at, got in enumerate((g0, g1, g2, g3)):
        cols = slice(at * BLOCK, (at + 1) * BLOCK)
        total = total + dot3((l_hi[:, cols], l_lo[:, cols]), split(got[...]))
    for at in range(spread.shape[0]):
        spread[at, :nmodes] = total
        spread[at, nmodes:] = main[nmodes:]


def faces_body(starts, image, c_hi, c_lo, g0, g1, g2, g3, qonce, qtwice, prod):
    width = image.shape[1]
    qonce[...] = image[...]
    qtwice[...] = image[...]
    for at, got in enumerate((g0, g1, g2, g3)):
        rows = pl.ds(pl.multiple_of(starts[at], BLOCK), BLOCK)
        mask = masks_of(starts, at, width)
        mine = image[rows, :]
        qonce[rows, :] = mine + (0.5 * mask) * got[...]
        qtwice[rows, :] = mine + mask * (got[...] + 0.25 * mine)
    prod[...] = dot3((c_hi[...], c_lo[...]), split(qtwice[...]))


def y_body(inverse_rows, i0, i1, gathered, own, others, coarse):
    count, rows, _ = gathered.shape
    nmodes = rows - PAD
    blocks = jnp.concatenate([gathered[at, :nmodes] for at in range(count)], 0)
    own[:nmodes] = dot6(inverse_rows[...], blocks)
    skip = i0.shape[0] - nmodes
    others[:nmodes] = dot6(i0[skip:], blocks)
    others[nmodes:] = dot6(i1[skip:], blocks)
    total = gathered[0, nmodes:]
    for at in range(1, count):
        total = total + gathered[at, nmodes:]
    own[nmodes:] = total
    me = lax.axis_index("sub")
    coarse[...] = gathered[me, :nmodes]


def scalars(sums, rz_old, alpha_old):
    rz, curve = sums[0:1], sums[1:2]
    if rz_old is None:
        return rz / curve, None, rz
    beta = rz / rz_old
    return rz / (curve - beta * rz / alpha_old), beta, rz


def pack(alpha, beta, rz):
    ids = lax.broadcasted_iota(jnp.int32, (PAD, alpha.shape[1]), 0)
    out = jnp.where(ids == 0, alpha, 0.0) + jnp.where(ids == 2, rz, 0.0)
    return out if beta is None else out + jnp.where(ids == 1, beta, 0.0)


def make_image_body(has_old):
    def body(starts, image, prod, k_hi, k_lo, own, others, first, second, *rest):
        *rest, f0, f1, f2, f3 = rest
        nmodes = others.shape[0] // 2
        sums = own[nmodes:] + first[nmodes:] + second[nmodes:]
        if has_old:
            scal_old, along_old, image_new, along, scal = rest
            alpha, beta, rz = scalars(sums, scal_old[2:3], scal_old[0:1])
        else:
            image_new, along, scal = rest
            alpha, beta, rz = scalars(sums, None, None)
        scal[...] = pack(alpha, beta, rz)
        ys = split(stacked(own, others, first, second))

        @pl.loop(0, image.shape[0] // ROWS)
        def _(at):
            rows = pl.ds(pl.multiple_of(at * ROWS, ROWS), ROWS)
            value = prod[rows, :] + dot3(half((k_hi, k_lo), rows), ys)
            if has_old:
                value = value + beta * along_old[rows, :]
            along[rows, :] = value
            image_new[rows, :] = image[rows, :] - alpha * value

        copy_faces(starts, image_new, (f0, f1, f2, f3))

    return body


def make_update_body(has_old, last):
    def body(scal, vee, qtwice, b_hi, b_lo, own, others, first, second,
             resid, qonce, kappa, coarse, eta, image, m_hi, m_lo, *rest):
        if has_old:
            t_old, q_old, k_old, y_old = rest[:4]
            rest = rest[4:]
        vee_new, resid_new, kappa_new, eta_new, t_along, q_along, k_along, y_along, out = rest
        alpha, beta = scal[0:1], scal[1:2]
        nmodes = kappa.shape[0]
        ys = split(stacked(own, others, first, second))

        def move(old, value, older):
            if has_old:
                value = value + beta * older
            return value, old - alpha * value

        @pl.loop(0, vee.shape[0] // ROWS)
        def _(at):
            rows = pl.ds(pl.multiple_of(at * ROWS, ROWS), ROWS)
            value = qtwice[rows, :] + dot3(half((b_hi, b_lo), rows), ys)
            t_along[rows, :], vee_new[rows, :] = move(
                vee[rows, :], value, t_old[rows, :] if has_old else None)
            q_along[rows, :], resid_new[rows, :] = move(
                resid[rows, :], qonce[rows, :], q_old[rows, :] if has_old else None)

        k_along[...], kappa_new[...] = move(kappa[...], coarse[...], k_old[...] if has_old else None)
        y_along[...], eta_new[...] = move(eta[...], own[:nmodes], y_old[...] if has_old else None)
        moments = moment_rows(vee_new, image, resid_new, kappa_new, eta_new)
        if last:
            for at in range(out.shape[0]):
                out[at] = moments
        else:
            out[:nmodes] = dot3((m_hi[...], m_lo[...]), split(image[...]))
            out[nmodes:] = moments

    return body


def finish_body(starts, sums, scal0, scal1, b_hi, b_lo, e0, e1, e2, r0, r1, r2, along, image,
                g0, g1, g2, g3, answer, resid):
    at = pl.program_id(0)
    rows = pl.ds(pl.multiple_of(at * ROWS, ROWS), ROWS)
    nmodes = e0.shape[0]
    width = r0.shape[1]
    alpha, beta, _ = scalars(sums[...], scal1[2:3], scal1[0:1])
    a1 = scal1[0:1] + beta * alpha
    a0 = scal0[0:1] + scal1[1:2] * a1
    ys = split(a0 * e0[...] + a1 * e1[...] + alpha * e2[...])
    maps = (b_hi[rows, :nmodes], b_lo[rows, :nmodes])
    last = r2[rows, :]
    answer[...] = a0 * r0[rows, :] + a1 * r1[rows, :] + alpha * last + dot3(maps, ys)
    resid[...] = last - alpha * (image[rows, :] + beta * along[rows, :])
    for which, got in enumerate((g0, g1, g2, g3)):
        offset = starts[which] - at * ROWS

        @pl.when((offset >= 0) & (offset < ROWS))
        def _(which=which, got=got, offset=offset):
            part = pl.ds(pl.multiple_of(offset, BLOCK), BLOCK)
            mask = (0.5 * masks_of(starts, which, width)) * alpha
            resid[part, :] = resid[part, :] - mask * got[...]


def shards(compliance, loads, modes, coarse_inverse, face_block, edge_rows):
    matrix = compliance[0, 0]
    rhs = loads[0, 0]
    basis = modes[0, 0]
    inverse_rows = coarse_inverse[0]
    nmodes, order = basis.shape
    width = rhs.shape[1]
    coarse_all = inverse_rows.shape[1]
    nclus, nsub = lax.axis_size("cluster"), lax.axis_size("sub")
    full = sds(order, width)
    small = sds(nmodes, width)
    block = sds(BLOCK, width)
    tall = 5 * nmodes
    doubled = nclus == 4

    links = [("sub", pair_list(nsub, parity)) for parity in (0, 1)]
    links += [("cluster", pair_list(nclus, parity)) for parity in (0, 1)]

    def exchange(messages):
        got = [None] * 4
        for at in (1, 0, 3, 2):
            got[at] = lax.ppermute(messages[at], links[at][0], links[at][1])
        return got

    def gather(blocks, axis="sub"):
        return lax.all_to_all(blocks, axis, 0, 0, tiled=False)

    def mirror(ymom):
        first = lax.ppermute(ymom, "cluster", pair_list(nclus, 0))
        if doubled:
            sums = ymom[nmodes:] + first[nmodes:]
            both = jnp.concatenate([ymom[:nmodes], sums], 0)
            second = lax.ppermute(both, "cluster", pair_list(nclus, 1, True))
            return first, second
        mine = ymom[nmodes:]
        rest = lax.psum(mine, "cluster") - mine
        second = lax.ppermute(ymom[:nmodes], "cluster", pair_list(nclus, 1))
        return (
            jnp.concatenate([first[:nmodes], rest], 0),
            jnp.concatenate([second, jnp.zeros_like(rest)], 0),
        )

    extra = nmodes * coarse_all // width
    sizes = [BLOCK + nmodes + (extra if at < 2 else 0) for at in range(4)]
    anywhere = pl.BlockSpec(memory_space=pl.ANY)
    *messages, meta, kappa, spread = pl.pallas_call(
        start_body,
        out_shape=[sds(size, width) for size in sizes]
        + [sds(8, dtype=jnp.int32), small, sds(nsub, nmodes, width)],
        in_specs=[SM, SM, anywhere, anywhere, anywhere],
        out_specs=[VM] * 4 + [SM, VM, VM],
        scratch_shapes=[
            pltpu.VMEM((order, width), F32),
            pltpu.VMEM((nmodes, order), F32),
            pltpu.VMEM((extra, width), F32),
            pltpu.SemaphoreType.DMA((3,)),
        ],
        compiler_params=pltpu.CompilerParams(vmem_limit_bytes=16 << 20),
        name="start",
    )(face_block.swapaxes(1, 2), edge_rows.swapaxes(1, 2), rhs, basis,
      inverse_rows.reshape(extra, width))
    got = exchange(messages)
    gathered = gather(spread).reshape(nsub * nmodes, width)
    c_pair = call(
        prepare_body, [sds(order, order, dtype=BF16)] * 2, [matrix],
        flops=10_000_000)
    inverses = [inverse_rows, *got[:2]]
    if coarse_all != width:
        inverses[1:] = [each[BLOCK + nmodes :].reshape(nmodes, coarse_all) for each in got[:2]]
    own = call(first_y_body, [small], [inverse_rows, gathered])[0]
    first = lax.ppermute(own, "cluster", pair_list(nclus, 0))
    second = lax.ppermute(own, "cluster", pair_list(nclus, 1))
    mapping = sds(order, tall, dtype=BF16)
    thin = sds(nmodes, order, dtype=BF16)
    lates = sds(nmodes, 4 * BLOCK, dtype=BF16)
    others, *pairs, base = call(
        setup_body,
        [sds(2 * nmodes, width), mapping, mapping, thin, thin, lates, lates, full],
        [meta, rhs, basis, *inverses[1:], gathered, *got], smem_in=(0,),
        flops=100_000_000)
    b_pair, m_pair, l_pair = pairs[0:2], pairs[2:4], pairs[4:6]
    vee, image, *own_faces = call(
        first_apply_body, [full, full] + [block] * 4,
        [meta, base, *c_pair, *b_pair, own, others, first, second], smem_in=(0,))
    resid, eta = rhs, own

    resids, etas, scals = [resid], [eta], []
    along = None
    u_along = None
    for step in range(ITERS - 1):
        got = exchange(own_faces)
        if step == 0:
            main = call(sums_body, [sds(nmodes + PAD, width)],
                        [*m_pair, vee, image, resid, kappa, eta])[0]
            k_pair = call(maps_body, [mapping, mapping], [*c_pair, *b_pair],
                          flops=50_000_000)
        else:
            vee, resid, kappa, eta, *along, main = update(False)
            resids.append(resid)
            etas.append(eta)
        spread = call(coarse_late_body, [sds(nsub, nmodes + PAD, width)],
                      [main, *l_pair, *got])[0]
        gathered = gather(spread)
        qonce, qtwice, prod = call(
            faces_body, [full, full, full], [meta, image, *c_pair, *got],
            smem_in=(0,), flops=100_000_000)
        own, others, coarse = call(
            y_body, [sds(nmodes + PAD, width), sds(2 * nmodes, width), small],
            [*inverses, gathered])
        first, second = mirror(own)
        old = step > 0
        image_new, u_along, scal, *own_faces = call(
            make_image_body(old), [full, full, sds(PAD, width)] + [block] * 4,
            [meta, image, prod, *k_pair, own, others, first, second]
            + ([scals[-1], u_along] if old else []), smem_in=(0,))
        scals.append(scal)

        def update(last, scal=scal, vee=vee, qtwice=qtwice, own=own, others=others, first=first,
                   second=second, resid=resid, qonce=qonce, kappa=kappa, coarse=coarse, eta=eta,
                   image_new=image_new, along=along, old=old):
            out = sds(nclus * nsub, PAD, width) if last else sds(nmodes + PAD, width)
            return call(
                make_update_body(old, last),
                [full, full, small, small, full, full, small, small, out],
                [scal, vee, qtwice, *b_pair, own, others, first, second, resid, qonce, kappa,
                 coarse, eta, image_new, *m_pair] + (list(along) if old else []))

        image = image_new

    vee, resid, kappa, eta, *along, main = update(True)
    resids.append(resid)
    etas.append(eta)
    got = exchange(own_faces)
    sums = call(fold_body, [sds(PAD, width)], [gather(main, ("cluster", "sub"))])[0]
    args = [meta, sums, *scals, *b_pair, *etas, *resids, along[1], image, *got]
    answer, resid = pl.pallas_call(
        finish_body,
        grid=(order // ROWS,),
        out_shape=[full, full],
        in_specs=[SM] + [VM] * (len(args) - 1),
        out_specs=[pl.BlockSpec((ROWS, width), lambda at: (at, 0))] * 2,
        compiler_params=pltpu.CompilerParams(vmem_limit_bytes=8 << 20),
        cost_estimate=pl.CostEstimate(
            flops=1_000_000, bytes_accessed=1 << 20, transcendentals=0),
        name="finish",
    )(*args)
    return (answer[None, None], resid[None, None])


def solution(mesh):
    return jax.shard_map(
        shards,
        mesh=mesh,
        in_specs=(
            P("cluster", "sub", None, None),
            P("cluster", "sub", None, None),
            P("cluster", "sub", None, None),
            P("cluster", "sub", None),
            P(),
            P(),
        ),
        out_specs=(P("cluster", "sub", None, None), P("cluster", "sub", None, None)),
        check_vma=False,
    )
```

time: 358 us -> 129 us (0.36)
  blocking collectives: 220 us -> 33 us
  Pallas kernels: 0 us -> 30.1 us
  starting transfers between devices: 59.7 us -> 29.7 us
  matrix products: 22.8 us -> 0 us
  other arithmetic: 11.4 us -> 0.02 us
  waiting for transfers between devices: 27.5 us -> 18.9 us
  local copies, waits for them, and re-layouts: 11 us -> 14.8 us
    psum x3 -> x0, blocking collectives: 126 us -> none  [paired_dots(): lax.psum((jnp.sum(first * second, axis=0), jnp.sum(third * second, axis=0...]
    all_gather x3 -> x0, blocking collectives: 94.3 us -> none  [precondition(): lax.all_gather(coarse, 'sub', axis=0, tiled=True)]
    ppermute x24 -> x22, starting transfers between devices: 59.7 us -> 19.5 us  [the longest x16 12.3 us: exchange(): got[at] = lax.ppermute(messages[at], links[at][0], links[at][1])]
    all_to_all x0 -> x2, blocking collectives: none -> 33 us  [gather(): return lax.all_to_all(blocks, axis, 0, 0, tiled=False)]
    pallas_call x0 -> x19, Pallas kernels: none -> 30.1 us  [the longest x17 23.9 us: call(): pl.pallas_call(body, out_shape=outs, in_specs=[SM if at in smem_in else V...]
    dot_general x12 -> x0, matrix products: 22.8 us -> none  [the longest x3 13.2 us: operator(): product = jnp.dot(matrix, inner, precision=lax.Precision.HIGHEST)]
    ppermute x24 -> x22, waiting for transfers between devices: 27.5 us -> 6.52 us  [the longest x16 4.44 us: exchange(): got[at] = lax.ppermute(messages[at], links[at][0], links[at][1])]
    all_to_all x0 -> x2, waiting for transfers between devices: none -> 12.3 us  [gather(): return lax.all_to_all(blocks, axis, 0, 0, tiled=False)]
  transfers between devices with their start and end apart: 24 -> 24, of which waited for: 8 -> 7; matrix products, arithmetic and copies ran while one was open for 1% -> 0% of each run, Pallas kernels for 0% -> 9%
where the time goes in v2:
time: 129 us; the launch traced here: 128 us
  blocking collectives  33 us (26%)
  Pallas kernels  30.1 us (23%)
  starting transfers between devices  29.7 us (23%)
  waiting for transfers between devices  18.9 us (15%)
  local copies, waits for them, and re-layouts  14.8 us (11%)
    all_to_all x2, blocking collectives, gather(): return lax.all_to_all(blocks, axis, 0, 0, tiled=False)  33 us
    pallas_call x17, Pallas kernels, call(): pl.pallas_call(body, out_shape=outs, in_specs=[SM if at in smem_in else V...  23.9 us
    unnamed x54, local copies, waits for them, and re-layouts  14.8 us
    all_to_all x2, waiting for transfers between devices, gather(): return lax.all_to_all(blocks, axis, 0, 0, tiled=False)  12.3 us
    ppermute x16, starting transfers between devices, exchange(): got[at] = lax.ppermute(messages[at], links[at][0], links[at][1])  12.3 us
    all_to_all x2, starting transfers between devices, gather(): return lax.all_to_all(blocks, axis, 0, 0, tiled=False)  10.2 us
    ppermute x16, waiting for transfers between devices, exchange(): got[at] = lax.ppermute(messages[at], links[at][0], links[at][1])  4.44 us
    pallas_call x1, Pallas kernels, shards(): pl.pallas_call(finish_body, grid=(order // ROWS,), out_shape=[full, full]...  3.7 us
  transfers between devices with their start and end apart: 24, of which 7 were waited for; matrix products, arithmetic and copies ran while one was open for 0% of the time, Pallas kernels for 9%

profile of v2, /device:TPU:0, one launch (start us, length us, event | category | flops | bytes accessed | tf_op | source)
XLA Modules:
  0.0 127.6 jit_solution(606152813855617990)
XLA Ops:
  4.9 2.5 %start.1 = (f32[192,256]{1,0:T(8,128)S(1)}, f32[192,256]{1,0:T(8,128)S(1)}, f32[160,256]{1,0:T(8,128)S(1)}, f32[160,256]{1,0:T(8,128)S(1)}, s32[8]{0:T(128)S(1)}...) custom-call(s32[4,4,8]{2,1,0:T(4,128)S(1)} %bitcast.23, s32[4,2,8]{2,1,0:T(2,128)S(1)} %bitcast.24, ...), custom_call_target="tpu_custom_call" | custom-call | tf_op jit(solution)/shard_map/start/pallas_call | solution.py:403
  7.5 7.3 %all-to-all-start = ((f32[8,32,256]{2,1,0:T(8,128)}), f32[8,32,256]{2,1,0:T(8,128)S(1)}, u32[]{:S(2)}, u32[]{:S(2)}) async-start(f32[8,32,256]{2,1,0:T(8,128)} %get-tuple-element.70), calls=%async_computation | async-start | bytes 524288 | tf_op jit(solution)/shard_map/all_to_all | solution.py:383
  14.7 2.0 %collective-permute-start = (f32[192,256]{1,0:T(8,128)S(1)}, f32[192,256]{1,0:T(8,128)S(1)}, u32[]{:S(2)}, u32[]{:S(2)}) collective-permute-start(f32[192,256]{1,0:T(8,128)S(1)} %get-tuple-element.68), channel_id=1, source_target_pairs={{0,1},{1,0},{2,3},{3,2},{4,5},{5,4},{6,7},{7,6},{8,9},{9,8},{10,11... | collective-permute-start | bytes 589832 | tf_op jit(solution)/shard_map/ppermute | solution.py:379
  18.2 6.4 %all-to-all-done = f32[8,32,256]{2,1,0:T(8,128)S(1)} async-done(((f32[8,32,256]{2,1,0:T(8,128)}), f32[8,32,256]{2,1,0:T(8,128)S(1)}, u32[]{:S(2)}, u32[]{:S(2)}) %all-to-all-start) | async-done | bytes 262176 | tf_op jit(solution)/shard_map/all_to_all | solution.py:383
  26.2 2.9 %collective-permute-start.4 = (f32[32,256]{1,0:T(8,128)S(1)}, f32[32,256]{1,0:T(8,128)S(1)}, u32[]{:S(2)}, u32[]{:S(2)}) collective-permute-start(f32[32,256]{1,0:T(8,128)S(1)} %shard_map.79.own.eta.e0), channel_id=1, source_target_pairs={{0,8},{8,0},{16,24},{24,16},{1,9},{9,1},{17,25},{25,17},{2,10},{10... | collective-permute-start | bytes 98312 | tf_op jit(solution)/shard_map/ppermute | solution.py:428
  29.2 2.2 %copy-done.2 = f32[1,1,1024,1024]{3,2,1,0:T(8,128)S(1)} copy-done((f32[1,1,1024,1024]{3,2,1,0:T(8,128)S(1)}, f32[1,1,1024,1024]{3,2,1,0:T(8,128)}, u32[]{:S(2)}) %copy-start.2) | copy-done | bytes 4194328
  33.8 3.4 %shard_map.80 = (f32[1024,256]{1,0:T(8,128)S(1)}, f32[1024,256]{1,0:T(8,128)S(1)}, f32[128,256]{1,0:T(8,128)S(1)}, f32[128,256]{1,0:T(8,128)S(1)}, f32[128,256]{1,0:T(8,128)S(1)}, /*index=5*/f32[128,256]{1,0:T(8,128)S(1)}) custom-call(s32[8]{0:T(128)S(1)} %get-tuple-element.67.starts, f32[1024,256]{1,0:T(8,128)S(1)} %get-tuple-element.73.base, ...), custom_call_target="tpu_custom_call" | custom-call | flops 1000000 | bytes 1048576 | tf_op jit(solution)/shard_map/pallas_call | solution.py:25
  39.9 2.8 %collective-permute-done.6.g0 = f32[128,256]{1,0:T(8,128)S(1)} collective-permute-done((f32[128,256]{1,0:T(8,128)S(1)}, f32[128,256]{1,0:T(8,128)S(1)}, u32[]{:S(2)}, u32[]{:S(2)}) %collective-permute-start.6) | collective-permute-done | bytes 131104 | tf_op jit(solution)/shard_map/ppermute | solution.py:379
  42.9 16.5 %all_to_all.20.gathered = f32[8,40,256]{2,1,0:T(8,128)S(1)} all-to-all(f32[8,40,256]{2,1,0:T(8,128)S(1)} %shard_map.84), channel_id=1, replica_groups=mesh['cluster'=4,'sub'=8] {'sub'}, dimensions={0} | all-to-all | bytes 655360 | tf_op jit(solution)/shard_map/all_to_all | solution.py:383
  59.9 1.7 %collective-permute-start.10 = (f32[40,256]{1,0:T(8,128)S(1)}, f32[40,256]{1,0:T(8,128)S(1)}, u32[]{:S(2)}, u32[]{:S(2)}) collective-permute-start(f32[40,256]{1,0:T(8,128)S(1)} %get-tuple-element.93.own), channel_id=1, source_target_pairs={{0,8},{8,0},{16,24},{24,16},{1,9},{9,1},{17,25},{25,17},{2,10},{10... | collective-permute-start | bytes 122888 | tf_op jit(solution)/shard_map/ppermute | solution.py:386
  62.5 1.8 %shard_map.82 = (bf16[1024,160]{1,0:T(8,128)(2,1)S(1)}, bf16[1024,160]{1,0:T(8,128)(2,1)S(1)}) custom-call(bf16[1024,1024]{1,0:T(8,128)(2,1)S(1)} %get-tuple-element.74.c_hi, bf16[1024,1024]{1,0:T(8,128)(2,1)S(1)} %get-tuple-element.75.c_lo, bf16[1024,160]{1,0:T(8,128)(2,1)S(1)} %get-tuple-element.76.b_hi, bf16[1024,160]{1,0:T(8,128)(2,1)S(1)} %get-tuple-element.77.b_lo), custom_call_target="tpu_custom_call" | custom-call | flops 50000000 | bytes 1048576 | tf_op jit(solution)/shard_map/pallas_call | solution.py:25
  64.3 2.7 %shard_map.81 = (f32[1024,256]{1,0:T(8,128)S(1)}, f32[1024,256]{1,0:T(8,128)S(1)}, f32[1024,256]{1,0:T(8,128)S(1)}) custom-call(s32[8]{0:T(128)S(1)} %get-tuple-element.67.starts, f32[1024,256]{1,0:T(8,128)S(1)} %get-tuple-element.79.image, bf16[1024,1024]{1,0:T(8,128)(2,1)S(1)} %get-tuple-element.74.c_hi, bf16[1024,1024]{1,0:T(8,128)(2,1)S(1)} %get-tuple-element.75.c_lo, ...), custom_call_target="tpu_custom_call" | custom-call | flops 100000000 | bytes 1048576 | tf_op jit(solution)/shard_map/pallas_call | solution.py:25
  67.0 1.7 %shard_map.86 = (f32[1024,256]{1,0:T(8,128)S(1)}, f32[1024,256]{1,0:T(8,128)S(1)}, f32[8,256]{1,0:T(8,128)S(1)}, f32[128,256]{1,0:T(8,128)S(1)}, f32[128,256]{1,...) custom-call(s32[8]{0:T(128)S(1)} %get-tuple-element.67.starts, f32[1024,256]{1,0:T(8,128)S(1)} %get-tuple-element.79.image, ...), custom_call_target="tpu_custom_call" | custom-call | flops 1000000 | bytes 1048576 | tf_op jit(solution)/shard_map/pallas_call | solution.py:25
  71.1 1.8 %shard_map.88 = (f32[1024,256]{1,0:T(8,128)S(1)}, f32[1024,256]{1,0:T(8,128)S(1)}, f32[32,256]{1,0:T(8,128)S(1)}, f32[32,256]{1,0:T(8,128)S(1)}, f32[1024,256]{1...) custom-call(f32[8,256]{1,0:T(8,128)S(1)} %get-tuple-element.101.scal, ...), custom_call_target="tpu_custom_call" | custom-call | flops 1000000 | bytes 1048576 | tf_op jit(solution)/shard_map/pallas_call | solution.py:25
  72.9 1.6 %collective-permute-done.12.g0 = f32[128,256]{1,0:T(8,128)S(1)} collective-permute-done((f32[128,256]{1,0:T(8,128)S(1)}, f32[128,256]{1,0:T(8,128)S(1)}, u32[]{:S(2)}, u32[]{:S(2)}) %collective-permute-start.12) | collective-permute-done | bytes 131104 | tf_op jit(solution)/shard_map/ppermute | solution.py:379
  74.8 16.5 %all_to_all.21.gathered = f32[8,40,256]{2,1,0:T(8,128)S(1)} all-to-all(f32[8,40,256]{2,1,0:T(8,128)S(1)} %shard_map.89), channel_id=1, replica_groups=mesh['cluster'=4,'sub'=8] {'sub'}, dimensions={0} | all-to-all | bytes 655360 | tf_op jit(solution)/shard_map/all_to_all | solution.py:383
  91.8 1.5 %collective-permute-start.16 = (f32[40,256]{1,0:T(8,128)S(1)}, f32[40,256]{1,0:T(8,128)S(1)}, u32[]{:S(2)}, u32[]{:S(2)}) collective-permute-start(f32[40,256]{1,0:T(8,128)S(1)} %get-tuple-element.106.own), channel_id=1, source_target_pairs={{0,8},{8,0},{16,24},{24,16},{1,9},{9,1},{17,25},{25,17},{2,10},{10... | collective-permute-start | bytes 122888 | tf_op jit(solution)/shard_map/ppermute | solution.py:386
  94.6 2.7 %shard_map.87 = (f32[1024,256]{1,0:T(8,128)S(1)}, f32[1024,256]{1,0:T(8,128)S(1)}, f32[1024,256]{1,0:T(8,128)S(1)}) custom-call(s32[8]{0:T(128)S(1)} %get-tuple-element.67.starts, f32[1024,256]{1,0:T(8,128)S(1)} %get-tuple-element.95.image, bf16[1024,1024]{1,0:T(8,128)(2,1)S(1)} %get-tuple-element.74.c_hi, bf16[1024,1024]{1,0:T(8,128)(2,1)S(1)} %get-tuple-element.75.c_lo, ...), custom_call_target="tpu_custom_call" | custom-call | flops 100000000 | bytes 1048576 | tf_op jit(solution)/shard_map/pallas_call | solution.py:25
  97.6 2.6 %shard_map.91 = (f32[1024,256]{1,0:T(8,128)S(1)}, f32[1024,256]{1,0:T(8,128)}, f32[8,256]{1,0:T(8,128)S(1)}, f32[128,256]{1,0:T(8,128)S(1)}, f32[128,256]{1,0:T(...) custom-call(s32[8]{0:T(128)S(1)} %get-tuple-element.67.starts, f32[1024,256]{1,0:T(8,128)S(1)} %get-tuple-element.95.image, ...), custom_call_target="tpu_custom_call" | custom-call | flops 1000000 | bytes 1048576 | tf_op jit(solution)/shard_map/pallas_call | solution.py:25
  100.3 3.0 %shard_map.92 = (f32[1024,256]{1,0:T(8,128)}, f32[1024,256]{1,0:T(8,128)S(1)}, f32[32,256]{1,0:T(8,128)}, f32[32,256]{1,0:T(8,128)S(1)}, f32[1024,256]{1,0:T(8,1...) custom-call(f32[8,256]{1,0:T(8,128)S(1)} %get-tuple-element.109.scal.scal1, ...), custom_call_target="tpu_custom_call" | custom-call | flops 1000000 | bytes 1048576 | tf_op jit(solution)/shard_map/pallas_call | solution.py:25
  106.0 2.9 %all-to-all-start.3 = ((f32[32,8,256]{2,1,0:T(8,128)}), f32[32,8,256]{2,1,0:T(8,128)S(1)}, u32[]{:S(2)}, u32[]{:S(2)}) async-start(f32[32,8,256]{2,1,0:T(8,128)} %copy-done.16), calls=%async_computation.3 | async-start | bytes 524288 | tf_op jit(solution)/shard_map/all_to_all | solution.py:383
  108.9 1.8 %collective-permute-start.18 = (f32[128,256]{1,0:T(8,128)}, f32[128,256]{1,0:T(8,128)}, u32[]{:S(2)}, u32[]{:S(2)}) collective-permute-start(f32[128,256]{1,0:T(8,128)} %copy-done.26), channel_id=1, source_target_pairs={{0,1},{1,0},{2,3},{3,2},{4,5},{5,4},{6,7},{7,6},{8,9},{9,8},{10,11... | collective-permute-start | bytes 393224 | tf_op jit(solution)/shard_map/ppermute | solution.py:379
  113.4 6.0 %all-to-all-done.3.everyone = f32[32,8,256]{2,1,0:T(8,128)S(1)} async-done(((f32[32,8,256]{2,1,0:T(8,128)}), f32[32,8,256]{2,1,0:T(8,128)S(1)}, u32[]{:S(2)}, u32[]{:S(2)}) %all-to-all-start.3) | async-done | bytes 262176 | tf_op jit(solution)/shard_map/all_to_all | solution.py:383
  123.9 3.7 %finish.1 = (f32[1024,256]{1,0:T(8,128)}, f32[1024,256]{1,0:T(8,128)}) custom-call(s32[8]{0:T(128)S(1)} %get-tuple-element.67.starts, f32[8,256]{1,0:T(8,128)S(1)} %shard_map.93.sums, f32[8,256]{1,0:T(8,128)S(1)} %get-tuple-element.101.scal.rest_0_.scal0, f32[8,256]{1,0:T(8,128)S(1)} %get-tuple-element.109.scal.scal1, ...), custom_call_target="tpu_custom_call" | custom-call | flops 1000000 | bytes 1048576 | tf_op jit(solution)/shard_map/finish/pallas_call | solution.py:493
  (105 shorter events, 28.5 us)
Async XLA Ops:
  7.5 17.1 %all-to-all-start = ((f32[8,32,256]{2,1,0:T(8,128)}), f32[8,32,256]{2,1,0:T(8,128)S(1)}, u32[]{:S(2)}, u32[]{:S(2)}) async-start(f32[8,32,256]{2,1,0:T(8,128)} %get-tuple-element.70), calls=%async_computation | async-start | bytes 524288 | tf_op jit(solution)/shard_map/all_to_all | solution.py:383
  14.7 17.4 %collective-permute-start = (f32[192,256]{1,0:T(8,128)S(1)}, f32[192,256]{1,0:T(8,128)S(1)}, u32[]{:S(2)}, u32[]{:S(2)}) collective-permute-start(f32[192,256]{1,0:T(8,128)S(1)} %get-tuple-element.68), channel_id=1, source_target_pairs={{0,1},{1,0},{2,3},{3,2},{4,5},{5,4},{6,7},{7,6},{8,9},{9,8},{10,11... | collective-permute-start | bytes 589832 | tf_op jit(solution)/shard_map/ppermute | solution.py:379
  16.8 15.4 %collective-permute-start.1 = (f32[192,256]{1,0:T(8,128)S(1)}, f32[192,256]{1,0:T(8,128)S(1)}, u32[]{:S(2)}, u32[]{:S(2)}) collective-permute-start(f32[192,256]{1,0:T(8,128)S(1)} %get-tuple-element.69), channel_id=1, source_target_pairs={{1,2},{2,1},{3,4},{4,3},{5,6},{6,5},{9,10},{10,9},{11,12},{12,11},... | collective-permute-start | bytes 589832 | tf_op jit(solution)/shard_map/ppermute | solution.py:379
  17.4 8.8 %collective-permute-start.2 = (f32[160,256]{1,0:T(8,128)S(1)}, f32[160,256]{1,0:T(8,128)S(1)}, u32[]{:S(2)}, u32[]{:S(2)}) collective-permute-start(f32[160,256]{1,0:T(8,128)S(1)} %get-tuple-element.71), channel_id=1, source_target_pairs={{0,8},{8,0},{16,24},{24,16},{1,9},{9,1},{17,25},{25,17},{2,10},{10... | collective-permute-start | bytes 491528 | tf_op jit(solution)/shard_map/ppermute | solution.py:379
  17.5 14.6 %collective-permute-start.3 = (f32[160,256]{1,0:T(8,128)S(1)}, f32[160,256]{1,0:T(8,128)S(1)}, u32[]{:S(2)}, u32[]{:S(2)}) collective-permute-start(f32[160,256]{1,0:T(8,128)S(1)} %get-tuple-element.72), channel_id=1, source_target_pairs={{8,16},{16,8},{9,17},{17,9},{10,18},{18,10},{11,19},{19,11},{12,20... | collective-permute-start | bytes 491528 | tf_op jit(solution)/shard_map/ppermute | solution.py:379
  25.5 8.2 %collective-permute-start.5 = (f32[32,256]{1,0:T(8,128)S(1)}, f32[32,256]{1,0:T(8,128)S(1)}, u32[]{:S(2)}, u32[]{:S(2)}) collective-permute-start(f32[32,256]{1,0:T(8,128)S(1)} %shard_map.79.own.eta.e0), channel_id=1, source_target_pairs={{8,16},{16,8},{9,17},{17,9},{10,18},{18,10},{11,19},{19,11},{12,20... | collective-permute-start | bytes 98312 | tf_op jit(solution)/shard_map/ppermute | solution.py:429
  26.2 7.5 %collective-permute-start.4 = (f32[32,256]{1,0:T(8,128)S(1)}, f32[32,256]{1,0:T(8,128)S(1)}, u32[]{:S(2)}, u32[]{:S(2)}) collective-permute-start(f32[32,256]{1,0:T(8,128)S(1)} %shard_map.79.own.eta.e0), channel_id=1, source_target_pairs={{0,8},{8,0},{16,24},{24,16},{1,9},{9,1},{17,25},{25,17},{2,10},{10... | collective-permute-start | bytes 98312 | tf_op jit(solution)/shard_map/ppermute | solution.py:428
  37.2 5.5 %collective-permute-start.6 = (f32[128,256]{1,0:T(8,128)S(1)}, f32[128,256]{1,0:T(8,128)S(1)}, u32[]{:S(2)}, u32[]{:S(2)}) collective-permute-start(f32[128,256]{1,0:T(8,128)S(1)} %get-tuple-element.80), channel_id=1, source_target_pairs={{0,1},{1,0},{2,3},{3,2},{4,5},{5,4},{6,7},{7,6},{8,9},{9,8},{10,11... | collective-permute-start | bytes 393224 | tf_op jit(solution)/shard_map/ppermute | solution.py:379
  37.8 4.9 %collective-permute-start.7 = (f32[128,256]{1,0:T(8,128)S(1)}, f32[128,256]{1,0:T(8,128)S(1)}, u32[]{:S(2)}, u32[]{:S(2)}) collective-permute-start(f32[128,256]{1,0:T(8,128)S(1)} %get-tuple-element.81), channel_id=1, source_target_pairs={{1,2},{2,1},{3,4},{4,3},{5,6},{6,5},{9,10},{10,9},{11,12},{12,11},... | collective-permute-start | bytes 393224 | tf_op jit(solution)/shard_map/ppermute | solution.py:379
  38.4 4.2 %collective-permute-start.8 = (f32[128,256]{1,0:T(8,128)S(1)}, f32[128,256]{1,0:T(8,128)S(1)}, u32[]{:S(2)}, u32[]{:S(2)}) collective-permute-start(f32[128,256]{1,0:T(8,128)S(1)} %get-tuple-element.82), channel_id=1, source_target_pairs={{0,8},{8,0},{16,24},{24,16},{1,9},{9,1},{17,25},{25,17},{2,10},{10... | collective-permute-start | bytes 393224 | tf_op jit(solution)/shard_map/ppermute | solution.py:379
  38.5 4.2 %collective-permute-start.9 = (f32[128,256]{1,0:T(8,128)S(1)}, f32[128,256]{1,0:T(8,128)S(1)}, u32[]{:S(2)}, u32[]{:S(2)}) collective-permute-start(f32[128,256]{1,0:T(8,128)S(1)} %get-tuple-element.83), channel_id=1, source_target_pairs={{8,16},{16,8},{9,17},{17,9},{10,18},{18,10},{11,19},{19,11},{12,20... | collective-permute-start | bytes 393224 | tf_op jit(solution)/shard_map/ppermute | solution.py:379
  59.9 2.5 %collective-permute-start.10 = (f32[40,256]{1,0:T(8,128)S(1)}, f32[40,256]{1,0:T(8,128)S(1)}, u32[]{:S(2)}, u32[]{:S(2)}) collective-permute-start(f32[40,256]{1,0:T(8,128)S(1)} %get-tuple-element.93.own), channel_id=1, source_target_pairs={{0,8},{8,0},{16,24},{24,16},{1,9},{9,1},{17,25},{25,17},{2,10},{10... | collective-permute-start | bytes 122888 | tf_op jit(solution)/shard_map/ppermute | solution.py:386
  62.5 4.5 %collective-permute-start.11 = (f32[40,256]{1,0:T(8,128)S(1)}, f32[40,256]{1,0:T(8,128)S(1)}, u32[]{:S(2)}, u32[]{:S(2)}) collective-permute-start(f32[40,256]{1,0:T(8,128)S(1)} %pad_maximum_fusion), channel_id=1, source_target_pairs={{8,16},{16,8},{24,0},{0,24},{9,17},{17,9},{25,1},{1,25},{10,18},{1... | collective-permute-start | bytes 122888 | tf_op jit(solution)/shard_map/ppermute | solution.py:390
  68.6 5.9 %collective-permute-start.12 = (f32[128,256]{1,0:T(8,128)S(1)}, f32[128,256]{1,0:T(8,128)S(1)}, u32[]{:S(2)}, u32[]{:S(2)}) collective-permute-start(f32[128,256]{1,0:T(8,128)S(1)} %get-tuple-element.96), channel_id=1, source_target_pairs={{0,1},{1,0},{2,3},{3,2},{4,5},{5,4},{6,7},{7,6},{8,9},{9,8},{10,11... | collective-permute-start | bytes 393224 | tf_op jit(solution)/shard_map/ppermute | solution.py:379
  69.5 5.0 %collective-permute-start.13 = (f32[128,256]{1,0:T(8,128)S(1)}, f32[128,256]{1,0:T(8,128)S(1)}, u32[]{:S(2)}, u32[]{:S(2)}) collective-permute-start(f32[128,256]{1,0:T(8,128)S(1)} %get-tuple-element.97), channel_id=1, source_target_pairs={{1,2},{2,1},{3,4},{4,3},{5,6},{6,5},{9,10},{10,9},{11,12},{12,11},... | collective-permute-start | bytes 393224 | tf_op jit(solution)/shard_map/ppermute | solution.py:379
  70.2 4.3 %collective-permute-start.14 = (f32[128,256]{1,0:T(8,128)S(1)}, f32[128,256]{1,0:T(8,128)S(1)}, u32[]{:S(2)}, u32[]{:S(2)}) collective-permute-start(f32[128,256]{1,0:T(8,128)S(1)} %get-tuple-element.98), channel_id=1, source_target_pairs={{0,8},{8,0},{16,24},{24,16},{1,9},{9,1},{17,25},{25,17},{2,10},{10... | collective-permute-start | bytes 393224 | tf_op jit(solution)/shard_map/ppermute | solution.py:379
  70.4 4.1 %collective-permute-start.15 = (f32[128,256]{1,0:T(8,128)S(1)}, f32[128,256]{1,0:T(8,128)S(1)}, u32[]{:S(2)}, u32[]{:S(2)}) collective-permute-start(f32[128,256]{1,0:T(8,128)S(1)} %get-tuple-element.99), channel_id=1, source_target_pairs={{8,16},{16,8},{9,17},{17,9},{10,18},{18,10},{11,19},{19,11},{12,20... | collective-permute-start | bytes 393224 | tf_op jit(solution)/shard_map/ppermute | solution.py:379
  91.8 2.4 %collective-permute-start.16 = (f32[40,256]{1,0:T(8,128)S(1)}, f32[40,256]{1,0:T(8,128)S(1)}, u32[]{:S(2)}, u32[]{:S(2)}) collective-permute-start(f32[40,256]{1,0:T(8,128)S(1)} %get-tuple-element.106.own), channel_id=1, source_target_pairs={{0,8},{8,0},{16,24},{24,16},{1,9},{9,1},{17,25},{25,17},{2,10},{10... | collective-permute-start | bytes 122888 | tf_op jit(solution)/shard_map/ppermute | solution.py:386
  94.2 3.4 %collective-permute-start.17 = (f32[40,256]{1,0:T(8,128)S(1)}, f32[40,256]{1,0:T(8,128)S(1)}, u32[]{:S(2)}, u32[]{:S(2)}) collective-permute-start(f32[40,256]{1,0:T(8,128)S(1)} %pad_maximum_fusion.1), channel_id=1, source_target_pairs={{8,16},{16,8},{24,0},{0,24},{9,17},{17,9},{25,1},{1,25},{10,18},{1... | collective-permute-start | bytes 122888 | tf_op jit(solution)/shard_map/ppermute | solution.py:390
  106.0 13.4 %all-to-all-start.3 = ((f32[32,8,256]{2,1,0:T(8,128)}), f32[32,8,256]{2,1,0:T(8,128)S(1)}, u32[]{:S(2)}, u32[]{:S(2)}) async-start(f32[32,8,256]{2,1,0:T(8,128)} %copy-done.16), calls=%async_computation.3 | async-start | bytes 524288 | tf_op jit(solution)/shard_map/all_to_all | solution.py:383
  108.9 10.5 %collective-permute-start.18 = (f32[128,256]{1,0:T(8,128)}, f32[128,256]{1,0:T(8,128)}, u32[]{:S(2)}, u32[]{:S(2)}) collective-permute-start(f32[128,256]{1,0:T(8,128)} %copy-done.26), channel_id=1, source_target_pairs={{0,1},{1,0},{2,3},{3,2},{4,5},{5,4},{6,7},{7,6},{8,9},{9,8},{10,11... | collective-permute-start | bytes 393224 | tf_op jit(solution)/shard_map/ppermute | solution.py:379
  110.8 8.7 %collective-permute-start.19 = (f32[128,256]{1,0:T(8,128)}, f32[128,256]{1,0:T(8,128)}, u32[]{:S(2)}, u32[]{:S(2)}) collective-permute-start(f32[128,256]{1,0:T(8,128)} %copy-done.25), channel_id=1, source_target_pairs={{1,2},{2,1},{3,4},{4,3},{5,6},{6,5},{9,10},{10,9},{11,12},{12,11},... | collective-permute-start | bytes 393224 | tf_op jit(solution)/shard_map/ppermute | solution.py:379
  112.1 7.4 %collective-permute-start.20 = (f32[128,256]{1,0:T(8,128)}, f32[128,256]{1,0:T(8,128)}, u32[]{:S(2)}, u32[]{:S(2)}) collective-permute-start(f32[128,256]{1,0:T(8,128)} %copy-done.24), channel_id=1, source_target_pairs={{0,8},{8,0},{16,24},{24,16},{1,9},{9,1},{17,25},{25,17},{2,10},{10... | collective-permute-start | bytes 393224 | tf_op jit(solution)/shard_map/ppermute | solution.py:379
  112.1 7.4 %collective-permute-start.21 = (f32[128,256]{1,0:T(8,128)}, f32[128,256]{1,0:T(8,128)}, u32[]{:S(2)}, u32[]{:S(2)}) collective-permute-start(f32[128,256]{1,0:T(8,128)} %copy-done.23), channel_id=1, source_target_pairs={{8,16},{16,8},{9,17},{17,9},{10,18},{18,10},{11,19},{19,11},{12,20... | collective-permute-start | bytes 393224 | tf_op jit(solution)/shard_map/ppermute | solution.py:379
  (27 other events, 180.1 us)

commit v3 on v2

--- a/solution.py
+++ b/solution.py
@@ -20,13 +20,15 @@
     return jax.ShapeDtypeStruct(shape, dtype)
 
 
-def call(body, outs, args, smem_in=(), smem_out=(), flops=1_000_000, mib=8):
+def call(body, outs, args, smem_in=(), smem_out=(), flops=1_000_000, mib=8,
+         scratch=()):
     outs = list(outs)
     return pl.pallas_call(
         body,
         out_shape=outs,
         in_specs=[SM if at in smem_in else VM for at in range(len(args))],
         out_specs=[SM if at in smem_out else VM for at in range(len(outs))],
+        scratch_shapes=list(scratch),
         compiler_params=pltpu.CompilerParams(vmem_limit_bytes=mib << 20),
         cost_estimate=pl.CostEstimate(
             flops=flops, bytes_accessed=1 << 20, transcendentals=0),
@@ -44,6 +46,13 @@
 
 def dot3(left, right):
     return dot(left[0], right[0]) + (dot(left[0], right[1]) + dot(left[1], right[0]))
+
+
+def dot_thin(left, right):
+    high, low = left
+    rows = high.shape[0]
+    both = dot(jnp.concatenate([high, low], 0), right[0])
+    return both[:rows] + (dot(high, right[1]) + both[rows:])
 
 
 def dot6(left, right):
@@ -63,15 +72,18 @@
     return refs[0][rows, :], refs[1][rows, :]
 
 
-def start_body(face_block, edge_rows, rhs_in, basis_in, inverse_in, *outs):
-    *messages, meta, kappa, spread, rhs, basis, inverse_rows, sems = outs
+def start_body(face_in, edge_in, rhs_in, basis_in, inverse_in, *outs):
+    *messages, meta, kappa, spread, rhs, basis, inverse_rows, face_block, edge_rows, sems = outs
     copies = [
         pltpu.make_async_copy(source, target, sems.at[at])
         for at, (source, target) in enumerate(
-            ((rhs_in, rhs), (basis_in, basis), (inverse_in, inverse_rows)))
+            ((face_in, face_block), (edge_in, edge_rows), (rhs_in, rhs), (basis_in, basis),
+             (inverse_in, inverse_rows)))
     ]
     for copy in copies:
         copy.start()
+    for copy in copies[:2]:
+        copy.wait()
     nmodes = basis.shape[0]
     width = rhs.shape[1]
     clus, sub = lax.axis_index("cluster"), lax.axis_index("sub")
@@ -89,7 +101,7 @@
             meta[link] = face_block[clus, jnp.where(is_low, upper, lower), sub] * BLOCK
             meta[4 + link] = jnp.where(valid, edge_rows[place[0], kind, place[1]], 0)
             link += 1
-    for copy in copies:
+    for copy in copies[2:]:
         copy.wait()
     for at, message in enumerate(messages):
         start = pl.multiple_of(meta[at], BLOCK)
@@ -99,27 +111,27 @@
             message[BLOCK : BLOCK + nmodes, BLOCK:] = jnp.zeros((nmodes, width - BLOCK), F32)
         if at < 2:
             message[BLOCK + nmodes :] = inverse_rows[...]
-    value = dot6(basis[...], rhs[...])
+    value = dot_thin(split(basis[...]), split(rhs[...]))
     kappa[...] = value
     for at in range(spread.shape[0]):
         spread[at] = value
 
 
-def prepare_body(matrix, c_hi, c_lo):
-    @pl.loop(0, matrix.shape[0] // BLOCK)
-    def _(at):
-        rows = pl.ds(pl.multiple_of(at * BLOCK, BLOCK), BLOCK)
-        c_hi[rows, :], c_lo[rows, :] = split(matrix[rows, :])
-
-
 def masks_of(starts, at, width):
     ids = lax.broadcasted_iota(jnp.int32, (BLOCK, width), 0)
     return (ids < starts[4 + at]).astype(F32)
 
 
-def setup_body(starts, rhs, basis, i0, i1, gathered, g0, g1, g2, g3,
-               others, b_hi, b_lo, m_hi, m_lo, l_hi, l_lo, base):
-    nmodes, _ = basis.shape
+def setup_body(starts, matrix, rhs, basis, i0, i1, gathered, g0, g1, g2, g3,
+               others, b_hi, b_lo, m_hi, m_lo, l_hi, l_lo, base, c_hi, c_lo, held, sems):
+    nmodes, order = basis.shape
+    parts = [pl.ds(at * ROWS, ROWS) for at in range(order // ROWS)]
+    copies = [
+        pltpu.make_async_copy(matrix.at[part], held.at[part], sems.at[at])
+        for at, part in enumerate(parts)
+    ]
+    for copy in copies:
+        copy.start()
     skip = i0.shape[0] - nmodes
     others[:nmodes] = dot6(i0[skip:], gathered[...])
     others[nmodes:] = dot6(i1[skip:], gathered[...])
@@ -142,6 +154,13 @@
         weight = 0.5 * (ids < starts[4 + at]).astype(F32)
         cols = slice(at * BLOCK, (at + 1) * BLOCK)
         l_hi[:, cols], l_lo[:, cols] = split(weight * basis[:, pl.ds(start, BLOCK)])
+    for part, copy in zip(parts, copies):
+        copy.wait()
+
+        @pl.loop(0, ROWS // 64)
+        def _(at, part=part):
+            rows = pl.ds(pl.multiple_of(part.start + at * 64, 64), 64)
+            c_hi[rows, :], c_lo[rows, :] = split(held[rows, :])
 
 
 def maps_body(c_hi, c_lo, b_hi, b_lo, k_hi, k_lo):
@@ -208,7 +227,7 @@
 def sums_body(m_hi, m_lo, vee, image, resid, kappa, eta, out):
     nmodes = kappa.shape[0]
     out[nmodes:] = moment_rows(vee, image, resid, kappa, eta)
-    out[:nmodes] = dot3((m_hi[...], m_lo[...]), split(image[...]))
+    out[:nmodes] = dot_thin((m_hi[...], m_lo[...]), split(image[...]))
 
 
 def coarse_late_body(main, l_hi, l_lo, g0, g1, g2, g3, spread):
@@ -216,7 +235,7 @@
     total = main[:nmodes]
     for at, got in enumerate((g0, g1, g2, g3)):
         cols = slice(at * BLOCK, (at + 1) * BLOCK)
-        total = total + dot3((l_hi[:, cols], l_lo[:, cols]), split(got[...]))
+        total = total + dot_thin((l_hi[:, cols], l_lo[:, cols]), split(got[...]))
     for at in range(spread.shape[0]):
         spread[at, :nmodes] = total
         spread[at, nmodes:] = main[nmodes:]
@@ -239,10 +258,10 @@
     count, rows, _ = gathered.shape
     nmodes = rows - PAD
     blocks = jnp.concatenate([gathered[at, :nmodes] for at in range(count)], 0)
-    own[:nmodes] = dot6(inverse_rows[...], blocks)
     skip = i0.shape[0] - nmodes
-    others[:nmodes] = dot6(i0[skip:], blocks)
-    others[nmodes:] = dot6(i1[skip:], blocks)
+    value = dot6(jnp.concatenate([inverse_rows[...], i0[skip:], i1[skip:]], 0), blocks)
+    own[:nmodes] = value[:nmodes]
+    others[...] = value[nmodes:]
     total = gathered[0, nmodes:]
     for at in range(1, count):
         total = total + gathered[at, nmodes:]
@@ -271,7 +290,7 @@
         nmodes = others.shape[0] // 2
         sums = own[nmodes:] + first[nmodes:] + second[nmodes:]
         if has_old:
-            scal_old, along_old, image_new, along, scal = rest
+            scal_old, along_old, image_new, scal = rest
             alpha, beta, rz = scalars(sums, scal_old[2:3], scal_old[0:1])
         else:
             image_new, along, scal = rest
@@ -285,7 +304,8 @@
             value = prod[rows, :] + dot3(half((k_hi, k_lo), rows), ys)
             if has_old:
                 value = value + beta * along_old[rows, :]
-            along[rows, :] = value
+            if not has_old:
+                along[rows, :] = value
             image_new[rows, :] = image[rows, :] - alpha * value
 
         copy_faces(starts, image_new, (f0, f1, f2, f3))
@@ -299,7 +319,11 @@
         if has_old:
             t_old, q_old, k_old, y_old = rest[:4]
             rest = rest[4:]
-        vee_new, resid_new, kappa_new, eta_new, t_along, q_along, k_along, y_along, out = rest
+        if last:
+            resid_new, eta_new, q_along, out, vee_new, kappa_new = rest
+            t_along = k_along = y_along = None
+        else:
+            vee_new, resid_new, kappa_new, eta_new, t_along, q_along, k_along, y_along, out = rest
         alpha, beta = scal[0:1], scal[1:2]
         nmodes = kappa.shape[0]
         ys = split(stacked(own, others, first, second))
@@ -313,19 +337,23 @@
         def _(at):
             rows = pl.ds(pl.multiple_of(at * ROWS, ROWS), ROWS)
             value = qtwice[rows, :] + dot3(half((b_hi, b_lo), rows), ys)
-            t_along[rows, :], vee_new[rows, :] = move(
+            value, vee_new[rows, :] = move(
                 vee[rows, :], value, t_old[rows, :] if has_old else None)
+            if not last:
+                t_along[rows, :] = value
             q_along[rows, :], resid_new[rows, :] = move(
                 resid[rows, :], qonce[rows, :], q_old[rows, :] if has_old else None)
 
-        k_along[...], kappa_new[...] = move(kappa[...], coarse[...], k_old[...] if has_old else None)
-        y_along[...], eta_new[...] = move(eta[...], own[:nmodes], y_old[...] if has_old else None)
+        k_value, kappa_new[...] = move(kappa[...], coarse[...], k_old[...] if has_old else None)
+        y_value, eta_new[...] = move(eta[...], own[:nmodes], y_old[...] if has_old else None)
+        if not last:
+            k_along[...], y_along[...] = k_value, y_value
         moments = moment_rows(vee_new, image, resid_new, kappa_new, eta_new)
         if last:
             for at in range(out.shape[0]):
-                out[at] = moments
+                out[at] = moments[: out.shape[1]]
         else:
-            out[:nmodes] = dot3((m_hi[...], m_lo[...]), split(image[...]))
+            out[:nmodes] = dot_thin((m_hi[...], m_lo[...]), split(image[...]))
             out[nmodes:] = moments
 
     return body
@@ -399,28 +427,28 @@
 
     extra = nmodes * coarse_all // width
     sizes = [BLOCK + nmodes + (extra if at < 2 else 0) for at in range(4)]
-    anywhere = pl.BlockSpec(memory_space=pl.ANY)
-    *messages, meta, kappa, spread = pl.pallas_call(
+    far = pl.BlockSpec(memory_space=pltpu.HBM)
+    *messages, meta, kappa, spread, rhs, basis, flat = pl.pallas_call(
         start_body,
         out_shape=[sds(size, width) for size in sizes]
-        + [sds(8, dtype=jnp.int32), small, sds(nsub, nmodes, width)],
-        in_specs=[SM, SM, anywhere, anywhere, anywhere],
-        out_specs=[VM] * 4 + [SM, VM, VM],
+        + [sds(8, dtype=jnp.int32), small, sds(nsub, nmodes, width), full,
+           sds(nmodes, order), sds(extra, width)],
+        in_specs=[far] * 5,
+        out_specs=[VM] * 4 + [SM] + [VM] * 5,
         scratch_shapes=[
-            pltpu.VMEM((order, width), F32),
-            pltpu.VMEM((nmodes, order), F32),
-            pltpu.VMEM((extra, width), F32),
-            pltpu.SemaphoreType.DMA((3,)),
+            pltpu.SMEM((nclus, 4, nsub), jnp.int32),
+            pltpu.SMEM((nclus, 2, nsub), jnp.int32),
+            pltpu.SemaphoreType.DMA((5,)),
         ],
         compiler_params=pltpu.CompilerParams(vmem_limit_bytes=16 << 20),
         name="start",
-    )(face_block.swapaxes(1, 2), edge_rows.swapaxes(1, 2), rhs, basis,
-      inverse_rows.reshape(extra, width))
+    )(*(pltpu.with_memory_space_constraint(each, pltpu.HBM) for each in (
+        face_block.swapaxes(1, 2), edge_rows.swapaxes(1, 2), rhs, basis,
+        inverse_rows.reshape(extra, width))))
+    if coarse_all == width:
+        inverse_rows = flat
     got = exchange(messages)
     gathered = gather(spread).reshape(nsub * nmodes, width)
-    c_pair = call(
-        prepare_body, [sds(order, order, dtype=BF16)] * 2, [matrix],
-        flops=10_000_000)
     inverses = [inverse_rows, *got[:2]]
     if coarse_all != width:
         inverses[1:] = [each[BLOCK + nmodes :].reshape(nmodes, coarse_all) for each in got[:2]]
@@ -430,11 +458,21 @@
     mapping = sds(order, tall, dtype=BF16)
     thin = sds(nmodes, order, dtype=BF16)
     lates = sds(nmodes, 4 * BLOCK, dtype=BF16)
-    others, *pairs, base = call(
+    args = [meta, pltpu.with_memory_space_constraint(matrix, pltpu.HBM), rhs, basis,
+            *inverses[1:], gathered, *got]
+    others, *pairs, base, c_hi, c_lo = pl.pallas_call(
         setup_body,
-        [sds(2 * nmodes, width), mapping, mapping, thin, thin, lates, lates, full],
-        [meta, rhs, basis, *inverses[1:], gathered, *got], smem_in=(0,),
-        flops=100_000_000)
+        out_shape=[sds(2 * nmodes, width), mapping, mapping, thin, thin, lates, lates, full]
+        + [sds(order, order, dtype=BF16)] * 2,
+        in_specs=[SM, far] + [VM] * (len(args) - 2),
+        out_specs=[VM] * 10,
+        scratch_shapes=[pltpu.VMEM((order, order), F32), pltpu.SemaphoreType.DMA((order // ROWS,))],
+        compiler_params=pltpu.CompilerParams(vmem_limit_bytes=16 << 20),
+        cost_estimate=pl.CostEstimate(
+            flops=100_000_000, bytes_accessed=1 << 22, transcendentals=0),
+        name="setup",
+    )(*args)
+    c_pair = (c_hi, c_lo)
     b_pair, m_pair, l_pair = pairs[0:2], pairs[2:4], pairs[4:6]
     vee, image, *own_faces = call(
         first_apply_body, [full, full] + [block] * 4,
@@ -466,30 +504,38 @@
             [*inverses, gathered])
         first, second = mirror(own)
         old = step > 0
-        image_new, u_along, scal, *own_faces = call(
-            make_image_body(old), [full, full, sds(PAD, width)] + [block] * 4,
+        image_new, *u_next, scal, f0, f1, f2, f3 = call(
+            make_image_body(old),
+            [full] * (1 if old else 2) + [sds(PAD, width)] + [block] * 4,
             [meta, image, prod, *k_pair, own, others, first, second]
-            + ([scals[-1], u_along] if old else []), smem_in=(0,))
+            + ([scals[-1], *u_along] if old else []), smem_in=(0,))
+        own_faces, u_along = (f0, f1, f2, f3), u_next
         scals.append(scal)
 
         def update(last, scal=scal, vee=vee, qtwice=qtwice, own=own, others=others, first=first,
                    second=second, resid=resid, qonce=qonce, kappa=kappa, coarse=coarse, eta=eta,
                    image_new=image_new, along=along, old=old):
-            out = sds(nclus * nsub, PAD, width) if last else sds(nmodes + PAD, width)
+            outs = (
+                [full, small, full, sds(nclus * nsub, 2, width)]
+                if last
+                else [full, full, small, small, full, full, small, small,
+                      sds(nmodes + PAD, width)]
+            )
             return call(
-                make_update_body(old, last),
-                [full, full, small, small, full, full, small, small, out],
+                make_update_body(old, last), outs,
                 [scal, vee, qtwice, *b_pair, own, others, first, second, resid, qonce, kappa,
-                 coarse, eta, image_new, *m_pair] + (list(along) if old else []))
+                 coarse, eta, image_new, *m_pair] + (list(along) if old else []),
+                scratch=[pltpu.VMEM((order, width), F32), pltpu.VMEM((nmodes, width), F32)]
+                if last else ())
 
         image = image_new
 
-    vee, resid, kappa, eta, *along, main = update(True)
+    resid, eta, q_along, main = update(True)
     resids.append(resid)
     etas.append(eta)
     got = exchange(own_faces)
-    sums = call(fold_body, [sds(PAD, width)], [gather(main, ("cluster", "sub"))])[0]
-    args = [meta, sums, *scals, *b_pair, *etas, *resids, along[1], image, *got]
+    sums = call(fold_body, [sds(2, width)], [gather(main, ("cluster", "sub"))])[0]
+    args = [meta, sums, *scals, *b_pair, *etas, *resids, q_along, image, *got]
     answer, resid = pl.pallas_call(
         finish_body,
         grid=(order // ROWS,),

time: 129 us -> 117 us (0.907)
  blocking collectives: 33 us -> 49.1 us
  local copies, waits for them, and re-layouts: 14.8 us -> 0.01 us
  waiting for transfers between devices: 18.9 us -> 13.3 us
  starting transfers between devices: 29.7 us -> 24.8 us
  Pallas kernels: 30.1 us -> 28 us
    all_to_all x2 -> x3, blocking collectives: 33 us -> 49.1 us  [gather(): return lax.all_to_all(blocks, axis, 0, 0, tiled=False)]
    unnamed x54 -> x0, local copies, waits for them, and re-layouts: 14.8 us -> none
    all_to_all x2 -> x1, waiting for transfers between devices: 12.3 us -> 6.36 us  [gather(): return lax.all_to_all(blocks, axis, 0, 0, tiled=False)]
    pallas_call x17 -> x15, Pallas kernels: 23.9 us -> 19.1 us  [call(): pl.pallas_call(body, out_shape=outs, in_specs=[SM if at in smem_in else V...]
    pallas_call x0 -> x1, Pallas kernels: none -> 3.38 us  [shards(): pl.pallas_call(setup_body, out_shape=[sds(2 * nmodes, width), mapping, ma...]
    all_to_all x2 -> x1, starting transfers between devices: 10.2 us -> 7.29 us  [gather(): return lax.all_to_all(blocks, axis, 0, 0, tiled=False)]
    ppermute x16, starting transfers between devices: 12.3 us -> 10.3 us  [exchange(): got[at] = lax.ppermute(messages[at], links[at][0], links[at][1])]
  transfers between devices with their start and end apart: 24 -> 23, of which waited for: 7 -> 6; matrix products, arithmetic and copies ran while one was open for 0% -> 0% of each run, Pallas kernels for 9% -> 13%
where the time goes in v3:
time: 117 us; the launch traced here: 116 us
  blocking collectives  49.1 us (42%)
  Pallas kernels  28 us (24%)
  starting transfers between devices  24.8 us (21%)
  waiting for transfers between devices  13.3 us (11%)
    all_to_all x3, blocking collectives, gather(): return lax.all_to_all(blocks, axis, 0, 0, tiled=False)  49.1 us
    pallas_call x15, Pallas kernels, call(): pl.pallas_call(body, out_shape=outs, in_specs=[SM if at in smem_in else V...  19.1 us
    ppermute x16, starting transfers between devices, exchange(): got[at] = lax.ppermute(messages[at], links[at][0], links[at][1])  10.3 us
    all_to_all x1, starting transfers between devices, gather(): return lax.all_to_all(blocks, axis, 0, 0, tiled=False)  7.29 us
    all_to_all x1, waiting for transfers between devices, gather(): return lax.all_to_all(blocks, axis, 0, 0, tiled=False)  6.36 us
    ppermute x16, waiting for transfers between devices, exchange(): got[at] = lax.ppermute(messages[at], links[at][0], links[at][1])  4.59 us
    pallas_call x1, Pallas kernels, shards(): pl.pallas_call(setup_body, out_shape=[sds(2 * nmodes, width), mapping, ma...  3.38 us
    pallas_call x1, Pallas kernels, shards(): pl.pallas_call(finish_body, grid=(order // ROWS,), out_shape=[full, full]...  3.2 us
  transfers between devices with their start and end apart: 23, of which 6 were waited for; matrix products, arithmetic and copies ran while one was open for 0% of the time, Pallas kernels for 13%

profile of v3, /device:TPU:0, one launch (start us, length us, event | category | flops | bytes accessed | tf_op | source)
XLA Modules:
  0.0 116.2 jit_solution(875193591373218045)
XLA Ops:
  0.6 2.3 %start.1 = (f32[192,256]{1,0:T(8,128)S(1)}, f32[192,256]{1,0:T(8,128)S(1)}, f32[160,256]{1,0:T(8,128)S(1)}, f32[160,256]{1,0:T(8,128)S(1)}, s32[8]{0:T(128)S(1)}...) custom-call(s32[4,4,8]{2,1,0:T(4,128)} %bitcast.15, ...), custom_call_target="tpu_custom_call" | custom-call | tf_op jit(solution)/shard_map/start/pallas_call | solution.py:431
  3.0 7.3 %all-to-all-start = ((f32[8,32,256]{2,1,0:T(8,128)}), f32[8,32,256]{2,1,0:T(8,128)S(1)}, u32[]{:S(2)}, u32[]{:S(2)}) async-start(f32[8,32,256]{2,1,0:T(8,128)} %get-tuple-element.75), calls=%async_computation | async-start | bytes 524288 | tf_op jit(solution)/shard_map/all_to_all | solution.py:411
  10.3 2.0 %collective-permute-start = (f32[192,256]{1,0:T(8,128)S(1)}, f32[192,256]{1,0:T(8,128)S(1)}, u32[]{:S(2)}, u32[]{:S(2)}) collective-permute-start(f32[192,256]{1,0:T(8,128)S(1)} %get-tuple-element.73), channel_id=1, source_target_pairs={{0,1},{1,0},{2,3},{3,2},{4,5},{5,4},{6,7},{7,6},{8,9},{9,8},{10,11... | collective-permute-start | bytes 589832 | tf_op jit(solution)/shard_map/ppermute | solution.py:407
  13.7 6.4 %all-to-all-done = f32[8,32,256]{2,1,0:T(8,128)S(1)} async-done(((f32[8,32,256]{2,1,0:T(8,128)}), f32[8,32,256]{2,1,0:T(8,128)S(1)}, u32[]{:S(2)}, u32[]{:S(2)}) %all-to-all-start) | async-done | bytes 262176 | tf_op jit(solution)/shard_map/all_to_all | solution.py:411
  21.0 2.9 %collective-permute-start.4 = (f32[32,256]{1,0:T(8,128)S(1)}, f32[32,256]{1,0:T(8,128)S(1)}, u32[]{:S(2)}, u32[]{:S(2)}) collective-permute-start(f32[32,256]{1,0:T(8,128)S(1)} %shard_map.77.own.eta.e0), channel_id=1, source_target_pairs={{0,8},{8,0},{16,24},{24,16},{1,9},{9,1},{17,25},{25,17},{2,10},{10... | collective-permute-start | bytes 98312 | tf_op jit(solution)/shard_map/ppermute | solution.py:456
  23.9 3.4 %setup.1 = (f32[64,256]{1,0:T(8,128)S(1)}, bf16[1024,160]{1,0:T(8,128)(2,1)S(1)}, bf16[1024,160]{1,0:T(8,128)(2,1)S(1)}, bf16[32,1024]{1,0:T(8,128)(2,1)S(1)}, b...) custom-call(s32[8]{0:T(128)S(1)} %get-tuple-element.70.starts, ...), custom_call_target="tpu_custom_call" | custom-call | flops 100000000 | bytes 4194304 | tf_op jit(solution)/shard_map/setup/pallas_call | solution.py:463
  27.3 3.4 %shard_map.78 = (f32[1024,256]{1,0:T(8,128)S(1)}, f32[1024,256]{1,0:T(8,128)S(1)}, f32[128,256]{1,0:T(8,128)S(1)}, f32[128,256]{1,0:T(8,128)S(1)}, f32[128,256]{1,0:T(8,128)S(1)}, /*index=5*/f32[128,256]{1,0:T(8,128)S(1)}) custom-call(s32[8]{0:T(128)S(1)} %get-tuple-element.70.starts, f32[1024,256]{1,0:T(8,128)S(1)} %get-tuple-element.78.base, ...), custom_call_target="tpu_custom_call" | custom-call | flops 1000000 | bytes 1048576 | tf_op jit(solution)/shard_map/pallas_call | solution.py:26
  30.8 1.0 collective-permute-start.6
  33.8 2.5 %collective-permute-done.6.g0 = f32[128,256]{1,0:T(8,128)S(1)} collective-permute-done((f32[128,256]{1,0:T(8,128)S(1)}, f32[128,256]{1,0:T(8,128)S(1)}, u32[]{:S(2)}, u32[]{:S(2)}) %collective-permute-start.6) | collective-permute-done | bytes 131104 | tf_op jit(solution)/shard_map/ppermute | solution.py:407
  36.5 17.5 %all_to_all.20.gathered = f32[8,40,256]{2,1,0:T(8,128)S(1)} all-to-all(f32[8,40,256]{2,1,0:T(8,128)S(1)} %shard_map.82), channel_id=1, replica_groups=mesh['cluster'=4,'sub'=8] {'sub'}, dimensions={0} | all-to-all | bytes 655360 | tf_op jit(solution)/shard_map/all_to_all | solution.py:411
  54.2 1.9 %collective-permute-start.10 = (f32[40,256]{1,0:T(8,128)S(1)}, f32[40,256]{1,0:T(8,128)S(1)}, u32[]{:S(2)}, u32[]{:S(2)}) collective-permute-start(f32[40,256]{1,0:T(8,128)S(1)} %get-tuple-element.99.own), channel_id=1, source_target_pairs={{0,8},{8,0},{16,24},{24,16},{1,9},{9,1},{17,25},{25,17},{2,10},{10... | collective-permute-start | bytes 122888 | tf_op jit(solution)/shard_map/ppermute | solution.py:414
  57.5 1.8 %shard_map.80 = (bf16[1024,160]{1,0:T(8,128)(2,1)S(1)}, bf16[1024,160]{1,0:T(8,128)(2,1)S(1)}) custom-call(bf16[1024,1024]{1,0:T(8,128)(2,1)S(1)} %get-tuple-element.79.c_hi, bf16[1024,1024]{1,0:T(8,128)(2,1)S(1)} %get-tuple-element.80.c_lo, bf16[1024,160]{1,0:T(8,128)(2,1)S(1)} %get-tuple-element.81.b_hi, bf16[1024,160]{1,0:T(8,128)(2,1)S(1)} %get-tuple-element.82.b_lo), custom_call_target="tpu_custom_call" | custom-call | flops 50000000 | bytes 1048576 | tf_op jit(solution)/shard_map/pallas_call | solution.py:26
  59.3 2.7 %shard_map.79 = (f32[1024,256]{1,0:T(8,128)S(1)}, f32[1024,256]{1,0:T(8,128)S(1)}, f32[1024,256]{1,0:T(8,128)S(1)}) custom-call(s32[8]{0:T(128)S(1)} %get-tuple-element.70.starts, f32[1024,256]{1,0:T(8,128)S(1)} %get-tuple-element.85.image, bf16[1024,1024]{1,0:T(8,128)(2,1)S(1)} %get-tuple-element.79.c_hi, bf16[1024,1024]{1,0:T(8,128)(2,1)S(1)} %get-tuple-element.80.c_lo, ...), custom_call_target="tpu_custom_call" | custom-call | flops 100000000 | bytes 1048576 | tf_op jit(solution)/shard_map/pallas_call | solution.py:26
  62.0 1.6 %shard_map.84 = (f32[1024,256]{1,0:T(8,128)S(1)}, f32[1024,256]{1,0:T(8,128)S(1)}, f32[8,256]{1,0:T(8,128)S(1)}, f32[128,256]{1,0:T(8,128)S(1)}, f32[128,256]{1,...) custom-call(s32[8]{0:T(128)S(1)} %get-tuple-element.70.starts, f32[1024,256]{1,0:T(8,128)S(1)} %get-tuple-element.85.image, ...), custom_call_target="tpu_custom_call" | custom-call | flops 1000000 | bytes 1048576 | tf_op jit(solution)/shard_map/pallas_call | solution.py:26
  65.6 1.8 %shard_map.86 = (f32[1024,256]{1,0:T(8,128)S(1)}, f32[1024,256]{1,0:T(8,128)S(1)}, f32[32,256]{1,0:T(8,128)S(1)}, f32[32,256]{1,0:T(8,128)S(1)}, f32[1024,256]{1...) custom-call(f32[8,256]{1,0:T(8,128)S(1)} %get-tuple-element.107.scal, ...), custom_call_target="tpu_custom_call" | custom-call | flops 1000000 | bytes 1048576 | tf_op jit(solution)/shard_map/pallas_call | solution.py:26
  67.4 2.1 %collective-permute-done.12.g0 = f32[128,256]{1,0:T(8,128)S(1)} collective-permute-done((f32[128,256]{1,0:T(8,128)S(1)}, f32[128,256]{1,0:T(8,128)S(1)}, u32[]{:S(2)}, u32[]{:S(2)}) %collective-permute-start.12) | collective-permute-done | bytes 131104 | tf_op jit(solution)/shard_map/ppermute | solution.py:407
  69.7 16.7 %all_to_all.21.gathered = f32[8,40,256]{2,1,0:T(8,128)S(1)} all-to-all(f32[8,40,256]{2,1,0:T(8,128)S(1)} %shard_map.87), channel_id=1, replica_groups=mesh['cluster'=4,'sub'=8] {'sub'}, dimensions={0} | all-to-all | bytes 655360 | tf_op jit(solution)/shard_map/all_to_all | solution.py:411
  86.7 1.2 %collective-permute-start.16 = (f32[40,256]{1,0:T(8,128)S(1)}, f32[40,256]{1,0:T(8,128)S(1)}, u32[]{:S(2)}, u32[]{:S(2)}) collective-permute-start(f32[40,256]{1,0:T(8,128)S(1)} %get-tuple-element.112.own), channel_id=1, source_target_pairs={{0,8},{8,0},{16,24},{24,16},{1,9},{9,1},{17,25},{25,17},{2,10},{10... | collective-permute-start | bytes 122888 | tf_op jit(solution)/shard_map/ppermute | solution.py:414
  88.9 2.7 %shard_map.85 = (f32[1024,256]{1,0:T(8,128)S(1)}, f32[1024,256]{1,0:T(8,128)S(1)}, f32[1024,256]{1,0:T(8,128)S(1)}) custom-call(s32[8]{0:T(128)S(1)} %get-tuple-element.70.starts, f32[1024,256]{1,0:T(8,128)S(1)} %get-tuple-element.101.image, bf16[1024,1024]{1,0:T(8,128)(2,1)S(1)} %get-tuple-element.79.c_hi, bf16[1024,1024]{1,0:T(8,128)(2,1)S(1)} %get-tuple-element.80.c_lo, ...), custom_call_target="tpu_custom_call" | custom-call | flops 100000000 | bytes 1048576 | tf_op jit(solution)/shard_map/pallas_call | solution.py:26
  92.2 1.7 %shard_map.89 = (f32[1024,256]{1,0:T(8,128)S(1)}, f32[8,256]{1,0:T(8,128)S(1)}, f32[128,256]{1,0:T(8,128)S(1)}, f32[128,256]{1,0:T(8,128)S(1)}, f32[128,256]{1,0:T(8,128)S(1)}, /*index=5*/f32[128,256]{1,0:T(8,128)S(1)}) custom-call(s32[8]{0:T(128)S(1)} %get-tuple-element.70.starts, f32[1024,256]{1,0:T(8,128)S(1)} %get-tuple-element.101.image, ...), custom_call_target="tpu_custom_call" | custom-call | flops 1000000 | bytes 1048576 | tf_op jit(solution)/shard_map/pallas_call | solution.py:26
  93.9 0.9 collective-permute-start.18
  96.3 1.7 %shard_map.90 = (f32[1024,256]{1,0:T(8,128)S(1)}, f32[32,256]{1,0:T(8,128)S(1)}, f32[1024,256]{1,0:T(8,128)S(1)}, f32[32,2,256]{2,1,0:T(2,128)S(1)}) custom-call(f32[8,256]{1,0:T(8,128)S(1)} %get-tuple-element.115.scal.scal1, f32[1024,256]{1,0:T(8,128)S(1)} %get-tuple-element.116.vee, f32[1024,256]{1,0:T(8,128)S(1)} %get-tuple-element.117.qtwice, ...), custom_call_target="tpu_custom_call" | custom-call | flops 1000000 | bytes 1048576 | tf_op jit(solution)/shard_map/pallas_call | solution.py:26
  97.9 15.0 %all_to_all.22.everyone = f32[32,2,256]{2,1,0:T(2,128)S(1)} all-to-all(f32[32,2,256]{2,1,0:T(2,128)S(1)} %get-tuple-element.128), channel_id=1, replica_groups=mesh['cluster'=4,'sub'=8] {'cluster','sub'}, dimensions={0} | all-to-all | bytes 131072 | tf_op jit(solution)/shard_map/all_to_all | solution.py:411
  113.0 3.2 %finish.1 = (f32[1024,256]{1,0:T(8,128)}, f32[1024,256]{1,0:T(8,128)}) custom-call(s32[8]{0:T(128)S(1)} %get-tuple-element.70.starts, f32[2,256]{1,0:T(2,128)S(1)} %shard_map.91.sums, f32[8,256]{1,0:T(8,128)S(1)} %get-tuple-element.107.scal.rest_0_.scal0, f32[8,256]{1,0:T(8,128)S(1)} %get-tuple-element.115.scal.scal1, ...), custom_call_target="tpu_custom_call" | custom-call | flops 1000000 | bytes 1048576 | tf_op jit(solution)/shard_map/finish/pallas_call | solution.py:539
  (49 shorter events, 11.8 us)
Async XLA Ops:
  3.0 17.1 %all-to-all-start = ((f32[8,32,256]{2,1,0:T(8,128)}), f32[8,32,256]{2,1,0:T(8,128)S(1)}, u32[]{:S(2)}, u32[]{:S(2)}) async-start(f32[8,32,256]{2,1,0:T(8,128)} %get-tuple-element.75), calls=%async_computation | async-start | bytes 524288 | tf_op jit(solution)/shard_map/all_to_all | solution.py:411
  10.3 13.7 %collective-permute-start = (f32[192,256]{1,0:T(8,128)S(1)}, f32[192,256]{1,0:T(8,128)S(1)}, u32[]{:S(2)}, u32[]{:S(2)}) collective-permute-start(f32[192,256]{1,0:T(8,128)S(1)} %get-tuple-element.73), channel_id=1, source_target_pairs={{0,1},{1,0},{2,3},{3,2},{4,5},{5,4},{6,7},{7,6},{8,9},{9,8},{10,11... | collective-permute-start | bytes 589832 | tf_op jit(solution)/shard_map/ppermute | solution.py:407
  12.3 11.6 %collective-permute-start.1 = (f32[192,256]{1,0:T(8,128)S(1)}, f32[192,256]{1,0:T(8,128)S(1)}, u32[]{:S(2)}, u32[]{:S(2)}) collective-permute-start(f32[192,256]{1,0:T(8,128)S(1)} %get-tuple-element.74), channel_id=1, source_target_pairs={{1,2},{2,1},{3,4},{4,3},{5,6},{6,5},{9,10},{10,9},{11,12},{12,11},... | collective-permute-start | bytes 589832 | tf_op jit(solution)/shard_map/ppermute | solution.py:407
  12.9 8.0 %collective-permute-start.2 = (f32[160,256]{1,0:T(8,128)S(1)}, f32[160,256]{1,0:T(8,128)S(1)}, u32[]{:S(2)}, u32[]{:S(2)}) collective-permute-start(f32[160,256]{1,0:T(8,128)S(1)} %get-tuple-element.76), channel_id=1, source_target_pairs={{0,8},{8,0},{16,24},{24,16},{1,9},{9,1},{17,25},{25,17},{2,10},{10... | collective-permute-start | bytes 491528 | tf_op jit(solution)/shard_map/ppermute | solution.py:407
  13.0 10.9 %collective-permute-start.3 = (f32[160,256]{1,0:T(8,128)S(1)}, f32[160,256]{1,0:T(8,128)S(1)}, u32[]{:S(2)}, u32[]{:S(2)}) collective-permute-start(f32[160,256]{1,0:T(8,128)S(1)} %get-tuple-element.77), channel_id=1, source_target_pairs={{8,16},{16,8},{9,17},{17,9},{10,18},{18,10},{11,19},{19,11},{12,20... | collective-permute-start | bytes 491528 | tf_op jit(solution)/shard_map/ppermute | solution.py:407
  20.3 7.0 %collective-permute-start.5 = (f32[32,256]{1,0:T(8,128)S(1)}, f32[32,256]{1,0:T(8,128)S(1)}, u32[]{:S(2)}, u32[]{:S(2)}) collective-permute-start(f32[32,256]{1,0:T(8,128)S(1)} %shard_map.77.own.eta.e0), channel_id=1, source_target_pairs={{8,16},{16,8},{9,17},{17,9},{10,18},{18,10},{11,19},{19,11},{12,20... | collective-permute-start | bytes 98312 | tf_op jit(solution)/shard_map/ppermute | solution.py:457
  21.0 6.4 %collective-permute-start.4 = (f32[32,256]{1,0:T(8,128)S(1)}, f32[32,256]{1,0:T(8,128)S(1)}, u32[]{:S(2)}, u32[]{:S(2)}) collective-permute-start(f32[32,256]{1,0:T(8,128)S(1)} %shard_map.77.own.eta.e0), channel_id=1, source_target_pairs={{0,8},{8,0},{16,24},{24,16},{1,9},{9,1},{17,25},{25,17},{2,10},{10... | collective-permute-start | bytes 98312 | tf_op jit(solution)/shard_map/ppermute | solution.py:456
  30.8 5.5 %collective-permute-start.6 = (f32[128,256]{1,0:T(8,128)S(1)}, f32[128,256]{1,0:T(8,128)S(1)}, u32[]{:S(2)}, u32[]{:S(2)}) collective-permute-start(f32[128,256]{1,0:T(8,128)S(1)} %get-tuple-element.86), channel_id=1, source_target_pairs={{0,1},{1,0},{2,3},{3,2},{4,5},{5,4},{6,7},{7,6},{8,9},{9,8},{10,11... | collective-permute-start | bytes 393224 | tf_op jit(solution)/shard_map/ppermute | solution.py:407
  31.8 4.5 %collective-permute-start.7 = (f32[128,256]{1,0:T(8,128)S(1)}, f32[128,256]{1,0:T(8,128)S(1)}, u32[]{:S(2)}, u32[]{:S(2)}) collective-permute-start(f32[128,256]{1,0:T(8,128)S(1)} %get-tuple-element.87), channel_id=1, source_target_pairs={{1,2},{2,1},{3,4},{4,3},{5,6},{6,5},{9,10},{10,9},{11,12},{12,11},... | collective-permute-start | bytes 393224 | tf_op jit(solution)/shard_map/ppermute | solution.py:407
  32.5 3.8 %collective-permute-start.8 = (f32[128,256]{1,0:T(8,128)S(1)}, f32[128,256]{1,0:T(8,128)S(1)}, u32[]{:S(2)}, u32[]{:S(2)}) collective-permute-start(f32[128,256]{1,0:T(8,128)S(1)} %get-tuple-element.88), channel_id=1, source_target_pairs={{0,8},{8,0},{16,24},{24,16},{1,9},{9,1},{17,25},{25,17},{2,10},{10... | collective-permute-start | bytes 393224 | tf_op jit(solution)/shard_map/ppermute | solution.py:407
  32.6 3.7 %collective-permute-start.9 = (f32[128,256]{1,0:T(8,128)S(1)}, f32[128,256]{1,0:T(8,128)S(1)}, u32[]{:S(2)}, u32[]{:S(2)}) collective-permute-start(f32[128,256]{1,0:T(8,128)S(1)} %get-tuple-element.89), channel_id=1, source_target_pairs={{8,16},{16,8},{9,17},{17,9},{10,18},{18,10},{11,19},{19,11},{12,20... | collective-permute-start | bytes 393224 | tf_op jit(solution)/shard_map/ppermute | solution.py:407
  54.2 2.7 %collective-permute-start.10 = (f32[40,256]{1,0:T(8,128)S(1)}, f32[40,256]{1,0:T(8,128)S(1)}, u32[]{:S(2)}, u32[]{:S(2)}) collective-permute-start(f32[40,256]{1,0:T(8,128)S(1)} %get-tuple-element.99.own), channel_id=1, source_target_pairs={{0,8},{8,0},{16,24},{24,16},{1,9},{9,1},{17,25},{25,17},{2,10},{10... | collective-permute-start | bytes 122888 | tf_op jit(solution)/shard_map/ppermute | solution.py:414
  57.0 5.0 %collective-permute-start.11 = (f32[40,256]{1,0:T(8,128)S(1)}, f32[40,256]{1,0:T(8,128)S(1)}, u32[]{:S(2)}, u32[]{:S(2)}) collective-permute-start(f32[40,256]{1,0:T(8,128)S(1)} %pad_maximum_fusion), channel_id=1, source_target_pairs={{8,16},{16,8},{24,0},{0,24},{9,17},{17,9},{25,1},{1,25},{10,18},{1... | collective-permute-start | bytes 122888 | tf_op jit(solution)/shard_map/ppermute | solution.py:418
  63.6 5.9 %collective-permute-start.12 = (f32[128,256]{1,0:T(8,128)S(1)}, f32[128,256]{1,0:T(8,128)S(1)}, u32[]{:S(2)}, u32[]{:S(2)}) collective-permute-start(f32[128,256]{1,0:T(8,128)S(1)} %get-tuple-element.102), channel_id=1, source_target_pairs={{0,1},{1,0},{2,3},{3,2},{4,5},{5,4},{6,7},{7,6},{8,9},{9,8},{10,11... | collective-permute-start | bytes 393224 | tf_op jit(solution)/shard_map/ppermute | solution.py:407
  64.1 5.4 %collective-permute-start.13 = (f32[128,256]{1,0:T(8,128)S(1)}, f32[128,256]{1,0:T(8,128)S(1)}, u32[]{:S(2)}, u32[]{:S(2)}) collective-permute-start(f32[128,256]{1,0:T(8,128)S(1)} %get-tuple-element.103), channel_id=1, source_target_pairs={{1,2},{2,1},{3,4},{4,3},{5,6},{6,5},{9,10},{10,9},{11,12},{12,11},... | collective-permute-start | bytes 393224 | tf_op jit(solution)/shard_map/ppermute | solution.py:407
  64.8 4.7 %collective-permute-start.14 = (f32[128,256]{1,0:T(8,128)S(1)}, f32[128,256]{1,0:T(8,128)S(1)}, u32[]{:S(2)}, u32[]{:S(2)}) collective-permute-start(f32[128,256]{1,0:T(8,128)S(1)} %get-tuple-element.104), channel_id=1, source_target_pairs={{0,8},{8,0},{16,24},{24,16},{1,9},{9,1},{17,25},{25,17},{2,10},{10... | collective-permute-start | bytes 393224 | tf_op jit(solution)/shard_map/ppermute | solution.py:407
  65.0 4.5 %collective-permute-start.15 = (f32[128,256]{1,0:T(8,128)S(1)}, f32[128,256]{1,0:T(8,128)S(1)}, u32[]{:S(2)}, u32[]{:S(2)}) collective-permute-start(f32[128,256]{1,0:T(8,128)S(1)} %get-tuple-element.105), channel_id=1, source_target_pairs={{8,16},{16,8},{9,17},{17,9},{10,18},{18,10},{11,19},{19,11},{12,20... | collective-permute-start | bytes 393224 | tf_op jit(solution)/shard_map/ppermute | solution.py:407
  86.7 2.0 %collective-permute-start.16 = (f32[40,256]{1,0:T(8,128)S(1)}, f32[40,256]{1,0:T(8,128)S(1)}, u32[]{:S(2)}, u32[]{:S(2)}) collective-permute-start(f32[40,256]{1,0:T(8,128)S(1)} %get-tuple-element.112.own), channel_id=1, source_target_pairs={{0,8},{8,0},{16,24},{24,16},{1,9},{9,1},{17,25},{25,17},{2,10},{10... | collective-permute-start | bytes 122888 | tf_op jit(solution)/shard_map/ppermute | solution.py:414
  88.7 3.4 %collective-permute-start.17 = (f32[40,256]{1,0:T(8,128)S(1)}, f32[40,256]{1,0:T(8,128)S(1)}, u32[]{:S(2)}, u32[]{:S(2)}) collective-permute-start(f32[40,256]{1,0:T(8,128)S(1)} %pad_maximum_fusion.1), channel_id=1, source_target_pairs={{8,16},{16,8},{24,0},{0,24},{9,17},{17,9},{25,1},{1,25},{10,18},{1... | collective-permute-start | bytes 122888 | tf_op jit(solution)/shard_map/ppermute | solution.py:418
  93.9 19.1 %collective-permute-start.18 = (f32[128,256]{1,0:T(8,128)S(1)}, f32[128,256]{1,0:T(8,128)S(1)}, u32[]{:S(2)}, u32[]{:S(2)}) collective-permute-start(f32[128,256]{1,0:T(8,128)S(1)} %get-tuple-element.132), channel_id=1, source_target_pairs={{0,1},{1,0},{2,3},{3,2},{4,5},{5,4},{6,7},{7,6},{8,9},{9,8},{10,11... | collective-permute-start | bytes 393224 | tf_op jit(solution)/shard_map/ppermute | solution.py:407
  94.8 18.2 %collective-permute-start.19 = (f32[128,256]{1,0:T(8,128)S(1)}, f32[128,256]{1,0:T(8,128)S(1)}, u32[]{:S(2)}, u32[]{:S(2)}) collective-permute-start(f32[128,256]{1,0:T(8,128)S(1)} %get-tuple-element.133), channel_id=1, source_target_pairs={{1,2},{2,1},{3,4},{4,3},{5,6},{6,5},{9,10},{10,9},{11,12},{12,11},... | collective-permute-start | bytes 393224 | tf_op jit(solution)/shard_map/ppermute | solution.py:407
  95.4 17.5 %collective-permute-start.20 = (f32[128,256]{1,0:T(8,128)S(1)}, f32[128,256]{1,0:T(8,128)S(1)}, u32[]{:S(2)}, u32[]{:S(2)}) collective-permute-start(f32[128,256]{1,0:T(8,128)S(1)} %get-tuple-element.134), channel_id=1, source_target_pairs={{0,8},{8,0},{16,24},{24,16},{1,9},{9,1},{17,25},{25,17},{2,10},{10... | collective-permute-start | bytes 393224 | tf_op jit(solution)/shard_map/ppermute | solution.py:407
  95.6 17.3 %collective-permute-start.21 = (f32[128,256]{1,0:T(8,128)S(1)}, f32[128,256]{1,0:T(8,128)S(1)}, u32[]{:S(2)}, u32[]{:S(2)}) collective-permute-start(f32[128,256]{1,0:T(8,128)S(1)} %get-tuple-element.135), channel_id=1, source_target_pairs={{8,16},{16,8},{9,17},{17,9},{10,18},{18,10},{11,19},{19,11},{12,20... | collective-permute-start | bytes 393224 | tf_op jit(solution)/shard_map/ppermute | solution.py:407

commit v4 on v3

--- a/solution.py
+++ b/solution.py
@@ -10,6 +10,8 @@
 ITERS = 3
 PAD = 8
 ROWS = 256
+TALL = 256
+WIDE = 1024
 F32 = jnp.float32
 BF16 = jnp.bfloat16
 VM = pl.BlockSpec(memory_space=pltpu.VMEM)
@@ -237,8 +239,14 @@
         cols = slice(at * BLOCK, (at + 1) * BLOCK)
         total = total + dot_thin((l_hi[:, cols], l_lo[:, cols]), split(got[...]))
     for at in range(spread.shape[0]):
-        spread[at, :nmodes] = total
-        spread[at, nmodes:] = main[nmodes:]
+        for col in range(total.shape[1] // BLOCK):
+            cols = slice(col * BLOCK, (col + 1) * BLOCK)
+            spread[at, col * nmodes : (col + 1) * nmodes] = total[:, cols]
+    packed = (total.shape[1] // BLOCK) * nmodes
+    for at in range(spread.shape[0]):
+        for col in range(total.shape[1] // BLOCK):
+            cols = slice(col * BLOCK, (col + 1) * BLOCK)
+            spread[at, packed + 2 * col : packed + 2 * (col + 1)] = main[nmodes : nmodes + 2, cols]
 
 
 def faces_body(starts, image, c_hi, c_lo, g0, g1, g2, g3, qonce, qtwice, prod):
@@ -255,19 +263,28 @@
 
 
 def y_body(inverse_rows, i0, i1, gathered, own, others, coarse):
-    count, rows, _ = gathered.shape
-    nmodes = rows - PAD
-    blocks = jnp.concatenate([gathered[at, :nmodes] for at in range(count)], 0)
+    count = gathered.shape[0]
+    nmodes, width = coarse.shape
+    groups = width // BLOCK
+
+    def part(at, col):
+        return gathered[at, col * nmodes : (col + 1) * nmodes]
+
+    blocks = jnp.concatenate(
+        [jnp.concatenate([part(at, col) for col in range(groups)], 1) for at in range(count)], 0)
     skip = i0.shape[0] - nmodes
     value = dot6(jnp.concatenate([inverse_rows[...], i0[skip:], i1[skip:]], 0), blocks)
     own[:nmodes] = value[:nmodes]
     others[...] = value[nmodes:]
-    total = gathered[0, nmodes:]
+    tail = gathered[0, groups * nmodes :]
     for at in range(1, count):
-        total = total + gathered[at, nmodes:]
-    own[nmodes:] = total
+        tail = tail + gathered[at, groups * nmodes :]
+    own[nmodes:] = jnp.zeros((PAD, width), F32)
     me = lax.axis_index("sub")
-    coarse[...] = gathered[me, :nmodes]
+    for col in range(groups):
+        cols = slice(col * BLOCK, (col + 1) * BLOCK)
+        own[nmodes : nmodes + 2, cols] = tail[2 * col : 2 * (col + 1)]
+        coarse[:, cols] = part(me, col)
 
 
 def scalars(sums, rz_old, alpha_old):
@@ -298,9 +315,9 @@
         scal[...] = pack(alpha, beta, rz)
         ys = split(stacked(own, others, first, second))
 
-        @pl.loop(0, image.shape[0] // ROWS)
+        @pl.loop(0, image.shape[0] // WIDE)
         def _(at):
-            rows = pl.ds(pl.multiple_of(at * ROWS, ROWS), ROWS)
+            rows = pl.ds(pl.multiple_of(at * WIDE, WIDE), WIDE)
             value = prod[rows, :] + dot3(half((k_hi, k_lo), rows), ys)
             if has_old:
                 value = value + beta * along_old[rows, :]
@@ -333,9 +350,9 @@
                 value = value + beta * older
             return value, old - alpha * value
 
-        @pl.loop(0, vee.shape[0] // ROWS)
+        @pl.loop(0, vee.shape[0] // WIDE)
         def _(at):
-            rows = pl.ds(pl.multiple_of(at * ROWS, ROWS), ROWS)
+            rows = pl.ds(pl.multiple_of(at * WIDE, WIDE), WIDE)
             value = qtwice[rows, :] + dot3(half((b_hi, b_lo), rows), ys)
             value, vee_new[rows, :] = move(
                 vee[rows, :], value, t_old[rows, :] if has_old else None)
@@ -360,27 +377,35 @@
 
 
 def finish_body(starts, sums, scal0, scal1, b_hi, b_lo, e0, e1, e2, r0, r1, r2, along, image,
-                g0, g1, g2, g3, answer, resid):
-    at = pl.program_id(0)
-    rows = pl.ds(pl.multiple_of(at * ROWS, ROWS), ROWS)
+                g0, g1, g2, g3, answer_out, resid_out, answer, resid, sems):
     nmodes = e0.shape[0]
-    width = r0.shape[1]
+    order, width = r0.shape
     alpha, beta, _ = scalars(sums[...], scal1[2:3], scal1[0:1])
     a1 = scal1[0:1] + beta * alpha
     a0 = scal0[0:1] + scal1[1:2] * a1
+    chunks = [pl.ds(at * TALL, TALL) for at in range(order // TALL)]
+    copies = []
+
+    def send(source, target, rows):
+        copy = pltpu.make_async_copy(source.at[rows], target.at[rows], sems.at[len(copies)])
+        copy.start()
+        copies.append(copy)
+
     ys = split(a0 * e0[...] + a1 * e1[...] + alpha * e2[...])
-    maps = (b_hi[rows, :nmodes], b_lo[rows, :nmodes])
-    last = r2[rows, :]
-    answer[...] = a0 * r0[rows, :] + a1 * r1[rows, :] + alpha * last + dot3(maps, ys)
-    resid[...] = last - alpha * (image[rows, :] + beta * along[rows, :])
+    for rows in chunks:
+        part = dot3((b_hi[rows, :nmodes], b_lo[rows, :nmodes]), ys)
+        answer[rows, :] = a0 * r0[rows, :] + a1 * r1[rows, :] + alpha * r2[rows, :] + part
+        send(answer, answer_out, rows)
+    for rows in chunks:
+        resid[rows, :] = r2[rows, :] - alpha * (image[rows, :] + beta * along[rows, :])
     for which, got in enumerate((g0, g1, g2, g3)):
-        offset = starts[which] - at * ROWS
-
-        @pl.when((offset >= 0) & (offset < ROWS))
-        def _(which=which, got=got, offset=offset):
-            part = pl.ds(pl.multiple_of(offset, BLOCK), BLOCK)
-            mask = (0.5 * masks_of(starts, which, width)) * alpha
-            resid[part, :] = resid[part, :] - mask * got[...]
+        part = pl.ds(pl.multiple_of(starts[which], BLOCK), BLOCK)
+        mask = (0.5 * masks_of(starts, which, width)) * alpha
+        resid[part, :] = resid[part, :] - mask * got[...]
+    for rows in chunks:
+        send(resid, resid_out, rows)
+    for copy in copies:
+        copy.wait()
 
 
 def shards(compliance, loads, modes, coarse_inverse, face_block, edge_rows):
@@ -493,7 +518,7 @@
             vee, resid, kappa, eta, *along, main = update(False)
             resids.append(resid)
             etas.append(eta)
-        spread = call(coarse_late_body, [sds(nsub, nmodes + PAD, width)],
+        spread = call(coarse_late_body, [sds(nsub, (nmodes + 2) * (width // BLOCK), BLOCK)],
                       [main, *l_pair, *got])[0]
         gathered = gather(spread)
         qonce, qtwice, prod = call(
@@ -538,10 +563,14 @@
     args = [meta, sums, *scals, *b_pair, *etas, *resids, q_along, image, *got]
     answer, resid = pl.pallas_call(
         finish_body,
-        grid=(order // ROWS,),
         out_shape=[full, full],
         in_specs=[SM] + [VM] * (len(args) - 1),
-        out_specs=[pl.BlockSpec((ROWS, width), lambda at: (at, 0))] * 2,
+        out_specs=[far, far],
+        scratch_shapes=[
+            pltpu.VMEM((order, width), F32),
+            pltpu.VMEM((order, width), F32),
+            pltpu.SemaphoreType.DMA((2 * order // TALL,)),
+        ],
         compiler_params=pltpu.CompilerParams(vmem_limit_bytes=8 << 20),
         cost_estimate=pl.CostEstimate(
             flops=1_000_000, bytes_accessed=1 << 20, transcendentals=0),

time: 117 us -> 114 us (0.974)
  Pallas kernels: 28 us -> 26.1 us
    pallas_call x15, Pallas kernels: 19.1 us -> 17.6 us  [call(): pl.pallas_call(body, out_shape=outs, in_specs=[SM if at in smem_in else V...]
where the time goes in v4:
time: 114 us
  blocking collectives  48 us (42%)
  Pallas kernels  26.1 us (23%)
  starting transfers between devices  24.9 us (22%)
  waiting for transfers between devices  13.4 us (12%)
    all_to_all x3, blocking collectives, gather(): return lax.all_to_all(blocks, axis, 0, 0, tiled=False)  48 us
    pallas_call x15, Pallas kernels, call(): pl.pallas_call(body, out_shape=outs, in_specs=[SM if at in smem_in else V...  17.6 us
    ppermute x16, starting transfers between devices, exchange(): got[at] = lax.ppermute(messages[at], links[at][0], links[at][1])  10.2 us
    all_to_all x1, starting transfers between devices, gather(): return lax.all_to_all(blocks, axis, 0, 0, tiled=False)  7.29 us
    all_to_all x1, waiting for transfers between devices, gather(): return lax.all_to_all(blocks, axis, 0, 0, tiled=False)  6.36 us
    ppermute x16, waiting for transfers between devices, exchange(): got[at] = lax.ppermute(messages[at], links[at][0], links[at][1])  4.68 us
    pallas_call x1, Pallas kernels, shards(): pl.pallas_call(setup_body, out_shape=[sds(2 * nmodes, width), mapping, ma...  3.38 us
    ppermute x1, starting transfers between devices, shards(): first = lax.ppermute(own, 'cluster', pair_list(nclus, 0))  2.94 us
  transfers between devices with their start and end apart: 23, of which 6 were waited for; matrix products, arithmetic and copies ran while one was open for 0% of the time, Pallas kernels for 13%

profile of v4, /device:TPU:0, one launch (start us, length us, event | category | flops | bytes accessed | tf_op | source)
XLA Modules:
  0.0 113.6 jit_solution(8976505400297818614)
XLA Ops:
  0.6 2.3 %start.1 = (f32[192,256]{1,0:T(8,128)S(1)}, f32[192,256]{1,0:T(8,128)S(1)}, f32[160,256]{1,0:T(8,128)S(1)}, f32[160,256]{1,0:T(8,128)S(1)}, s32[8]{0:T(128)S(1)}...) custom-call(s32[4,4,8]{2,1,0:T(4,128)} %bitcast.15, ...), custom_call_target="tpu_custom_call" | custom-call | tf_op jit(solution)/shard_map/start/pallas_call | solution.py:456
  3.0 7.3 %all-to-all-start = ((f32[8,32,256]{2,1,0:T(8,128)}), f32[8,32,256]{2,1,0:T(8,128)S(1)}, u32[]{:S(2)}, u32[]{:S(2)}) async-start(f32[8,32,256]{2,1,0:T(8,128)} %get-tuple-element.75), calls=%async_computation | async-start | bytes 524288 | tf_op jit(solution)/shard_map/all_to_all | solution.py:436
  10.3 2.0 %collective-permute-start = (f32[192,256]{1,0:T(8,128)S(1)}, f32[192,256]{1,0:T(8,128)S(1)}, u32[]{:S(2)}, u32[]{:S(2)}) collective-permute-start(f32[192,256]{1,0:T(8,128)S(1)} %get-tuple-element.73), channel_id=1, source_target_pairs={{0,1},{1,0},{2,3},{3,2},{4,5},{5,4},{6,7},{7,6},{8,9},{9,8},{10,11... | collective-permute-start | bytes 589832 | tf_op jit(solution)/shard_map/ppermute | solution.py:432
  13.7 6.4 %all-to-all-done = f32[8,32,256]{2,1,0:T(8,128)S(1)} async-done(((f32[8,32,256]{2,1,0:T(8,128)}), f32[8,32,256]{2,1,0:T(8,128)S(1)}, u32[]{:S(2)}, u32[]{:S(2)}) %all-to-all-start) | async-done | bytes 262176 | tf_op jit(solution)/shard_map/all_to_all | solution.py:436
  21.0 2.9 %collective-permute-start.4 = (f32[32,256]{1,0:T(8,128)S(1)}, f32[32,256]{1,0:T(8,128)S(1)}, u32[]{:S(2)}, u32[]{:S(2)}) collective-permute-start(f32[32,256]{1,0:T(8,128)S(1)} %shard_map.77.own.eta.e0), channel_id=1, source_target_pairs={{0,8},{8,0},{16,24},{24,16},{1,9},{9,1},{17,25},{25,17},{2,10},{10... | collective-permute-start | bytes 98312 | tf_op jit(solution)/shard_map/ppermute | solution.py:481
  23.9 3.4 %setup.1 = (f32[64,256]{1,0:T(8,128)S(1)}, bf16[1024,160]{1,0:T(8,128)(2,1)S(1)}, bf16[1024,160]{1,0:T(8,128)(2,1)S(1)}, bf16[32,1024]{1,0:T(8,128)(2,1)S(1)}, b...) custom-call(s32[8]{0:T(128)S(1)} %get-tuple-element.70.starts, ...), custom_call_target="tpu_custom_call" | custom-call | flops 100000000 | bytes 4194304 | tf_op jit(solution)/shard_map/setup/pallas_call | solution.py:488
  27.3 3.4 %shard_map.78 = (f32[1024,256]{1,0:T(8,128)S(1)}, f32[1024,256]{1,0:T(8,128)S(1)}, f32[128,256]{1,0:T(8,128)S(1)}, f32[128,256]{1,0:T(8,128)S(1)}, f32[128,256]{1,0:T(8,128)S(1)}, /*index=5*/f32[128,256]{1,0:T(8,128)S(1)}) custom-call(s32[8]{0:T(128)S(1)} %get-tuple-element.70.starts, f32[1024,256]{1,0:T(8,128)S(1)} %get-tuple-element.78.base, ...), custom_call_target="tpu_custom_call" | custom-call | flops 1000000 | bytes 1048576 | tf_op jit(solution)/shard_map/pallas_call | solution.py:28
  30.8 1.1 collective-permute-start.6
  33.8 2.5 %collective-permute-done.6.g0 = f32[128,256]{1,0:T(8,128)S(1)} collective-permute-done((f32[128,256]{1,0:T(8,128)S(1)}, f32[128,256]{1,0:T(8,128)S(1)}, u32[]{:S(2)}, u32[]{:S(2)}) %collective-permute-start.6) | collective-permute-done | bytes 131104 | tf_op jit(solution)/shard_map/ppermute | solution.py:432
  36.5 17.0 %all_to_all.20.gathered = f32[8,68,128]{2,1,0:T(8,128)S(1)} all-to-all(f32[8,68,128]{2,1,0:T(8,128)S(1)} %shard_map.82), channel_id=1, replica_groups=mesh['cluster'=4,'sub'=8] {'sub'}, dimensions={0} | all-to-all | bytes 557056 | tf_op jit(solution)/shard_map/all_to_all | solution.py:436
  53.8 1.7 %collective-permute-start.10 = (f32[40,256]{1,0:T(8,128)S(1)}, f32[40,256]{1,0:T(8,128)S(1)}, u32[]{:S(2)}, u32[]{:S(2)}) collective-permute-start(f32[40,256]{1,0:T(8,128)S(1)} %get-tuple-element.99.own), channel_id=1, source_target_pairs={{0,8},{8,0},{16,24},{24,16},{1,9},{9,1},{17,25},{25,17},{2,10},{10... | collective-permute-start | bytes 122888 | tf_op jit(solution)/shard_map/ppermute | solution.py:439
  55.5 0.9 collective-permute-done.10.first
  57.2 1.8 %shard_map.80 = (bf16[1024,160]{1,0:T(8,128)(2,1)S(1)}, bf16[1024,160]{1,0:T(8,128)(2,1)S(1)}) custom-call(bf16[1024,1024]{1,0:T(8,128)(2,1)S(1)} %get-tuple-element.79.c_hi, bf16[1024,1024]{1,0:T(8,128)(2,1)S(1)} %get-tuple-element.80.c_lo, bf16[1024,160]{1,0:T(8,128)(2,1)S(1)} %get-tuple-element.81.b_hi, bf16[1024,160]{1,0:T(8,128)(2,1)S(1)} %get-tuple-element.82.b_lo), custom_call_target="tpu_custom_call" | custom-call | flops 50000000 | bytes 1048576 | tf_op jit(solution)/shard_map/pallas_call | solution.py:28
  59.0 2.7 %shard_map.79 = (f32[1024,256]{1,0:T(8,128)S(1)}, f32[1024,256]{1,0:T(8,128)S(1)}, f32[1024,256]{1,0:T(8,128)S(1)}) custom-call(s32[8]{0:T(128)S(1)} %get-tuple-element.70.starts, f32[1024,256]{1,0:T(8,128)S(1)} %get-tuple-element.85.image, bf16[1024,1024]{1,0:T(8,128)(2,1)S(1)} %get-tuple-element.79.c_hi, bf16[1024,1024]{1,0:T(8,128)(2,1)S(1)} %get-tuple-element.80.c_lo, ...), custom_call_target="tpu_custom_call" | custom-call | flops 100000000 | bytes 1048576 | tf_op jit(solution)/shard_map/pallas_call | solution.py:28
  61.7 1.2 %shard_map.84 = (f32[1024,256]{1,0:T(8,128)S(1)}, f32[1024,256]{1,0:T(8,128)S(1)}, f32[8,256]{1,0:T(8,128)S(1)}, f32[128,256]{1,0:T(8,128)S(1)}, f32[128,256]{1,...) custom-call(s32[8]{0:T(128)S(1)} %get-tuple-element.70.starts, f32[1024,256]{1,0:T(8,128)S(1)} %get-tuple-element.85.image, ...), custom_call_target="tpu_custom_call" | custom-call | flops 1000000 | bytes 1048576 | tf_op jit(solution)/shard_map/pallas_call | solution.py:28
  65.0 1.6 %shard_map.86 = (f32[1024,256]{1,0:T(8,128)S(1)}, f32[1024,256]{1,0:T(8,128)S(1)}, f32[32,256]{1,0:T(8,128)S(1)}, f32[32,256]{1,0:T(8,128)S(1)}, f32[1024,256]{1...) custom-call(f32[8,256]{1,0:T(8,128)S(1)} %get-tuple-element.107.scal, ...), custom_call_target="tpu_custom_call" | custom-call | flops 1000000 | bytes 1048576 | tf_op jit(solution)/shard_map/pallas_call | solution.py:28
  66.6 2.2 %collective-permute-done.12.g0 = f32[128,256]{1,0:T(8,128)S(1)} collective-permute-done((f32[128,256]{1,0:T(8,128)S(1)}, f32[128,256]{1,0:T(8,128)S(1)}, u32[]{:S(2)}, u32[]{:S(2)}) %collective-permute-start.12) | collective-permute-done | bytes 131104 | tf_op jit(solution)/shard_map/ppermute | solution.py:432
  69.0 16.1 %all_to_all.21.gathered = f32[8,68,128]{2,1,0:T(8,128)S(1)} all-to-all(f32[8,68,128]{2,1,0:T(8,128)S(1)} %shard_map.87), channel_id=1, replica_groups=mesh['cluster'=4,'sub'=8] {'sub'}, dimensions={0} | all-to-all | bytes 557056 | tf_op jit(solution)/shard_map/all_to_all | solution.py:436
  85.3 1.2 %collective-permute-start.16 = (f32[40,256]{1,0:T(8,128)S(1)}, f32[40,256]{1,0:T(8,128)S(1)}, u32[]{:S(2)}, u32[]{:S(2)}) collective-permute-start(f32[40,256]{1,0:T(8,128)S(1)} %get-tuple-element.112.own), channel_id=1, source_target_pairs={{0,8},{8,0},{16,24},{24,16},{1,9},{9,1},{17,25},{25,17},{2,10},{10... | collective-permute-start | bytes 122888 | tf_op jit(solution)/shard_map/ppermute | solution.py:439
  87.5 2.7 %shard_map.85 = (f32[1024,256]{1,0:T(8,128)S(1)}, f32[1024,256]{1,0:T(8,128)S(1)}, f32[1024,256]{1,0:T(8,128)S(1)}) custom-call(s32[8]{0:T(128)S(1)} %get-tuple-element.70.starts, f32[1024,256]{1,0:T(8,128)S(1)} %get-tuple-element.101.image, bf16[1024,1024]{1,0:T(8,128)(2,1)S(1)} %get-tuple-element.79.c_hi, bf16[1024,1024]{1,0:T(8,128)(2,1)S(1)} %get-tuple-element.80.c_lo, ...), custom_call_target="tpu_custom_call" | custom-call | flops 100000000 | bytes 1048576 | tf_op jit(solution)/shard_map/pallas_call | solution.py:28
  90.8 1.2 %shard_map.89 = (f32[1024,256]{1,0:T(8,128)S(1)}, f32[8,256]{1,0:T(8,128)S(1)}, f32[128,256]{1,0:T(8,128)S(1)}, f32[128,256]{1,0:T(8,128)S(1)}, f32[128,256]{1,0:T(8,128)S(1)}, /*index=5*/f32[128,256]{1,0:T(8,128)S(1)}) custom-call(s32[8]{0:T(128)S(1)} %get-tuple-element.70.starts, f32[1024,256]{1,0:T(8,128)S(1)} %get-tuple-element.101.image, ...), custom_call_target="tpu_custom_call" | custom-call | flops 1000000 | bytes 1048576 | tf_op jit(solution)/shard_map/pallas_call | solution.py:28
  94.3 1.3 %shard_map.90 = (f32[1024,256]{1,0:T(8,128)S(1)}, f32[32,256]{1,0:T(8,128)S(1)}, f32[1024,256]{1,0:T(8,128)S(1)}, f32[32,2,256]{2,1,0:T(2,128)S(1)}) custom-call(f32[8,256]{1,0:T(8,128)S(1)} %get-tuple-element.115.scal.scal1, f32[1024,256]{1,0:T(8,128)S(1)} %get-tuple-element.116.vee, f32[1024,256]{1,0:T(8,128)S(1)} %get-tuple-element.117.qtwice, ...), custom_call_target="tpu_custom_call" | custom-call | flops 1000000 | bytes 1048576 | tf_op jit(solution)/shard_map/pallas_call | solution.py:28
  95.6 14.9 %all_to_all.22.everyone = f32[32,2,256]{2,1,0:T(2,128)S(1)} all-to-all(f32[32,2,256]{2,1,0:T(2,128)S(1)} %get-tuple-element.128), channel_id=1, replica_groups=mesh['cluster'=4,'sub'=8] {'cluster','sub'}, dimensions={0} | all-to-all | bytes 131072 | tf_op jit(solution)/shard_map/all_to_all | solution.py:436
  110.6 2.8 %finish.1 = (f32[1024,256]{1,0:T(8,128)}, f32[1024,256]{1,0:T(8,128)}) custom-call(s32[8]{0:T(128)S(1)} %get-tuple-element.70.starts, f32[2,256]{1,0:T(2,128)S(1)} %shard_map.91.sums, f32[8,256]{1,0:T(8,128)S(1)} %get-tuple-element.107.scal.rest_0_.scal0, f32[8,256]{1,0:T(8,128)S(1)} %get-tuple-element.115.scal.scal1, ...), custom_call_target="tpu_custom_call" | custom-call | flops 1000000 | bytes 1048576 | tf_op jit(solution)/shard_map/finish/pallas_call | solution.py:564
  (49 shorter events, 12.1 us)
Async XLA Ops:
  3.0 17.1 %all-to-all-start = ((f32[8,32,256]{2,1,0:T(8,128)}), f32[8,32,256]{2,1,0:T(8,128)S(1)}, u32[]{:S(2)}, u32[]{:S(2)}) async-start(f32[8,32,256]{2,1,0:T(8,128)} %get-tuple-element.75), calls=%async_computation | async-start | bytes 524288 | tf_op jit(solution)/shard_map/all_to_all | solution.py:436
  10.3 13.7 %collective-permute-start = (f32[192,256]{1,0:T(8,128)S(1)}, f32[192,256]{1,0:T(8,128)S(1)}, u32[]{:S(2)}, u32[]{:S(2)}) collective-permute-start(f32[192,256]{1,0:T(8,128)S(1)} %get-tuple-element.73), channel_id=1, source_target_pairs={{0,1},{1,0},{2,3},{3,2},{4,5},{5,4},{6,7},{7,6},{8,9},{9,8},{10,11... | collective-permute-start | bytes 589832 | tf_op jit(solution)/shard_map/ppermute | solution.py:432
  12.3 11.6 %collective-permute-start.1 = (f32[192,256]{1,0:T(8,128)S(1)}, f32[192,256]{1,0:T(8,128)S(1)}, u32[]{:S(2)}, u32[]{:S(2)}) collective-permute-start(f32[192,256]{1,0:T(8,128)S(1)} %get-tuple-element.74), channel_id=1, source_target_pairs={{1,2},{2,1},{3,4},{4,3},{5,6},{6,5},{9,10},{10,9},{11,12},{12,11},... | collective-permute-start | bytes 589832 | tf_op jit(solution)/shard_map/ppermute | solution.py:432
  12.9 8.0 %collective-permute-start.2 = (f32[160,256]{1,0:T(8,128)S(1)}, f32[160,256]{1,0:T(8,128)S(1)}, u32[]{:S(2)}, u32[]{:S(2)}) collective-permute-start(f32[160,256]{1,0:T(8,128)S(1)} %get-tuple-element.76), channel_id=1, source_target_pairs={{0,8},{8,0},{16,24},{24,16},{1,9},{9,1},{17,25},{25,17},{2,10},{10... | collective-permute-start | bytes 491528 | tf_op jit(solution)/shard_map/ppermute | solution.py:432
  13.0 10.9 %collective-permute-start.3 = (f32[160,256]{1,0:T(8,128)S(1)}, f32[160,256]{1,0:T(8,128)S(1)}, u32[]{:S(2)}, u32[]{:S(2)}) collective-permute-start(f32[160,256]{1,0:T(8,128)S(1)} %get-tuple-element.77), channel_id=1, source_target_pairs={{8,16},{16,8},{9,17},{17,9},{10,18},{18,10},{11,19},{19,11},{12,20... | collective-permute-start | bytes 491528 | tf_op jit(solution)/shard_map/ppermute | solution.py:432
  20.3 7.0 %collective-permute-start.5 = (f32[32,256]{1,0:T(8,128)S(1)}, f32[32,256]{1,0:T(8,128)S(1)}, u32[]{:S(2)}, u32[]{:S(2)}) collective-permute-start(f32[32,256]{1,0:T(8,128)S(1)} %shard_map.77.own.eta.e0), channel_id=1, source_target_pairs={{8,16},{16,8},{9,17},{17,9},{10,18},{18,10},{11,19},{19,11},{12,20... | collective-permute-start | bytes 98312 | tf_op jit(solution)/shard_map/ppermute | solution.py:482
  21.0 6.3 %collective-permute-start.4 = (f32[32,256]{1,0:T(8,128)S(1)}, f32[32,256]{1,0:T(8,128)S(1)}, u32[]{:S(2)}, u32[]{:S(2)}) collective-permute-start(f32[32,256]{1,0:T(8,128)S(1)} %shard_map.77.own.eta.e0), channel_id=1, source_target_pairs={{0,8},{8,0},{16,24},{24,16},{1,9},{9,1},{17,25},{25,17},{2,10},{10... | collective-permute-start | bytes 98312 | tf_op jit(solution)/shard_map/ppermute | solution.py:481
  30.8 5.5 %collective-permute-start.6 = (f32[128,256]{1,0:T(8,128)S(1)}, f32[128,256]{1,0:T(8,128)S(1)}, u32[]{:S(2)}, u32[]{:S(2)}) collective-permute-start(f32[128,256]{1,0:T(8,128)S(1)} %get-tuple-element.86), channel_id=1, source_target_pairs={{0,1},{1,0},{2,3},{3,2},{4,5},{5,4},{6,7},{7,6},{8,9},{9,8},{10,11... | collective-permute-start | bytes 393224 | tf_op jit(solution)/shard_map/ppermute | solution.py:432
  31.8 4.5 %collective-permute-start.7 = (f32[128,256]{1,0:T(8,128)S(1)}, f32[128,256]{1,0:T(8,128)S(1)}, u32[]{:S(2)}, u32[]{:S(2)}) collective-permute-start(f32[128,256]{1,0:T(8,128)S(1)} %get-tuple-element.87), channel_id=1, source_target_pairs={{1,2},{2,1},{3,4},{4,3},{5,6},{6,5},{9,10},{10,9},{11,12},{12,11},... | collective-permute-start | bytes 393224 | tf_op jit(solution)/shard_map/ppermute | solution.py:432
  32.5 3.8 %collective-permute-start.8 = (f32[128,256]{1,0:T(8,128)S(1)}, f32[128,256]{1,0:T(8,128)S(1)}, u32[]{:S(2)}, u32[]{:S(2)}) collective-permute-start(f32[128,256]{1,0:T(8,128)S(1)} %get-tuple-element.88), channel_id=1, source_target_pairs={{0,8},{8,0},{16,24},{24,16},{1,9},{9,1},{17,25},{25,17},{2,10},{10... | collective-permute-start | bytes 393224 | tf_op jit(solution)/shard_map/ppermute | solution.py:432
  32.6 3.7 %collective-permute-start.9 = (f32[128,256]{1,0:T(8,128)S(1)}, f32[128,256]{1,0:T(8,128)S(1)}, u32[]{:S(2)}, u32[]{:S(2)}) collective-permute-start(f32[128,256]{1,0:T(8,128)S(1)} %get-tuple-element.89), channel_id=1, source_target_pairs={{8,16},{16,8},{9,17},{17,9},{10,18},{18,10},{11,19},{19,11},{12,20... | collective-permute-start | bytes 393224 | tf_op jit(solution)/shard_map/ppermute | solution.py:432
  53.8 2.6 %collective-permute-start.10 = (f32[40,256]{1,0:T(8,128)S(1)}, f32[40,256]{1,0:T(8,128)S(1)}, u32[]{:S(2)}, u32[]{:S(2)}) collective-permute-start(f32[40,256]{1,0:T(8,128)S(1)} %get-tuple-element.99.own), channel_id=1, source_target_pairs={{0,8},{8,0},{16,24},{24,16},{1,9},{9,1},{17,25},{25,17},{2,10},{10... | collective-permute-start | bytes 122888 | tf_op jit(solution)/shard_map/ppermute | solution.py:439
  56.4 5.3 %collective-permute-start.11 = (f32[40,256]{1,0:T(8,128)S(1)}, f32[40,256]{1,0:T(8,128)S(1)}, u32[]{:S(2)}, u32[]{:S(2)}) collective-permute-start(f32[40,256]{1,0:T(8,128)S(1)} %pad_maximum_fusion), channel_id=1, source_target_pairs={{8,16},{16,8},{24,0},{0,24},{9,17},{17,9},{25,1},{1,25},{10,18},{1... | collective-permute-start | bytes 122888 | tf_op jit(solution)/shard_map/ppermute | solution.py:443
  62.9 5.9 %collective-permute-start.12 = (f32[128,256]{1,0:T(8,128)S(1)}, f32[128,256]{1,0:T(8,128)S(1)}, u32[]{:S(2)}, u32[]{:S(2)}) collective-permute-start(f32[128,256]{1,0:T(8,128)S(1)} %get-tuple-element.102), channel_id=1, source_target_pairs={{0,1},{1,0},{2,3},{3,2},{4,5},{5,4},{6,7},{7,6},{8,9},{9,8},{10,11... | collective-permute-start | bytes 393224 | tf_op jit(solution)/shard_map/ppermute | solution.py:432
  63.4 5.3 %collective-permute-start.13 = (f32[128,256]{1,0:T(8,128)S(1)}, f32[128,256]{1,0:T(8,128)S(1)}, u32[]{:S(2)}, u32[]{:S(2)}) collective-permute-start(f32[128,256]{1,0:T(8,128)S(1)} %get-tuple-element.103), channel_id=1, source_target_pairs={{1,2},{2,1},{3,4},{4,3},{5,6},{6,5},{9,10},{10,9},{11,12},{12,11},... | collective-permute-start | bytes 393224 | tf_op jit(solution)/shard_map/ppermute | solution.py:432
  64.1 4.7 %collective-permute-start.14 = (f32[128,256]{1,0:T(8,128)S(1)}, f32[128,256]{1,0:T(8,128)S(1)}, u32[]{:S(2)}, u32[]{:S(2)}) collective-permute-start(f32[128,256]{1,0:T(8,128)S(1)} %get-tuple-element.104), channel_id=1, source_target_pairs={{0,8},{8,0},{16,24},{24,16},{1,9},{9,1},{17,25},{25,17},{2,10},{10... | collective-permute-start | bytes 393224 | tf_op jit(solution)/shard_map/ppermute | solution.py:432
  64.3 4.5 %collective-permute-start.15 = (f32[128,256]{1,0:T(8,128)S(1)}, f32[128,256]{1,0:T(8,128)S(1)}, u32[]{:S(2)}, u32[]{:S(2)}) collective-permute-start(f32[128,256]{1,0:T(8,128)S(1)} %get-tuple-element.105), channel_id=1, source_target_pairs={{8,16},{16,8},{9,17},{17,9},{10,18},{18,10},{11,19},{19,11},{12,20... | collective-permute-start | bytes 393224 | tf_op jit(solution)/shard_map/ppermute | solution.py:432
  85.3 2.0 %collective-permute-start.16 = (f32[40,256]{1,0:T(8,128)S(1)}, f32[40,256]{1,0:T(8,128)S(1)}, u32[]{:S(2)}, u32[]{:S(2)}) collective-permute-start(f32[40,256]{1,0:T(8,128)S(1)} %get-tuple-element.112.own), channel_id=1, source_target_pairs={{0,8},{8,0},{16,24},{24,16},{1,9},{9,1},{17,25},{25,17},{2,10},{10... | collective-permute-start | bytes 122888 | tf_op jit(solution)/shard_map/ppermute | solution.py:439
  87.4 3.4 %collective-permute-start.17 = (f32[40,256]{1,0:T(8,128)S(1)}, f32[40,256]{1,0:T(8,128)S(1)}, u32[]{:S(2)}, u32[]{:S(2)}) collective-permute-start(f32[40,256]{1,0:T(8,128)S(1)} %pad_maximum_fusion.1), channel_id=1, source_target_pairs={{8,16},{16,8},{24,0},{0,24},{9,17},{17,9},{25,1},{1,25},{10,18},{1... | collective-permute-start | bytes 122888 | tf_op jit(solution)/shard_map/ppermute | solution.py:443
  92.0 18.6 %collective-permute-start.18 = (f32[128,256]{1,0:T(8,128)S(1)}, f32[128,256]{1,0:T(8,128)S(1)}, u32[]{:S(2)}, u32[]{:S(2)}) collective-permute-start(f32[128,256]{1,0:T(8,128)S(1)} %get-tuple-element.132), channel_id=1, source_target_pairs={{0,1},{1,0},{2,3},{3,2},{4,5},{5,4},{6,7},{7,6},{8,9},{9,8},{10,11... | collective-permute-start | bytes 393224 | tf_op jit(solution)/shard_map/ppermute | solution.py:432
  92.8 17.8 %collective-permute-start.19 = (f32[128,256]{1,0:T(8,128)S(1)}, f32[128,256]{1,0:T(8,128)S(1)}, u32[]{:S(2)}, u32[]{:S(2)}) collective-permute-start(f32[128,256]{1,0:T(8,128)S(1)} %get-tuple-element.133), channel_id=1, source_target_pairs={{1,2},{2,1},{3,4},{4,3},{5,6},{6,5},{9,10},{10,9},{11,12},{12,11},... | collective-permute-start | bytes 393224 | tf_op jit(solution)/shard_map/ppermute | solution.py:432
  93.5 17.2 %collective-permute-start.20 = (f32[128,256]{1,0:T(8,128)S(1)}, f32[128,256]{1,0:T(8,128)S(1)}, u32[]{:S(2)}, u32[]{:S(2)}) collective-permute-start(f32[128,256]{1,0:T(8,128)S(1)} %get-tuple-element.134), channel_id=1, source_target_pairs={{0,8},{8,0},{16,24},{24,16},{1,9},{9,1},{17,25},{25,17},{2,10},{10... | collective-permute-start | bytes 393224 | tf_op jit(solution)/shard_map/ppermute | solution.py:432
  93.7 17.0 %collective-permute-start.21 = (f32[128,256]{1,0:T(8,128)S(1)}, f32[128,256]{1,0:T(8,128)S(1)}, u32[]{:S(2)}, u32[]{:S(2)}) collective-permute-start(f32[128,256]{1,0:T(8,128)S(1)} %get-tuple-element.135), channel_id=1, source_target_pairs={{8,16},{16,8},{9,17},{17,9},{10,18},{18,10},{11,19},{19,11},{12,20... | collective-permute-start | bytes 393224 | tf_op jit(solution)/shard_map/ppermute | solution.py:432

commit v5 on v4

--- a/solution.py
+++ b/solution.py
@@ -108,11 +108,13 @@
     for at, message in enumerate(messages):
         start = pl.multiple_of(meta[at], BLOCK)
         message[:BLOCK] = rhs[pl.ds(start, BLOCK), :]
-        message[BLOCK : BLOCK + nmodes, :BLOCK] = basis[:, pl.ds(start, BLOCK)]
-        if width > BLOCK:
-            message[BLOCK : BLOCK + nmodes, BLOCK:] = jnp.zeros((nmodes, width - BLOCK), F32)
+        groups = width // BLOCK
+        rows = nmodes // groups
+        for col in range(groups):
+            message[BLOCK : BLOCK + rows, col * BLOCK : (col + 1) * BLOCK] = basis[
+                col * rows : (col + 1) * rows, pl.ds(start, BLOCK)]
         if at < 2:
-            message[BLOCK + nmodes :] = inverse_rows[...]
+            message[BLOCK + rows :] = inverse_rows[...]
     value = dot_thin(split(basis[...]), split(rhs[...]))
     kappa[...] = value
     for at in range(spread.shape[0]):
@@ -124,7 +126,13 @@
     return (ids < starts[4 + at]).astype(F32)
 
 
-def setup_body(starts, matrix, rhs, basis, i0, i1, gathered, g0, g1, g2, g3,
+def link_maps(got, mask, rows, at, nmodes, base, b_hi, b_lo):
+    base[rows, :] = base[rows, :] + mask * got[:BLOCK, :]
+    cols = slice((at + 1) * nmodes, (at + 2) * nmodes)
+    b_hi[rows, cols], b_lo[rows, cols] = split(mask[:, :nmodes] * modes_of(got, nmodes).T)
+
+
+def setup_body(starts, matrix, rhs, basis, i0, i1, gathered, g0, g1,
                others, b_hi, b_lo, m_hi, m_lo, l_hi, l_lo, base, c_hi, c_lo, held, sems):
     nmodes, order = basis.shape
     parts = [pl.ds(at * ROWS, ROWS) for at in range(order // ROWS)]
@@ -144,14 +152,12 @@
     b_lo[...] = jnp.zeros_like(b_lo)
     own = basis[...].T
     b_hi[:, :nmodes], b_lo[:, :nmodes] = split(own)
-    for at, got in enumerate((g0, g1, g2, g3)):
+    for at in range(4):
         start = pl.multiple_of(starts[at], BLOCK)
         rows = pl.ds(start, BLOCK)
-        mask = 0.5 * masks_of(starts, at, width)
-        base[rows, :] = base[rows, :] + mask * got[:BLOCK, :]
-        theirs = got[BLOCK : BLOCK + nmodes, :BLOCK].T
-        cols = slice((at + 1) * nmodes, (at + 2) * nmodes)
-        b_hi[rows, cols], b_lo[rows, cols] = split(mask[:, :nmodes] * theirs)
+        if at < 2:
+            got = (g0, g1)[at]
+            link_maps(got, 0.5 * masks_of(starts, at, width), rows, at, nmodes, base, b_hi, b_lo)
         ids = lax.broadcasted_iota(jnp.int32, (nmodes, BLOCK), 1)
         weight = 0.5 * (ids < starts[4 + at]).astype(F32)
         cols = slice(at * BLOCK, (at + 1) * BLOCK)
@@ -174,8 +180,19 @@
         out[...] = field[pl.ds(pl.multiple_of(starts[at], BLOCK), BLOCK), :]
 
 
-def first_y_body(inverse_rows, gathered, own):
-    own[...] = dot6(inverse_rows[...], gathered[...])
+def modes_of(got, nmodes):
+    groups = got.shape[1] // BLOCK
+    rows = nmodes // groups
+    return jnp.concatenate(
+        [got[BLOCK : BLOCK + rows, col * BLOCK : (col + 1) * BLOCK] for col in range(groups)], 0)
+
+
+def first_y_body(inverse_rows, gathered, head0, head1, own, message0, message1):
+    value = dot6(inverse_rows[...], gathered[...])
+    own[...] = value
+    for head, message in ((head0, message0), (head1, message1)):
+        message[: head.shape[0]] = head[...]
+        message[head.shape[0] :] = value
 
 
 def fold_body(everyone, out):
@@ -190,17 +207,24 @@
     return jnp.concatenate([own[:nmodes], others[...], first[:nmodes], second[:nmodes]], 0)
 
 
-def first_apply_body(starts, base, c_hi, c_lo, b_hi, b_lo, own, others, first, second,
-                     vee, image, *outs):
-    ys = split(stacked(own, others, first, second))
-
-    @pl.loop(0, base.shape[0] // ROWS)
+def first_apply_body(starts, base, c_hi, c_lo, b_in_hi, b_in_lo, own, others, first, second,
+                     vee, image, b_hi, b_lo, *outs):
+    nmodes, width = own.shape
+    vee[...] = base[...]
+    b_hi[...], b_lo[...] = b_in_hi[...], b_in_lo[...]
+    for at, got in ((2, first), (3, second)):
+        rows = pl.ds(pl.multiple_of(starts[at], BLOCK), BLOCK)
+        mask = 0.5 * masks_of(starts, at, width)
+        link_maps(got, mask, rows, at, nmodes, vee, b_hi, b_lo)
+    skip = first.shape[0] - nmodes
+    ys = split(jnp.concatenate([own[...], others[...], first[skip:], second[skip:]], 0))
+
+    @pl.loop(0, base.shape[0] // WIDE)
     def _(at):
-        rows = pl.ds(pl.multiple_of(at * ROWS, ROWS), ROWS)
-        vee[rows, :] = base[rows, :] + dot3(half((b_hi, b_lo), rows), ys)
+        rows = pl.ds(pl.multiple_of(at * WIDE, WIDE), WIDE)
+        vee[rows, :] = vee[rows, :] + dot3(half((b_hi, b_lo), rows), ys)
 
     image[...] = dot3((c_hi[...], c_lo[...]), split(vee[...]))
-
     copy_faces(starts, image, outs)
 
 
@@ -451,7 +475,8 @@
         )
 
     extra = nmodes * coarse_all // width
-    sizes = [BLOCK + nmodes + (extra if at < 2 else 0) for at in range(4)]
+    head = BLOCK + nmodes * BLOCK // width
+    sizes = [head + (extra if at < 2 else 0) for at in range(4)]
     far = pl.BlockSpec(memory_space=pltpu.HBM)
     *messages, meta, kappa, spread, rhs, basis, flat = pl.pallas_call(
         start_body,
@@ -472,14 +497,18 @@
         inverse_rows.reshape(extra, width))))
     if coarse_all == width:
         inverse_rows = flat
-    got = exchange(messages)
+    got = [None] * 2
+    for at in (1, 0):
+        got[at] = lax.ppermute(messages[at], links[at][0], links[at][1])
     gathered = gather(spread).reshape(nsub * nmodes, width)
-    inverses = [inverse_rows, *got[:2]]
+    inverses = [inverse_rows, *got]
     if coarse_all != width:
-        inverses[1:] = [each[BLOCK + nmodes :].reshape(nmodes, coarse_all) for each in got[:2]]
-    own = call(first_y_body, [small], [inverse_rows, gathered])[0]
-    first = lax.ppermute(own, "cluster", pair_list(nclus, 0))
-    second = lax.ppermute(own, "cluster", pair_list(nclus, 1))
+        inverses[1:] = [each[head:].reshape(nmodes, coarse_all) for each in got]
+    joined = sds(head + nmodes, width)
+    own, *tails = call(
+        first_y_body, [small, joined, joined], [inverse_rows, gathered, *messages[2:]])
+    second = lax.ppermute(tails[1], "cluster", pair_list(nclus, 1))
+    first = lax.ppermute(tails[0], "cluster", pair_list(nclus, 0))
     mapping = sds(order, tall, dtype=BF16)
     thin = sds(nmodes, order, dtype=BF16)
     lates = sds(nmodes, 4 * BLOCK, dtype=BF16)
@@ -499,9 +528,10 @@
     )(*args)
     c_pair = (c_hi, c_lo)
     b_pair, m_pair, l_pair = pairs[0:2], pairs[2:4], pairs[4:6]
-    vee, image, *own_faces = call(
-        first_apply_body, [full, full] + [block] * 4,
+    vee, image, *b_pair, f0, f1, f2, f3 = call(
+        first_apply_body, [full, full, mapping, mapping] + [block] * 4,
         [meta, base, *c_pair, *b_pair, own, others, first, second], smem_in=(0,))
+    own_faces = (f0, f1, f2, f3)
     resid, eta = rhs, own
 
     resids, etas, scals = [resid], [eta], []

time: 114 us -> 114 us (level)
  starting transfers between devices: 24.9 us -> 23.1 us
    ppermute x16 -> x12, starting transfers between devices: 10.2 us -> 8.58 us  [exchange(): got[at] = lax.ppermute(messages[at], links[at][0], links[at][1])]
    ppermute x16 -> x12, waiting for transfers between devices: 4.68 us -> 3.45 us  [exchange(): got[at] = lax.ppermute(messages[at], links[at][0], links[at][1])]
    ppermute x2 -> x4, starting transfers between devices: 3.6 us -> 3.42 us  [the longest x2 2.68 us: shards(): got[at] = lax.ppermute(messages[at], links[at][0], links[at][1])]
  transfers between devices with their start and end apart: 23 -> 21, of which waited for: 6 -> 7; matrix products, arithmetic and copies ran while one was open for 0% -> 0% of each run, Pallas kernels for 13% -> 13%
where the time goes in v5:
time: 114 us; the launch traced here: 113 us
  blocking collectives  49 us (43%)
  Pallas kernels  26.4 us (23%)
  starting transfers between devices  23.1 us (20%)
  waiting for transfers between devices  13.7 us (12%)
    all_to_all x3, blocking collectives, gather(): return lax.all_to_all(blocks, axis, 0, 0, tiled=False)  49 us
    pallas_call x15, Pallas kernels, call(): pl.pallas_call(body, out_shape=outs, in_specs=[SM if at in smem_in else V...  17.9 us
    ppermute x12, starting transfers between devices, exchange(): got[at] = lax.ppermute(messages[at], links[at][0], links[at][1])  8.58 us
    all_to_all x1, starting transfers between devices, gather(): return lax.all_to_all(blocks, axis, 0, 0, tiled=False)  7.29 us
    all_to_all x1, waiting for transfers between devices, gather(): return lax.all_to_all(blocks, axis, 0, 0, tiled=False)  7.12 us
    ppermute x12, waiting for transfers between devices, exchange(): got[at] = lax.ppermute(messages[at], links[at][0], links[at][1])  3.45 us
    pallas_call x1, Pallas kernels, shards(): pl.pallas_call(setup_body, out_shape=[sds(2 * nmodes, width), mapping, ma...  3.33 us
    ppermute x2, starting transfers between devices, mirror(): first = lax.ppermute(ymom, 'cluster', pair_list(nclus, 0))  2.9 us
  transfers between devices with their start and end apart: 21, of which 7 were waited for; matrix products, arithmetic and copies ran while one was open for 0% of the time, Pallas kernels for 13%

profile of v5, /device:TPU:0, one launch (start us, length us, event | category | flops | bytes accessed | tf_op | source)
XLA Modules:
  0.0 113.1 jit_solution(5043177136914706727)
XLA Ops:
  0.6 2.3 %start.1 = (f32[176,256]{1,0:T(8,128)S(1)}, f32[176,256]{1,0:T(8,128)S(1)}, f32[144,256]{1,0:T(8,128)S(1)}, f32[144,256]{1,0:T(8,128)S(1)}, s32[8]{0:T(128)S(1)}...) custom-call(s32[4,4,8]{2,1,0:T(4,128)} %bitcast.15, ...), custom_call_target="tpu_custom_call" | custom-call | tf_op jit(solution)/shard_map/start/pallas_call | solution.py:481
  3.0 7.3 %all-to-all-start = ((f32[8,32,256]{2,1,0:T(8,128)}), f32[8,32,256]{2,1,0:T(8,128)S(1)}, u32[]{:S(2)}, u32[]{:S(2)}) async-start(f32[8,32,256]{2,1,0:T(8,128)} %get-tuple-element.80), calls=%async_computation | async-start | bytes 524288 | tf_op jit(solution)/shard_map/all_to_all | solution.py:460
  10.3 2.0 %collective-permute-start = (f32[176,256]{1,0:T(8,128)S(1)}, f32[176,256]{1,0:T(8,128)S(1)}, u32[]{:S(2)}, u32[]{:S(2)}) collective-permute-start(f32[176,256]{1,0:T(8,128)S(1)} %get-tuple-element.78), channel_id=1, source_target_pairs={{0,1},{1,0},{2,3},{3,2},{4,5},{5,4},{6,7},{7,6},{8,9},{9,8},{10,11... | collective-permute-start | bytes 540680 | tf_op jit(solution)/shard_map/ppermute | solution.py:502
  12.9 7.1 %all-to-all-done = f32[8,32,256]{2,1,0:T(8,128)S(1)} async-done(((f32[8,32,256]{2,1,0:T(8,128)}), f32[8,32,256]{2,1,0:T(8,128)S(1)}, u32[]{:S(2)}, u32[]{:S(2)}) %all-to-all-start) | async-done | bytes 262176 | tf_op jit(solution)/shard_map/all_to_all | solution.py:460
  21.7 3.3 %setup.1 = (f32[64,256]{1,0:T(8,128)S(1)}, bf16[1024,160]{1,0:T(8,128)(2,1)S(1)}, bf16[1024,160]{1,0:T(8,128)(2,1)S(1)}, bf16[32,1024]{1,0:T(8,128)(2,1)S(1)}, b...) custom-call(s32[8]{0:T(128)S(1)} %get-tuple-element.75.starts, ...), custom_call_target="tpu_custom_call" | custom-call | flops 100000000 | bytes 4194304 | tf_op jit(solution)/shard_map/setup/pallas_call | solution.py:517
  25.1 3.7 %shard_map.78 = (f32[1024,256]{1,0:T(8,128)S(1)}, f32[1024,256]{1,0:T(8,128)S(1)}, bf16[1024,160]{1,0:T(8,128)(2,1)S(1)}, bf16[1024,160]{1,0:T(8,128)(2,1)S(1)},...) custom-call(s32[8]{0:T(128)S(1)} %get-tuple-element.75.starts, ...), custom_call_target="tpu_custom_call" | custom-call | flops 1000000 | bytes 1048576 | tf_op jit(solution)/shard_map/pallas_call | solution.py:28
  28.8 2.5 %collective-permute-start.4 = (f32[128,256]{1,0:T(8,128)S(1)}, f32[128,256]{1,0:T(8,128)S(1)}, u32[]{:S(2)}, u32[]{:S(2)}) collective-permute-start(f32[128,256]{1,0:T(8,128)S(1)} %get-tuple-element.94), channel_id=1, source_target_pairs={{0,1},{1,0},{2,3},{3,2},{4,5},{5,4},{6,7},{7,6},{8,9},{9,8},{10,11... | collective-permute-start | bytes 393224 | tf_op jit(solution)/shard_map/ppermute | solution.py:456
  33.6 1.2 %collective-permute-done.4.g0 = f32[128,256]{1,0:T(8,128)S(1)} collective-permute-done((f32[128,256]{1,0:T(8,128)S(1)}, f32[128,256]{1,0:T(8,128)S(1)}, u32[]{:S(2)}, u32[]{:S(2)}) %collective-permute-start.4) | collective-permute-done | bytes 131104 | tf_op jit(solution)/shard_map/ppermute | solution.py:456
  35.1 17.9 %all_to_all.20.gathered = f32[8,68,128]{2,1,0:T(8,128)S(1)} all-to-all(f32[8,68,128]{2,1,0:T(8,128)S(1)} %shard_map.82), channel_id=1, replica_groups=mesh['cluster'=4,'sub'=8] {'sub'}, dimensions={0} | all-to-all | bytes 557056 | tf_op jit(solution)/shard_map/all_to_all | solution.py:460
  53.3 1.7 %collective-permute-start.8 = (f32[40,256]{1,0:T(8,128)S(1)}, f32[40,256]{1,0:T(8,128)S(1)}, u32[]{:S(2)}, u32[]{:S(2)}) collective-permute-start(f32[40,256]{1,0:T(8,128)S(1)} %get-tuple-element.109.own), channel_id=1, source_target_pairs={{0,8},{8,0},{16,24},{24,16},{1,9},{9,1},{17,25},{25,17},{2,10},{10... | collective-permute-start | bytes 122888 | tf_op jit(solution)/shard_map/ppermute | solution.py:463
  55.0 0.9 collective-permute-done.8.first
  56.8 1.8 %shard_map.80 = (bf16[1024,160]{1,0:T(8,128)(2,1)S(1)}, bf16[1024,160]{1,0:T(8,128)(2,1)S(1)}) custom-call(bf16[1024,1024]{1,0:T(8,128)(2,1)S(1)} %get-tuple-element.82.c_hi, bf16[1024,1024]{1,0:T(8,128)(2,1)S(1)} %get-tuple-element.83.c_lo, bf16[1024,160]{1,0:T(8,128)(2,1)S(1)} %get-tuple-element.99.b_hi, bf16[1024,160]{1,0:T(8,128)(2,1)S(1)} %get-tuple-element.100.b_lo), custom_call_target="tpu_custom_call" | custom-call | flops 50000000 | bytes 1048576 | tf_op jit(solution)/shard_map/pallas_call | solution.py:28
  58.6 2.7 %shard_map.79 = (f32[1024,256]{1,0:T(8,128)S(1)}, f32[1024,256]{1,0:T(8,128)S(1)}, f32[1024,256]{1,0:T(8,128)S(1)}) custom-call(s32[8]{0:T(128)S(1)} %get-tuple-element.75.starts, f32[1024,256]{1,0:T(8,128)S(1)} %get-tuple-element.93.image, bf16[1024,1024]{1,0:T(8,128)(2,1)S(1)} %get-tuple-element.82.c_hi, bf16[1024,1024]{1,0:T(8,128)(2,1)S(1)} %get-tuple-element.83.c_lo, ...), custom_call_target="tpu_custom_call" | custom-call | flops 100000000 | bytes 1048576 | tf_op jit(solution)/shard_map/pallas_call | solution.py:28
  61.2 1.2 %shard_map.84 = (f32[1024,256]{1,0:T(8,128)S(1)}, f32[1024,256]{1,0:T(8,128)S(1)}, f32[8,256]{1,0:T(8,128)S(1)}, f32[128,256]{1,0:T(8,128)S(1)}, f32[128,256]{1,...) custom-call(s32[8]{0:T(128)S(1)} %get-tuple-element.75.starts, f32[1024,256]{1,0:T(8,128)S(1)} %get-tuple-element.93.image, ...), custom_call_target="tpu_custom_call" | custom-call | flops 1000000 | bytes 1048576 | tf_op jit(solution)/shard_map/pallas_call | solution.py:28
  64.5 1.6 %shard_map.86 = (f32[1024,256]{1,0:T(8,128)S(1)}, f32[1024,256]{1,0:T(8,128)S(1)}, f32[32,256]{1,0:T(8,128)S(1)}, f32[32,256]{1,0:T(8,128)S(1)}, f32[1024,256]{1...) custom-call(f32[8,256]{1,0:T(8,128)S(1)} %get-tuple-element.117.scal, ...), custom_call_target="tpu_custom_call" | custom-call | flops 1000000 | bytes 1048576 | tf_op jit(solution)/shard_map/pallas_call | solution.py:28
  66.1 2.2 %collective-permute-done.10.g0 = f32[128,256]{1,0:T(8,128)S(1)} collective-permute-done((f32[128,256]{1,0:T(8,128)S(1)}, f32[128,256]{1,0:T(8,128)S(1)}, u32[]{:S(2)}, u32[]{:S(2)}) %collective-permute-start.10) | collective-permute-done | bytes 131104 | tf_op jit(solution)/shard_map/ppermute | solution.py:456
  68.5 16.1 %all_to_all.21.gathered = f32[8,68,128]{2,1,0:T(8,128)S(1)} all-to-all(f32[8,68,128]{2,1,0:T(8,128)S(1)} %shard_map.87), channel_id=1, replica_groups=mesh['cluster'=4,'sub'=8] {'sub'}, dimensions={0} | all-to-all | bytes 557056 | tf_op jit(solution)/shard_map/all_to_all | solution.py:460
  84.8 1.2 %collective-permute-start.14 = (f32[40,256]{1,0:T(8,128)S(1)}, f32[40,256]{1,0:T(8,128)S(1)}, u32[]{:S(2)}, u32[]{:S(2)}) collective-permute-start(f32[40,256]{1,0:T(8,128)S(1)} %get-tuple-element.122.own), channel_id=1, source_target_pairs={{0,8},{8,0},{16,24},{24,16},{1,9},{9,1},{17,25},{25,17},{2,10},{10... | collective-permute-start | bytes 122888 | tf_op jit(solution)/shard_map/ppermute | solution.py:463
  86.0 0.9 collective-permute-done.14.first
  87.0 2.7 %shard_map.85 = (f32[1024,256]{1,0:T(8,128)S(1)}, f32[1024,256]{1,0:T(8,128)S(1)}, f32[1024,256]{1,0:T(8,128)S(1)}) custom-call(s32[8]{0:T(128)S(1)} %get-tuple-element.75.starts, f32[1024,256]{1,0:T(8,128)S(1)} %get-tuple-element.111.image, bf16[1024,1024]{1,0:T(8,128)(2,1)S(1)} %get-tuple-element.82.c_hi, bf16[1024,1024]{1,0:T(8,128)(2,1)S(1)} %get-tuple-element.83.c_lo, ...), custom_call_target="tpu_custom_call" | custom-call | flops 100000000 | bytes 1048576 | tf_op jit(solution)/shard_map/pallas_call | solution.py:28
  90.3 1.2 %shard_map.89 = (f32[1024,256]{1,0:T(8,128)S(1)}, f32[8,256]{1,0:T(8,128)S(1)}, f32[128,256]{1,0:T(8,128)S(1)}, f32[128,256]{1,0:T(8,128)S(1)}, f32[128,256]{1,0:T(8,128)S(1)}, /*index=5*/f32[128,256]{1,0:T(8,128)S(1)}) custom-call(s32[8]{0:T(128)S(1)} %get-tuple-element.75.starts, f32[1024,256]{1,0:T(8,128)S(1)} %get-tuple-element.111.image, ...), custom_call_target="tpu_custom_call" | custom-call | flops 1000000 | bytes 1048576 | tf_op jit(solution)/shard_map/pallas_call | solution.py:28
  93.8 1.3 %shard_map.90 = (f32[1024,256]{1,0:T(8,128)S(1)}, f32[32,256]{1,0:T(8,128)S(1)}, f32[1024,256]{1,0:T(8,128)S(1)}, f32[32,2,256]{2,1,0:T(2,128)S(1)}) custom-call(f32[8,256]{1,0:T(8,128)S(1)} %get-tuple-element.125.scal.scal1, f32[1024,256]{1,0:T(8,128)S(1)} %get-tuple-element.126.vee, f32[1024,256]{1,0:T(8,128)S(1)} %get-tuple-element.127.qtwice, ...), custom_call_target="tpu_custom_call" | custom-call | flops 1000000 | bytes 1048576 | tf_op jit(solution)/shard_map/pallas_call | solution.py:28
  95.2 14.9 %all_to_all.22.everyone = f32[32,2,256]{2,1,0:T(2,128)S(1)} all-to-all(f32[32,2,256]{2,1,0:T(2,128)S(1)} %get-tuple-element.138), channel_id=1, replica_groups=mesh['cluster'=4,'sub'=8] {'cluster','sub'}, dimensions={0} | all-to-all | bytes 131072 | tf_op jit(solution)/shard_map/all_to_all | solution.py:460
  110.2 2.8 %finish.1 = (f32[1024,256]{1,0:T(8,128)}, f32[1024,256]{1,0:T(8,128)}) custom-call(s32[8]{0:T(128)S(1)} %get-tuple-element.75.starts, f32[2,256]{1,0:T(2,128)S(1)} %shard_map.91.sums, f32[8,256]{1,0:T(8,128)S(1)} %get-tuple-element.117.scal.rest_0_.scal0, f32[8,256]{1,0:T(8,128)S(1)} %get-tuple-element.125.scal.scal1, ...), custom_call_target="tpu_custom_call" | custom-call | flops 1000000 | bytes 1048576 | tf_op jit(solution)/shard_map/finish/pallas_call | solution.py:594
  (45 shorter events, 11.5 us)
Async XLA Ops:
  3.0 17.1 %all-to-all-start = ((f32[8,32,256]{2,1,0:T(8,128)}), f32[8,32,256]{2,1,0:T(8,128)S(1)}, u32[]{:S(2)}, u32[]{:S(2)}) async-start(f32[8,32,256]{2,1,0:T(8,128)} %get-tuple-element.80), calls=%async_computation | async-start | bytes 524288 | tf_op jit(solution)/shard_map/all_to_all | solution.py:460
  10.3 11.5 %collective-permute-start = (f32[176,256]{1,0:T(8,128)S(1)}, f32[176,256]{1,0:T(8,128)S(1)}, u32[]{:S(2)}, u32[]{:S(2)}) collective-permute-start(f32[176,256]{1,0:T(8,128)S(1)} %get-tuple-element.78), channel_id=1, source_target_pairs={{0,1},{1,0},{2,3},{3,2},{4,5},{5,4},{6,7},{7,6},{8,9},{9,8},{10,11... | collective-permute-start | bytes 540680 | tf_op jit(solution)/shard_map/ppermute | solution.py:502
  12.3 9.5 %collective-permute-start.1 = (f32[176,256]{1,0:T(8,128)S(1)}, f32[176,256]{1,0:T(8,128)S(1)}, u32[]{:S(2)}, u32[]{:S(2)}) collective-permute-start(f32[176,256]{1,0:T(8,128)S(1)} %get-tuple-element.79), channel_id=1, source_target_pairs={{1,2},{2,1},{3,4},{4,3},{5,6},{6,5},{9,10},{10,9},{11,12},{12,11},... | collective-permute-start | bytes 540680 | tf_op jit(solution)/shard_map/ppermute | solution.py:502
  20.3 4.8 %collective-permute-start.2 = (f32[176,256]{1,0:T(8,128)S(1)}, f32[176,256]{1,0:T(8,128)S(1)}, u32[]{:S(2)}, u32[]{:S(2)}) collective-permute-start(f32[176,256]{1,0:T(8,128)S(1)} %get-tuple-element.91), channel_id=1, source_target_pairs={{0,8},{8,0},{16,24},{24,16},{1,9},{9,1},{17,25},{25,17},{2,10},{10... | collective-permute-start | bytes 540680 | tf_op jit(solution)/shard_map/ppermute | solution.py:511
  20.4 4.7 %collective-permute-start.3 = (f32[176,256]{1,0:T(8,128)S(1)}, f32[176,256]{1,0:T(8,128)S(1)}, u32[]{:S(2)}, u32[]{:S(2)}) collective-permute-start(f32[176,256]{1,0:T(8,128)S(1)} %get-tuple-element.92), channel_id=1, source_target_pairs={{8,16},{16,8},{9,17},{17,9},{10,18},{18,10},{11,19},{19,11},{12,20... | collective-permute-start | bytes 540680 | tf_op jit(solution)/shard_map/ppermute | solution.py:510
  28.8 6.1 %collective-permute-start.4 = (f32[128,256]{1,0:T(8,128)S(1)}, f32[128,256]{1,0:T(8,128)S(1)}, u32[]{:S(2)}, u32[]{:S(2)}) collective-permute-start(f32[128,256]{1,0:T(8,128)S(1)} %get-tuple-element.94), channel_id=1, source_target_pairs={{0,1},{1,0},{2,3},{3,2},{4,5},{5,4},{6,7},{7,6},{8,9},{9,8},{10,11... | collective-permute-start | bytes 393224 | tf_op jit(solution)/shard_map/ppermute | solution.py:456
  31.3 3.5 %collective-permute-start.5 = (f32[128,256]{1,0:T(8,128)S(1)}, f32[128,256]{1,0:T(8,128)S(1)}, u32[]{:S(2)}, u32[]{:S(2)}) collective-permute-start(f32[128,256]{1,0:T(8,128)S(1)} %get-tuple-element.95), channel_id=1, source_target_pairs={{1,2},{2,1},{3,4},{4,3},{5,6},{6,5},{9,10},{10,9},{11,12},{12,11},... | collective-permute-start | bytes 393224 | tf_op jit(solution)/shard_map/ppermute | solution.py:456
  32.0 2.9 %collective-permute-start.6 = (f32[128,256]{1,0:T(8,128)S(1)}, f32[128,256]{1,0:T(8,128)S(1)}, u32[]{:S(2)}, u32[]{:S(2)}) collective-permute-start(f32[128,256]{1,0:T(8,128)S(1)} %get-tuple-element.96), channel_id=1, source_target_pairs={{0,8},{8,0},{16,24},{24,16},{1,9},{9,1},{17,25},{25,17},{2,10},{10... | collective-permute-start | bytes 393224 | tf_op jit(solution)/shard_map/ppermute | solution.py:456
  32.4 2.5 %collective-permute-start.7 = (f32[128,256]{1,0:T(8,128)S(1)}, f32[128,256]{1,0:T(8,128)S(1)}, u32[]{:S(2)}, u32[]{:S(2)}) collective-permute-start(f32[128,256]{1,0:T(8,128)S(1)} %get-tuple-element.97), channel_id=1, source_target_pairs={{8,16},{16,8},{9,17},{17,9},{10,18},{18,10},{11,19},{19,11},{12,20... | collective-permute-start | bytes 393224 | tf_op jit(solution)/shard_map/ppermute | solution.py:456
  53.3 2.6 %collective-permute-start.8 = (f32[40,256]{1,0:T(8,128)S(1)}, f32[40,256]{1,0:T(8,128)S(1)}, u32[]{:S(2)}, u32[]{:S(2)}) collective-permute-start(f32[40,256]{1,0:T(8,128)S(1)} %get-tuple-element.109.own), channel_id=1, source_target_pairs={{0,8},{8,0},{16,24},{24,16},{1,9},{9,1},{17,25},{25,17},{2,10},{10... | collective-permute-start | bytes 122888 | tf_op jit(solution)/shard_map/ppermute | solution.py:463
  55.9 5.3 %collective-permute-start.9 = (f32[40,256]{1,0:T(8,128)S(1)}, f32[40,256]{1,0:T(8,128)S(1)}, u32[]{:S(2)}, u32[]{:S(2)}) collective-permute-start(f32[40,256]{1,0:T(8,128)S(1)} %pad_maximum_fusion), channel_id=1, source_target_pairs={{8,16},{16,8},{24,0},{0,24},{9,17},{17,9},{25,1},{1,25},{10,18},{1... | collective-permute-start | bytes 122888 | tf_op jit(solution)/shard_map/ppermute | solution.py:467
  62.4 5.9 %collective-permute-start.10 = (f32[128,256]{1,0:T(8,128)S(1)}, f32[128,256]{1,0:T(8,128)S(1)}, u32[]{:S(2)}, u32[]{:S(2)}) collective-permute-start(f32[128,256]{1,0:T(8,128)S(1)} %get-tuple-element.112), channel_id=1, source_target_pairs={{0,1},{1,0},{2,3},{3,2},{4,5},{5,4},{6,7},{7,6},{8,9},{9,8},{10,11... | collective-permute-start | bytes 393224 | tf_op jit(solution)/shard_map/ppermute | solution.py:456
  62.9 5.3 %collective-permute-start.11 = (f32[128,256]{1,0:T(8,128)S(1)}, f32[128,256]{1,0:T(8,128)S(1)}, u32[]{:S(2)}, u32[]{:S(2)}) collective-permute-start(f32[128,256]{1,0:T(8,128)S(1)} %get-tuple-element.113), channel_id=1, source_target_pairs={{1,2},{2,1},{3,4},{4,3},{5,6},{6,5},{9,10},{10,9},{11,12},{12,11},... | collective-permute-start | bytes 393224 | tf_op jit(solution)/shard_map/ppermute | solution.py:456
  63.6 4.7 %collective-permute-start.12 = (f32[128,256]{1,0:T(8,128)S(1)}, f32[128,256]{1,0:T(8,128)S(1)}, u32[]{:S(2)}, u32[]{:S(2)}) collective-permute-start(f32[128,256]{1,0:T(8,128)S(1)} %get-tuple-element.114), channel_id=1, source_target_pairs={{0,8},{8,0},{16,24},{24,16},{1,9},{9,1},{17,25},{25,17},{2,10},{10... | collective-permute-start | bytes 393224 | tf_op jit(solution)/shard_map/ppermute | solution.py:456
  63.8 4.5 %collective-permute-start.13 = (f32[128,256]{1,0:T(8,128)S(1)}, f32[128,256]{1,0:T(8,128)S(1)}, u32[]{:S(2)}, u32[]{:S(2)}) collective-permute-start(f32[128,256]{1,0:T(8,128)S(1)} %get-tuple-element.115), channel_id=1, source_target_pairs={{8,16},{16,8},{9,17},{17,9},{10,18},{18,10},{11,19},{19,11},{12,20... | collective-permute-start | bytes 393224 | tf_op jit(solution)/shard_map/ppermute | solution.py:456
  84.8 2.0 %collective-permute-start.14 = (f32[40,256]{1,0:T(8,128)S(1)}, f32[40,256]{1,0:T(8,128)S(1)}, u32[]{:S(2)}, u32[]{:S(2)}) collective-permute-start(f32[40,256]{1,0:T(8,128)S(1)} %get-tuple-element.122.own), channel_id=1, source_target_pairs={{0,8},{8,0},{16,24},{24,16},{1,9},{9,1},{17,25},{25,17},{2,10},{10... | collective-permute-start | bytes 122888 | tf_op jit(solution)/shard_map/ppermute | solution.py:463
  86.9 3.4 %collective-permute-start.15 = (f32[40,256]{1,0:T(8,128)S(1)}, f32[40,256]{1,0:T(8,128)S(1)}, u32[]{:S(2)}, u32[]{:S(2)}) collective-permute-start(f32[40,256]{1,0:T(8,128)S(1)} %pad_maximum_fusion.1), channel_id=1, source_target_pairs={{8,16},{16,8},{24,0},{0,24},{9,17},{17,9},{25,1},{1,25},{10,18},{1... | collective-permute-start | bytes 122888 | tf_op jit(solution)/shard_map/ppermute | solution.py:467
  91.5 18.6 %collective-permute-start.16 = (f32[128,256]{1,0:T(8,128)S(1)}, f32[128,256]{1,0:T(8,128)S(1)}, u32[]{:S(2)}, u32[]{:S(2)}) collective-permute-start(f32[128,256]{1,0:T(8,128)S(1)} %get-tuple-element.142), channel_id=1, source_target_pairs={{0,1},{1,0},{2,3},{3,2},{4,5},{5,4},{6,7},{7,6},{8,9},{9,8},{10,11... | collective-permute-start | bytes 393224 | tf_op jit(solution)/shard_map/ppermute | solution.py:456
  92.3 17.8 %collective-permute-start.17 = (f32[128,256]{1,0:T(8,128)S(1)}, f32[128,256]{1,0:T(8,128)S(1)}, u32[]{:S(2)}, u32[]{:S(2)}) collective-permute-start(f32[128,256]{1,0:T(8,128)S(1)} %get-tuple-element.143), channel_id=1, source_target_pairs={{1,2},{2,1},{3,4},{4,3},{5,6},{6,5},{9,10},{10,9},{11,12},{12,11},... | collective-permute-start | bytes 393224 | tf_op jit(solution)/shard_map/ppermute | solution.py:456
  93.0 17.2 %collective-permute-start.18 = (f32[128,256]{1,0:T(8,128)S(1)}, f32[128,256]{1,0:T(8,128)S(1)}, u32[]{:S(2)}, u32[]{:S(2)}) collective-permute-start(f32[128,256]{1,0:T(8,128)S(1)} %get-tuple-element.144), channel_id=1, source_target_pairs={{0,8},{8,0},{16,24},{24,16},{1,9},{9,1},{17,25},{25,17},{2,10},{10... | collective-permute-start | bytes 393224 | tf_op jit(solution)/shard_map/ppermute | solution.py:456
  93.2 17.0 %collective-permute-start.19 = (f32[128,256]{1,0:T(8,128)S(1)}, f32[128,256]{1,0:T(8,128)S(1)}, u32[]{:S(2)}, u32[]{:S(2)}) collective-permute-start(f32[128,256]{1,0:T(8,128)S(1)} %get-tuple-element.145), channel_id=1, source_target_pairs={{8,16},{16,8},{9,17},{17,9},{10,18},{18,10},{11,19},{19,11},{12,20... | collective-permute-start | bytes 393224 | tf_op jit(solution)/shard_map/ppermute | solution.py:456

commit v6 on v5

--- a/solution.py
+++ b/solution.py
@@ -460,12 +460,13 @@
         return lax.all_to_all(blocks, axis, 0, 0, tiled=False)
 
     def mirror(ymom):
+        if doubled:
+            second = lax.ppermute(ymom, "cluster", pair_list(nclus, 1, True))
+            sums = ymom[nmodes:] + second[nmodes:]
+            both = jnp.concatenate([ymom[:nmodes], sums], 0)
+            first = lax.ppermute(both, "cluster", pair_list(nclus, 0))
+            return first, second
         first = lax.ppermute(ymom, "cluster", pair_list(nclus, 0))
-        if doubled:
-            sums = ymom[nmodes:] + first[nmodes:]
-            both = jnp.concatenate([ymom[:nmodes], sums], 0)
-            second = lax.ppermute(both, "cluster", pair_list(nclus, 1, True))
-            return first, second
         mine = ymom[nmodes:]
         rest = lax.psum(mine, "cluster") - mine
         second = lax.ppermute(ymom[:nmodes], "cluster", pair_list(nclus, 1))

time: 114 us -> 117 us (1.026)
  waiting for transfers between devices: 13.7 us -> 17.6 us
    ppermute x4, waiting for transfers between devices: 2.4 us -> 6.81 us  [the longest x2 6.8 us: mirror(): second = lax.ppermute(ymom, 'cluster', pair_list(nclus, 1, True))]
  transfers between devices with their start and end apart: 21 -> 21, of which waited for: 7 -> 6; matrix products, arithmetic and copies ran while one was open for 0% -> 0% of each run, Pallas kernels for 13% -> 12%
where the time goes in v6:
time: 117 us
  blocking collectives  49.3 us (42%)
  Pallas kernels  26.4 us (23%)
  starting transfers between devices  22.4 us (19%)
  waiting for transfers between devices  17.6 us (15%)
    all_to_all x3, blocking collectives, gather(): return lax.all_to_all(blocks, axis, 0, 0, tiled=False)  49.3 us
    pallas_call x15, Pallas kernels, call(): pl.pallas_call(body, out_shape=outs, in_specs=[SM if at in smem_in else V...  17.9 us
    ppermute x12, starting transfers between devices, exchange(): got[at] = lax.ppermute(messages[at], links[at][0], links[at][1])  8.58 us
    all_to_all x1, starting transfers between devices, gather(): return lax.all_to_all(blocks, axis, 0, 0, tiled=False)  7.29 us
    all_to_all x1, waiting for transfers between devices, gather(): return lax.all_to_all(blocks, axis, 0, 0, tiled=False)  7.12 us
    ppermute x2, waiting for transfers between devices, mirror(): second = lax.ppermute(ymom, 'cluster', pair_list(nclus, 1, True))  6.8 us
    pallas_call x1, Pallas kernels, shards(): pl.pallas_call(setup_body, out_shape=[sds(2 * nmodes, width), mapping, ma...  3.33 us
    ppermute x2, starting transfers between devices, mirror(): first = lax.ppermute(both, 'cluster', pair_list(nclus, 0))  2.95 us
  transfers between devices with their start and end apart: 21, of which 6 were waited for; matrix products, arithmetic and copies ran while one was open for 0% of the time, Pallas kernels for 12%

profile of v6, /device:TPU:0, one launch (start us, length us, event | category | flops | bytes accessed | tf_op | source)
XLA Modules:
  0.0 116.7 jit_solution(17737460735249689812)
XLA Ops:
  0.6 2.3 %start.1 = (f32[176,256]{1,0:T(8,128)S(1)}, f32[176,256]{1,0:T(8,128)S(1)}, f32[144,256]{1,0:T(8,128)S(1)}, f32[144,256]{1,0:T(8,128)S(1)}, s32[8]{0:T(128)S(1)}...) custom-call(s32[4,4,8]{2,1,0:T(4,128)} %bitcast.15, ...), custom_call_target="tpu_custom_call" | custom-call | tf_op jit(solution)/shard_map/start/pallas_call | solution.py:482
  3.0 7.3 %all-to-all-start = ((f32[8,32,256]{2,1,0:T(8,128)}), f32[8,32,256]{2,1,0:T(8,128)S(1)}, u32[]{:S(2)}, u32[]{:S(2)}) async-start(f32[8,32,256]{2,1,0:T(8,128)} %get-tuple-element.80), calls=%async_computation | async-start | bytes 524288 | tf_op jit(solution)/shard_map/all_to_all | solution.py:460
  10.3 2.0 %collective-permute-start = (f32[176,256]{1,0:T(8,128)S(1)}, f32[176,256]{1,0:T(8,128)S(1)}, u32[]{:S(2)}, u32[]{:S(2)}) collective-permute-start(f32[176,256]{1,0:T(8,128)S(1)} %get-tuple-element.78), channel_id=1, source_target_pairs={{0,1},{1,0},{2,3},{3,2},{4,5},{5,4},{6,7},{7,6},{8,9},{9,8},{10,11... | collective-permute-start | bytes 540680 | tf_op jit(solution)/shard_map/ppermute | solution.py:503
  12.9 7.1 %all-to-all-done = f32[8,32,256]{2,1,0:T(8,128)S(1)} async-done(((f32[8,32,256]{2,1,0:T(8,128)}), f32[8,32,256]{2,1,0:T(8,128)S(1)}, u32[]{:S(2)}, u32[]{:S(2)}) %all-to-all-start) | async-done | bytes 262176 | tf_op jit(solution)/shard_map/all_to_all | solution.py:460
  21.7 3.3 %setup.1 = (f32[64,256]{1,0:T(8,128)S(1)}, bf16[1024,160]{1,0:T(8,128)(2,1)S(1)}, bf16[1024,160]{1,0:T(8,128)(2,1)S(1)}, bf16[32,1024]{1,0:T(8,128)(2,1)S(1)}, b...) custom-call(s32[8]{0:T(128)S(1)} %get-tuple-element.75.starts, ...), custom_call_target="tpu_custom_call" | custom-call | flops 100000000 | bytes 4194304 | tf_op jit(solution)/shard_map/setup/pallas_call | solution.py:518
  25.1 3.7 %shard_map.78 = (f32[1024,256]{1,0:T(8,128)S(1)}, f32[1024,256]{1,0:T(8,128)S(1)}, bf16[1024,160]{1,0:T(8,128)(2,1)S(1)}, bf16[1024,160]{1,0:T(8,128)(2,1)S(1)},...) custom-call(s32[8]{0:T(128)S(1)} %get-tuple-element.75.starts, ...), custom_call_target="tpu_custom_call" | custom-call | flops 1000000 | bytes 1048576 | tf_op jit(solution)/shard_map/pallas_call | solution.py:28
  28.8 2.5 %collective-permute-start.4 = (f32[128,256]{1,0:T(8,128)S(1)}, f32[128,256]{1,0:T(8,128)S(1)}, u32[]{:S(2)}, u32[]{:S(2)}) collective-permute-start(f32[128,256]{1,0:T(8,128)S(1)} %get-tuple-element.94), channel_id=1, source_target_pairs={{0,1},{1,0},{2,3},{3,2},{4,5},{5,4},{6,7},{7,6},{8,9},{9,8},{10,11... | collective-permute-start | bytes 393224 | tf_op jit(solution)/shard_map/ppermute | solution.py:456
  33.6 1.2 %collective-permute-done.4.g0 = f32[128,256]{1,0:T(8,128)S(1)} collective-permute-done((f32[128,256]{1,0:T(8,128)S(1)}, f32[128,256]{1,0:T(8,128)S(1)}, u32[]{:S(2)}, u32[]{:S(2)}) %collective-permute-start.4) | collective-permute-done | bytes 131104 | tf_op jit(solution)/shard_map/ppermute | solution.py:456
  35.1 17.9 %all_to_all.20.gathered = f32[8,68,128]{2,1,0:T(8,128)S(1)} all-to-all(f32[8,68,128]{2,1,0:T(8,128)S(1)} %shard_map.82), channel_id=1, replica_groups=mesh['cluster'=4,'sub'=8] {'sub'}, dimensions={0} | all-to-all | bytes 557056 | tf_op jit(solution)/shard_map/all_to_all | solution.py:460
  53.4 3.4 %collective-permute-done.8.second = f32[40,256]{1,0:T(8,128)S(1)} collective-permute-done((f32[40,256]{1,0:T(8,128)S(1)}, f32[40,256]{1,0:T(8,128)S(1)}, u32[]{:S(2)}, u32[]{:S(2)}) %collective-permute-start.8) | collective-permute-done | bytes 40992 | tf_op jit(solution)/shard_map/ppermute | solution.py:464
  56.8 1.7 %collective-permute-start.9 = (f32[40,256]{1,0:T(8,128)S(1)}, f32[40,256]{1,0:T(8,128)S(1)}, u32[]{:S(2)}, u32[]{:S(2)}) collective-permute-start(f32[40,256]{1,0:T(8,128)S(1)} %pad_maximum_fusion), channel_id=1, source_target_pairs={{0,8},{8,0},{16,24},{24,16},{1,9},{9,1},{17,25},{25,17},{2,10},{10... | collective-permute-start | bytes 122888 | tf_op jit(solution)/shard_map/ppermute | solution.py:467
  58.5 1.8 %shard_map.80 = (bf16[1024,160]{1,0:T(8,128)(2,1)S(1)}, bf16[1024,160]{1,0:T(8,128)(2,1)S(1)}) custom-call(bf16[1024,1024]{1,0:T(8,128)(2,1)S(1)} %get-tuple-element.82.c_hi, bf16[1024,1024]{1,0:T(8,128)(2,1)S(1)} %get-tuple-element.83.c_lo, bf16[1024,160]{1,0:T(8,128)(2,1)S(1)} %get-tuple-element.99.b_hi, bf16[1024,160]{1,0:T(8,128)(2,1)S(1)} %get-tuple-element.100.b_lo), custom_call_target="tpu_custom_call" | custom-call | flops 50000000 | bytes 1048576 | tf_op jit(solution)/shard_map/pallas_call | solution.py:28
  60.3 2.7 %shard_map.79 = (f32[1024,256]{1,0:T(8,128)S(1)}, f32[1024,256]{1,0:T(8,128)S(1)}, f32[1024,256]{1,0:T(8,128)S(1)}) custom-call(s32[8]{0:T(128)S(1)} %get-tuple-element.75.starts, f32[1024,256]{1,0:T(8,128)S(1)} %get-tuple-element.93.image, bf16[1024,1024]{1,0:T(8,128)(2,1)S(1)} %get-tuple-element.82.c_hi, bf16[1024,1024]{1,0:T(8,128)(2,1)S(1)} %get-tuple-element.83.c_lo, ...), custom_call_target="tpu_custom_call" | custom-call | flops 100000000 | bytes 1048576 | tf_op jit(solution)/shard_map/pallas_call | solution.py:28
  63.0 1.2 shard_map.84
  66.4 1.6 %shard_map.86 = (f32[1024,256]{1,0:T(8,128)S(1)}, f32[1024,256]{1,0:T(8,128)S(1)}, f32[32,256]{1,0:T(8,128)S(1)}, f32[32,256]{1,0:T(8,128)S(1)}, f32[1024,256]{1...) custom-call(f32[8,256]{1,0:T(8,128)S(1)} %get-tuple-element.117.scal, ...), custom_call_target="tpu_custom_call" | custom-call | flops 1000000 | bytes 1048576 | tf_op jit(solution)/shard_map/pallas_call | solution.py:28
  68.0 1.7 %collective-permute-done.10.g0 = f32[128,256]{1,0:T(8,128)S(1)} collective-permute-done((f32[128,256]{1,0:T(8,128)S(1)}, f32[128,256]{1,0:T(8,128)S(1)}, u32[]{:S(2)}, u32[]{:S(2)}) %collective-permute-start.10) | collective-permute-done | bytes 131104 | tf_op jit(solution)/shard_map/ppermute | solution.py:456
  69.9 16.5 %all_to_all.21.gathered = f32[8,68,128]{2,1,0:T(8,128)S(1)} all-to-all(f32[8,68,128]{2,1,0:T(8,128)S(1)} %shard_map.87), channel_id=1, replica_groups=mesh['cluster'=4,'sub'=8] {'sub'}, dimensions={0} | all-to-all | bytes 557056 | tf_op jit(solution)/shard_map/all_to_all | solution.py:460
  86.8 3.4 %collective-permute-done.14.second = f32[40,256]{1,0:T(8,128)S(1)} collective-permute-done((f32[40,256]{1,0:T(8,128)S(1)}, f32[40,256]{1,0:T(8,128)S(1)}, u32[]{:S(2)}, u32[]{:S(2)}) %collective-permute-start.14) | collective-permute-done | bytes 40992 | tf_op jit(solution)/shard_map/ppermute | solution.py:464
  90.2 1.2 %collective-permute-start.15 = (f32[40,256]{1,0:T(8,128)S(1)}, f32[40,256]{1,0:T(8,128)S(1)}, u32[]{:S(2)}, u32[]{:S(2)}) collective-permute-start(f32[40,256]{1,0:T(8,128)S(1)} %pad_maximum_fusion.1), channel_id=1, source_target_pairs={{0,8},{8,0},{16,24},{24,16},{1,9},{9,1},{17,25},{25,17},{2,10},{10... | collective-permute-start | bytes 122888 | tf_op jit(solution)/shard_map/ppermute | solution.py:467
  91.4 2.7 %shard_map.85 = (f32[1024,256]{1,0:T(8,128)S(1)}, f32[1024,256]{1,0:T(8,128)S(1)}, f32[1024,256]{1,0:T(8,128)S(1)}) custom-call(s32[8]{0:T(128)S(1)} %get-tuple-element.75.starts, f32[1024,256]{1,0:T(8,128)S(1)} %get-tuple-element.111.image, bf16[1024,1024]{1,0:T(8,128)(2,1)S(1)} %get-tuple-element.82.c_hi, bf16[1024,1024]{1,0:T(8,128)(2,1)S(1)} %get-tuple-element.83.c_lo, ...), custom_call_target="tpu_custom_call" | custom-call | flops 100000000 | bytes 1048576 | tf_op jit(solution)/shard_map/pallas_call | solution.py:28
  94.1 1.2 %shard_map.89 = (f32[1024,256]{1,0:T(8,128)S(1)}, f32[8,256]{1,0:T(8,128)S(1)}, f32[128,256]{1,0:T(8,128)S(1)}, f32[128,256]{1,0:T(8,128)S(1)}, f32[128,256]{1,0:T(8,128)S(1)}, /*index=5*/f32[128,256]{1,0:T(8,128)S(1)}) custom-call(s32[8]{0:T(128)S(1)} %get-tuple-element.75.starts, f32[1024,256]{1,0:T(8,128)S(1)} %get-tuple-element.111.image, ...), custom_call_target="tpu_custom_call" | custom-call | flops 1000000 | bytes 1048576 | tf_op jit(solution)/shard_map/pallas_call | solution.py:28
  97.5 1.3 %shard_map.90 = (f32[1024,256]{1,0:T(8,128)S(1)}, f32[32,256]{1,0:T(8,128)S(1)}, f32[1024,256]{1,0:T(8,128)S(1)}, f32[32,2,256]{2,1,0:T(2,128)S(1)}) custom-call(f32[8,256]{1,0:T(8,128)S(1)} %get-tuple-element.125.scal.scal1, f32[1024,256]{1,0:T(8,128)S(1)} %get-tuple-element.126.vee, f32[1024,256]{1,0:T(8,128)S(1)} %get-tuple-element.127.qtwice, ...), custom_call_target="tpu_custom_call" | custom-call | flops 1000000 | bytes 1048576 | tf_op jit(solution)/shard_map/pallas_call | solution.py:28
  98.9 14.8 %all_to_all.22.everyone = f32[32,2,256]{2,1,0:T(2,128)S(1)} all-to-all(f32[32,2,256]{2,1,0:T(2,128)S(1)} %get-tuple-element.138), channel_id=1, replica_groups=mesh['cluster'=4,'sub'=8] {'cluster','sub'}, dimensions={0} | all-to-all | bytes 131072 | tf_op jit(solution)/shard_map/all_to_all | solution.py:460
  113.7 2.8 %finish.1 = (f32[1024,256]{1,0:T(8,128)}, f32[1024,256]{1,0:T(8,128)}) custom-call(s32[8]{0:T(128)S(1)} %get-tuple-element.75.starts, f32[2,256]{1,0:T(2,128)S(1)} %shard_map.91.sums, f32[8,256]{1,0:T(8,128)S(1)} %get-tuple-element.117.scal.rest_0_.scal0, f32[8,256]{1,0:T(8,128)S(1)} %get-tuple-element.125.scal.scal1, ...), custom_call_target="tpu_custom_call" | custom-call | flops 1000000 | bytes 1048576 | tf_op jit(solution)/shard_map/finish/pallas_call | solution.py:595
  (45 shorter events, 10.1 us)
Async XLA Ops:
  3.0 17.1 %all-to-all-start = ((f32[8,32,256]{2,1,0:T(8,128)}), f32[8,32,256]{2,1,0:T(8,128)S(1)}, u32[]{:S(2)}, u32[]{:S(2)}) async-start(f32[8,32,256]{2,1,0:T(8,128)} %get-tuple-element.80), calls=%async_computation | async-start | bytes 524288 | tf_op jit(solution)/shard_map/all_to_all | solution.py:460
  10.3 11.5 %collective-permute-start = (f32[176,256]{1,0:T(8,128)S(1)}, f32[176,256]{1,0:T(8,128)S(1)}, u32[]{:S(2)}, u32[]{:S(2)}) collective-permute-start(f32[176,256]{1,0:T(8,128)S(1)} %get-tuple-element.78), channel_id=1, source_target_pairs={{0,1},{1,0},{2,3},{3,2},{4,5},{5,4},{6,7},{7,6},{8,9},{9,8},{10,11... | collective-permute-start | bytes 540680 | tf_op jit(solution)/shard_map/ppermute | solution.py:503
  12.3 9.5 %collective-permute-start.1 = (f32[176,256]{1,0:T(8,128)S(1)}, f32[176,256]{1,0:T(8,128)S(1)}, u32[]{:S(2)}, u32[]{:S(2)}) collective-permute-start(f32[176,256]{1,0:T(8,128)S(1)} %get-tuple-element.79), channel_id=1, source_target_pairs={{1,2},{2,1},{3,4},{4,3},{5,6},{6,5},{9,10},{10,9},{11,12},{12,11},... | collective-permute-start | bytes 540680 | tf_op jit(solution)/shard_map/ppermute | solution.py:503
  20.3 4.8 %collective-permute-start.2 = (f32[176,256]{1,0:T(8,128)S(1)}, f32[176,256]{1,0:T(8,128)S(1)}, u32[]{:S(2)}, u32[]{:S(2)}) collective-permute-start(f32[176,256]{1,0:T(8,128)S(1)} %get-tuple-element.91), channel_id=1, source_target_pairs={{0,8},{8,0},{16,24},{24,16},{1,9},{9,1},{17,25},{25,17},{2,10},{10... | collective-permute-start | bytes 540680 | tf_op jit(solution)/shard_map/ppermute | solution.py:512
  20.4 4.7 %collective-permute-start.3 = (f32[176,256]{1,0:T(8,128)S(1)}, f32[176,256]{1,0:T(8,128)S(1)}, u32[]{:S(2)}, u32[]{:S(2)}) collective-permute-start(f32[176,256]{1,0:T(8,128)S(1)} %get-tuple-element.92), channel_id=1, source_target_pairs={{8,16},{16,8},{9,17},{17,9},{10,18},{18,10},{11,19},{19,11},{12,20... | collective-permute-start | bytes 540680 | tf_op jit(solution)/shard_map/ppermute | solution.py:511
  28.8 6.1 %collective-permute-start.4 = (f32[128,256]{1,0:T(8,128)S(1)}, f32[128,256]{1,0:T(8,128)S(1)}, u32[]{:S(2)}, u32[]{:S(2)}) collective-permute-start(f32[128,256]{1,0:T(8,128)S(1)} %get-tuple-element.94), channel_id=1, source_target_pairs={{0,1},{1,0},{2,3},{3,2},{4,5},{5,4},{6,7},{7,6},{8,9},{9,8},{10,11... | collective-permute-start | bytes 393224 | tf_op jit(solution)/shard_map/ppermute | solution.py:456
  31.3 3.5 %collective-permute-start.5 = (f32[128,256]{1,0:T(8,128)S(1)}, f32[128,256]{1,0:T(8,128)S(1)}, u32[]{:S(2)}, u32[]{:S(2)}) collective-permute-start(f32[128,256]{1,0:T(8,128)S(1)} %get-tuple-element.95), channel_id=1, source_target_pairs={{1,2},{2,1},{3,4},{4,3},{5,6},{6,5},{9,10},{10,9},{11,12},{12,11},... | collective-permute-start | bytes 393224 | tf_op jit(solution)/shard_map/ppermute | solution.py:456
  32.0 2.9 %collective-permute-start.6 = (f32[128,256]{1,0:T(8,128)S(1)}, f32[128,256]{1,0:T(8,128)S(1)}, u32[]{:S(2)}, u32[]{:S(2)}) collective-permute-start(f32[128,256]{1,0:T(8,128)S(1)} %get-tuple-element.96), channel_id=1, source_target_pairs={{0,8},{8,0},{16,24},{24,16},{1,9},{9,1},{17,25},{25,17},{2,10},{10... | collective-permute-start | bytes 393224 | tf_op jit(solution)/shard_map/ppermute | solution.py:456
  32.4 2.5 %collective-permute-start.7 = (f32[128,256]{1,0:T(8,128)S(1)}, f32[128,256]{1,0:T(8,128)S(1)}, u32[]{:S(2)}, u32[]{:S(2)}) collective-permute-start(f32[128,256]{1,0:T(8,128)S(1)} %get-tuple-element.97), channel_id=1, source_target_pairs={{8,16},{16,8},{9,17},{17,9},{10,18},{18,10},{11,19},{19,11},{12,20... | collective-permute-start | bytes 393224 | tf_op jit(solution)/shard_map/ppermute | solution.py:456
  53.3 3.5 %collective-permute-start.8 = (f32[40,256]{1,0:T(8,128)S(1)}, f32[40,256]{1,0:T(8,128)S(1)}, u32[]{:S(2)}, u32[]{:S(2)}) collective-permute-start(f32[40,256]{1,0:T(8,128)S(1)} %get-tuple-element.109.own), channel_id=1, source_target_pairs={{8,16},{16,8},{24,0},{0,24},{9,17},{17,9},{25,1},{1,25},{10,18},{1... | collective-permute-start | bytes 122888 | tf_op jit(solution)/shard_map/ppermute | solution.py:464
  56.8 6.2 %collective-permute-start.9 = (f32[40,256]{1,0:T(8,128)S(1)}, f32[40,256]{1,0:T(8,128)S(1)}, u32[]{:S(2)}, u32[]{:S(2)}) collective-permute-start(f32[40,256]{1,0:T(8,128)S(1)} %pad_maximum_fusion), channel_id=1, source_target_pairs={{0,8},{8,0},{16,24},{24,16},{1,9},{9,1},{17,25},{25,17},{2,10},{10... | collective-permute-start | bytes 122888 | tf_op jit(solution)/shard_map/ppermute | solution.py:467
  64.2 5.5 %collective-permute-start.10 = (f32[128,256]{1,0:T(8,128)S(1)}, f32[128,256]{1,0:T(8,128)S(1)}, u32[]{:S(2)}, u32[]{:S(2)}) collective-permute-start(f32[128,256]{1,0:T(8,128)S(1)} %get-tuple-element.112), channel_id=1, source_target_pairs={{0,1},{1,0},{2,3},{3,2},{4,5},{5,4},{6,7},{7,6},{8,9},{9,8},{10,11... | collective-permute-start | bytes 393224 | tf_op jit(solution)/shard_map/ppermute | solution.py:456
  64.9 4.7 %collective-permute-start.11 = (f32[128,256]{1,0:T(8,128)S(1)}, f32[128,256]{1,0:T(8,128)S(1)}, u32[]{:S(2)}, u32[]{:S(2)}) collective-permute-start(f32[128,256]{1,0:T(8,128)S(1)} %get-tuple-element.113), channel_id=1, source_target_pairs={{1,2},{2,1},{3,4},{4,3},{5,6},{6,5},{9,10},{10,9},{11,12},{12,11},... | collective-permute-start | bytes 393224 | tf_op jit(solution)/shard_map/ppermute | solution.py:456
  65.6 4.1 %collective-permute-start.12 = (f32[128,256]{1,0:T(8,128)S(1)}, f32[128,256]{1,0:T(8,128)S(1)}, u32[]{:S(2)}, u32[]{:S(2)}) collective-permute-start(f32[128,256]{1,0:T(8,128)S(1)} %get-tuple-element.114), channel_id=1, source_target_pairs={{0,8},{8,0},{16,24},{24,16},{1,9},{9,1},{17,25},{25,17},{2,10},{10... | collective-permute-start | bytes 393224 | tf_op jit(solution)/shard_map/ppermute | solution.py:456
  65.7 4.0 %collective-permute-start.13 = (f32[128,256]{1,0:T(8,128)S(1)}, f32[128,256]{1,0:T(8,128)S(1)}, u32[]{:S(2)}, u32[]{:S(2)}) collective-permute-start(f32[128,256]{1,0:T(8,128)S(1)} %get-tuple-element.115), channel_id=1, source_target_pairs={{8,16},{16,8},{9,17},{17,9},{10,18},{18,10},{11,19},{19,11},{12,20... | collective-permute-start | bytes 393224 | tf_op jit(solution)/shard_map/ppermute | solution.py:456
  86.7 3.5 %collective-permute-start.14 = (f32[40,256]{1,0:T(8,128)S(1)}, f32[40,256]{1,0:T(8,128)S(1)}, u32[]{:S(2)}, u32[]{:S(2)}) collective-permute-start(f32[40,256]{1,0:T(8,128)S(1)} %get-tuple-element.122.own), channel_id=1, source_target_pairs={{8,16},{16,8},{24,0},{0,24},{9,17},{17,9},{25,1},{1,25},{10,18},{1... | collective-permute-start | bytes 122888 | tf_op jit(solution)/shard_map/ppermute | solution.py:464
  90.2 3.9 %collective-permute-start.15 = (f32[40,256]{1,0:T(8,128)S(1)}, f32[40,256]{1,0:T(8,128)S(1)}, u32[]{:S(2)}, u32[]{:S(2)}) collective-permute-start(f32[40,256]{1,0:T(8,128)S(1)} %pad_maximum_fusion.1), channel_id=1, source_target_pairs={{0,8},{8,0},{16,24},{24,16},{1,9},{9,1},{17,25},{25,17},{2,10},{10... | collective-permute-start | bytes 122888 | tf_op jit(solution)/shard_map/ppermute | solution.py:467
  95.4 18.3 %collective-permute-start.16 = (f32[128,256]{1,0:T(8,128)S(1)}, f32[128,256]{1,0:T(8,128)S(1)}, u32[]{:S(2)}, u32[]{:S(2)}) collective-permute-start(f32[128,256]{1,0:T(8,128)S(1)} %get-tuple-element.142), channel_id=1, source_target_pairs={{0,1},{1,0},{2,3},{3,2},{4,5},{5,4},{6,7},{7,6},{8,9},{9,8},{10,11... | collective-permute-start | bytes 393224 | tf_op jit(solution)/shard_map/ppermute | solution.py:456
  96.1 17.6 %collective-permute-start.17 = (f32[128,256]{1,0:T(8,128)S(1)}, f32[128,256]{1,0:T(8,128)S(1)}, u32[]{:S(2)}, u32[]{:S(2)}) collective-permute-start(f32[128,256]{1,0:T(8,128)S(1)} %get-tuple-element.143), channel_id=1, source_target_pairs={{1,2},{2,1},{3,4},{4,3},{5,6},{6,5},{9,10},{10,9},{11,12},{12,11},... | collective-permute-start | bytes 393224 | tf_op jit(solution)/shard_map/ppermute | solution.py:456
  96.8 16.9 %collective-permute-start.18 = (f32[128,256]{1,0:T(8,128)S(1)}, f32[128,256]{1,0:T(8,128)S(1)}, u32[]{:S(2)}, u32[]{:S(2)}) collective-permute-start(f32[128,256]{1,0:T(8,128)S(1)} %get-tuple-element.144), channel_id=1, source_target_pairs={{0,8},{8,0},{16,24},{24,16},{1,9},{9,1},{17,25},{25,17},{2,10},{10... | collective-permute-start | bytes 393224 | tf_op jit(solution)/shard_map/ppermute | solution.py:456
  96.9 16.9 %collective-permute-start.19 = (f32[128,256]{1,0:T(8,128)S(1)}, f32[128,256]{1,0:T(8,128)S(1)}, u32[]{:S(2)}, u32[]{:S(2)}) collective-permute-start(f32[128,256]{1,0:T(8,128)S(1)} %get-tuple-element.145), channel_id=1, source_target_pairs={{8,16},{16,8},{9,17},{17,9},{10,18},{18,10},{11,19},{19,11},{12,20... | collective-permute-start | bytes 393224 | tf_op jit(solution)/shard_map/ppermute | solution.py:456
